TPU v7x, 256 devices: a 2x2x32 block of a 4x8x32 slice. The times are simulated.
256 devices in a mesh: clip: 4 (over x, y), slab: 64 (over z, core).
Axes of the slice: x: 2, y: 2, z: 32, core: 2. Of those that a mesh axis runs over, the one named last changes fastest.
The devices are a block of a 4x8x32 slice.
Arguments:
- mask_field: float32 [8192, 2048], P(('clip', 'slab')), parts along dimension 0, may hold values from -1.8 to 2.9
- target_print: int32 [8192, 2048], P(('clip', 'slab')), parts along dimension 0, may hold values from 0 to 1
- source_points: int32 [64, 2], P('clip'), parts along dimension 0, may hold values from 0 to 60
- source_groups: int32 [64], P('clip'), parts along dimension 0, may hold values from 0 to 7
- group_logits: float32 [32], P('clip'), parts along dimension 0, may hold values from -1 to 1
- pupil_radius: int32 [4], P('clip'), parts along dimension 0, may hold values from 32 to 127
Outputs:
- loss_value: float32 [4], P('clip'), parts along dimension 0
- mask_grad: float32 [8192, 2048], P(('clip', 'slab')), parts along dimension 0
- group_grad: float32 [32], P('clip'), parts along dimension 0
There are 4 independent parts, one for each index of `clip`. A program takes and returns all parts, laid end to end along the dimension named above; each array names one. Nothing has to cross between parts.
All inputs are finite; a program needn't handle non-finite values.
Results may differ from a plain program's by a relative error of at most 0.0003.
Values sent between devices are 32-bit elements; how exact they have to be, the bound alone decides.
No kernel may reach another device: no remote copies, remote signals or barrier semaphores. Data moves between devices by JAX's collectives and lax.ppermute only.
A program may use at most 128 MiB of HBM per device.

v0:
```python
import math

import jax
import jax.numpy as jnp
from jax import lax
from jax.sharding import Mesh
from jax.sharding import PartitionSpec as P

K = 256
GRID = 61
NG = 8
SLAB = ("slab_0", "slab_1")
CLIP_SLAB = ("clip", "slab_0", "slab_1")


steepness = 8.0
threshold = 0.3
shift_scale = 45
full_turn = 2.0 * math.pi
highest = lax.Precision.HIGHEST


def joined_along(parts, dim):
    parts = jnp.moveaxis(parts, 0, dim)
    lengths = parts.shape
    return parts.reshape(*lengths[:dim], lengths[dim] * lengths[dim + 1], *lengths[dim + 2 :])


def all_blocks(shard, axes, sequence):
    parts = shard
    for k in sequence:
        parts = lax.all_gather(parts, axes[k])
    done = sequence[::-1]
    back = [done.index(k) for k in range(len(axes))]
    parts = parts.transpose(*back, *range(len(axes), parts.ndim))
    return parts.reshape(-1, *shard.shape)


def whole_of(shard, axes, sequence, dim):
    return joined_along(all_blocks(shard, axes, sequence), dim)


def copy_for_each(shard, axis):
    copies = jnp.broadcast_to(shard, (lax.axis_size(axis), *shard.shape))
    return lax.all_to_all(copies, axis, split_axis=0, concat_axis=0, tiled=True)


def over_copies(shard, axis):
    return copy_for_each(shard, axis).sum(axis=0)


def in_one(arrays, axis):
    ends = [0]
    for a in arrays:
        ends.append(ends[-1] + a.size)
    so_far = over_copies(jnp.concatenate([a.ravel() for a in arrays]), axis)
    return tuple((so_far[b:e].reshape(a.shape) for a, b, e in zip(arrays, ends, ends[1:])))


def contract(form, left, right):
    return jnp.einsum(form, left, right, precision=highest)


def turn_table(left, right, length):
    product = jnp.mod(left[:, None] * right[None, :], length)
    angles = full_turn * product.astype(jnp.float32) / length
    return (jnp.cos(angles), jnp.sin(angles))


def pupil_mask(shifted, radius_sq, along_first, along_second):
    first_axis = along_first[None, :, None] + shifted[:, 0, None, None]
    second_axis = along_second[None, None, :] + shifted[:, 1, None, None]
    return (first_axis * first_axis + second_axis * second_axis <= radius_sq).astype(jnp.float32)


def on_device(mask_field, target_print, source_points, source_groups, group_logits, pupil_radius):
    row_count = mask_field.shape[0]
    length = mask_field.shape[1]
    half_band = K // 2
    device = lax.axis_index(SLAB)
    positions = device * row_count + jnp.arange(row_count, dtype=jnp.int32)
    everywhere = jnp.arange(length, dtype=jnp.int32)
    frequency = jnp.arange(K, dtype=jnp.int32) - half_band
    cos_full, sin_full = turn_table(everywhere, frequency, length)
    cos_local, sin_local = turn_table(positions, frequency, length)
    cutoff = pupil_radius[0]
    radius_sq = cutoff * cutoff
    shifted = (source_points - GRID // 2) * cutoff // shift_scale
    norming = 1.0 / (length * length)
    row_real = jnp.dot(mask_field, cos_full, precision=highest)
    row_imag = -jnp.dot(mask_field, sin_full, precision=highest)
    row_spectrum = jnp.stack([row_real, row_imag], 1)
    columns_in = lax.all_to_all(row_spectrum, SLAB, split_axis=2, concat_axis=0, tiled=True)
    spec_real = contract("nk,nj->kj", cos_full, columns_in[:, 0]) + contract(
        "nk,nj->kj", sin_full, columns_in[:, 1]
    )
    spec_imag = contract("nk,nj->kj", cos_full, columns_in[:, 1]) - contract(
        "nk,nj->kj", sin_full, columns_in[:, 0]
    )
    block_cols = whole_of(jnp.stack([spec_real, spec_imag], 0), SLAB, (0, 1), 2)
    width_here = block_cols.shape[2]
    columns = jnp.arange(width_here, dtype=jnp.int32) - half_band
    passed = pupil_mask(shifted, radius_sq, frequency, columns)
    real_part = passed * block_cols[0][None]
    imag_part = passed * block_cols[1][None]
    lifted_real = contract("xk,skj->sxj", cos_local, real_part) - contract(
        "xk,skj->sxj", sin_local, imag_part
    )
    lifted_imag = contract("xk,skj->sxj", cos_local, imag_part) + contract(
        "xk,skj->sxj", sin_local, real_part
    )
    lifted = jnp.stack([lifted_real, lifted_imag], 1)
    field_real = (
        contract("sxk,yk->sxy", lifted[:, 0], cos_full)
        - contract("sxk,yk->sxy", lifted[:, 1], sin_full)
    ) * norming
    field_imag = (
        contract("sxk,yk->sxy", lifted[:, 0], sin_full)
        + contract("sxk,yk->sxy", lifted[:, 1], cos_full)
    ) * norming
    bright = field_real * field_real + field_imag * field_imag
    onehot_table = (source_groups[:, None] == jnp.arange(NG, dtype=jnp.int32)[None, :]).astype(
        jnp.float32
    )
    weights = jnp.exp(jnp.sum(onehot_table * group_logits[None, :], 1))
    total_weight = jnp.sum(weights)
    weight_share = weights / total_weight
    intensity = jnp.einsum("s,sxy->xy", weight_share, bright, precision=highest)
    resist = jax.nn.sigmoid(steepness * (intensity - threshold))
    misfit = resist - target_print.astype(jnp.float32)
    slope_map = 2.0 * misfit * steepness * resist * (1.0 - resist)
    per_source = contract("sxy,xy->s", bright, slope_map)
    against = jnp.sum(slope_map * intensity)
    squares = jnp.sum(misfit * misfit)
    per_source, against, squares = in_one((per_source, against, squares), SLAB)
    loss_value = (squares * norming).reshape(1)
    source_pull = weights * (per_source - against) / total_weight
    group_grad = jnp.sum(onehot_table * source_pull[:, None], 0) * norming
    factor = 2.0 * weight_share[:, None, None] * slope_map[None] * norming
    back_real = factor * field_real
    back_imag = factor * field_imag
    down_real = contract("sxy,yk->sxk", back_real, cos_full) + contract(
        "sxy,yk->sxk", back_imag, sin_full
    )
    down_imag = contract("sxy,yk->sxk", back_imag, cos_full) - contract(
        "sxy,yk->sxk", back_real, sin_full
    )
    stacked = jnp.stack([down_real, down_imag], 2)
    gathered_rows = lax.all_to_all(stacked, SLAB, split_axis=3, concat_axis=1, tiled=True)
    width_here = gathered_rows.shape[3]
    settle_real = contract("nk,snj->skj", cos_full, gathered_rows[:, :, 0]) + contract(
        "nk,snj->skj", sin_full, gathered_rows[:, :, 1]
    )
    settle_imag = contract("nk,snj->skj", cos_full, gathered_rows[:, :, 1]) - contract(
        "nk,snj->skj", sin_full, gathered_rows[:, :, 0]
    )
    own_columns = device * width_here + jnp.arange(width_here, dtype=jnp.int32) - half_band
    passed = pupil_mask(shifted, radius_sq, frequency, own_columns)
    pull_cols = jnp.stack([jnp.sum(passed * settle_real, 0), jnp.sum(passed * settle_imag, 0)], 0)
    block_cols = lax.all_gather(pull_cols, SLAB, axis=2, tiled=True)
    spread_real = contract("xk,kj->xj", cos_local, block_cols[0]) - contract(
        "xk,kj->xj", sin_local, block_cols[1]
    )
    spread_imag = contract("xk,kj->xj", cos_local, block_cols[1]) + contract(
        "xk,kj->xj", sin_local, block_cols[0]
    )
    spread_out = jnp.stack([spread_real, spread_imag], 0)
    mask_grad = contract("xk,yk->xy", spread_out[0], cos_full) - contract(
        "xk,yk->xy", spread_out[1], sin_full
    )
    return (loss_value, mask_grad, group_grad)


def solution(mesh):
    split = Mesh(mesh.devices.reshape(mesh.shape["clip"], 32, 2), ("clip", "slab_0", "slab_1"))
    return jax.shard_map(
        on_device,
        mesh=split,
        in_specs=(
            P(CLIP_SLAB, None),
            P(CLIP_SLAB, None),
            P("clip", None),
            P("clip"),
            P("clip"),
            P("clip"),
        ),
        out_specs=(P("clip"), P(CLIP_SLAB, None), P("clip")),
        check_vma=False,
    )
```

profile of v0, /device:TPU:37, one launch (start us, length us, event | category | flops | bytes accessed | tf_op | source)
XLA Modules:
  0.0 587.9 jit_solution(12435882736107836107)
XLA Ops:
  0.7 0.9 copy-done
  1.6 8.8 %convolution_bitcast_fusion = f32[32,1,256]{2,0,1:T(8,128)S(1)} fusion(f32[32,2048]{1,0:T(8,128)S(1)} %copy-done, s32[256]{0:T(256)S(1)} %iota_add_fusion), kind=kOutput, calls=%fused_computation.103 | convolution fusion | flops 208666624 | bytes 295936 | tf_op jit(solution)/shard_map/dot_general | solution.py:90
  10.5 9.1 %fusion.134 = f32[32,1,256]{2,0,1:T(8,128)S(1)} fusion(f32[32,2048]{1,0:T(8,128)S(1)} %copy-done, s32[256]{0:T(256)S(1)} %iota_add_fusion), kind=kOutput, calls=%fused_computation.102 | convolution fusion | flops 208674816 | bytes 295936 | tf_op jit(solution)/shard_map/dot_general | solution.py:91
  19.8 0.9 reshape.178
  20.7 34.7 %all-to-all-start = ((f32[64,1,256]{2,1,0:T(1,128)}), f32[64,1,256]{2,1,0:T(1,128)S(1)}, u32[]{:S(2)}, u32[]{:S(2)}) async-start(f32[64,1,256]{2,1,0:T(1,128)} %reshape.178), calls=%async_computation | async-start | bytes 131072 | tf_op jit(solution)/shard_map/all_to_all | solution.py:93
  56.2 0.6 exponential_reduce_fusion
  56.9 23.5 %all-to-all-done = f32[64,1,256]{2,1,0:T(1,128)S(1)} async-done(((f32[64,1,256]{2,1,0:T(1,128)}), f32[64,1,256]{2,1,0:T(1,128)S(1)}, u32[]{:S(2)}, u32[]{:S(2)}) %all-to-all-start) | async-done | bytes 65568 | tf_op jit(solution)/shard_map/all_to_all | solution.py:93
  81.0 0.8 reduce.1
  82.2 8.7 %fusion.152 = f32[256,4]{0,1:T(4,128)S(1)} fusion(s32[256]{0:T(256)S(1)} %iota_add_fusion, f32[2048,2,4]{0,2,1:T(4,128)S(1)} %all_to_all.33), kind=kOutput, calls=%fused_computation.114 | convolution fusion | flops 32505856 | bytes 37888 | tf_op jit(solution)/shard_map/nk,nj->kj/dot_general | solution.py:61
  90.9 8.9 %fusion.150 = f32[256,4]{0,1:T(4,128)S(1)} fusion(s32[256]{0:T(256)S(1)} %iota_add_fusion, f32[2048,2,4]{0,2,1:T(4,128)S(1)} %all_to_all.33), kind=kOutput, calls=%fused_computation.113 | convolution fusion | flops 32505856 | bytes 37888 | tf_op jit(solution)/shard_map/nk,nj->kj/dot_general | solution.py:61
  99.8 9.2 %fusion.136 = f32[1,256,4]{1,2,0:T(4,128)S(1)} fusion(f32[256,4]{0,1:T(4,128)S(1)} %fusion.152, s32[256]{0:T(256)S(1)} %iota_add_fusion, f32[2048,2,4]{0,2,1:T(4,128)S(1)} %all_to_all.33), kind=kOutput, calls=%fused_computation.107 | convolution fusion | flops 32506880 | bytes 41984 | tf_op jit(solution)/shard_map/nk,nj->kj/dot_general | solution.py:61
  109.0 9.0 %fusion.135 = f32[1,256,4]{1,2,0:T(4,128)S(1)} fusion(f32[256,4]{0,1:T(4,128)S(1)} %fusion.150, s32[256]{0:T(256)S(1)} %iota_add_fusion, f32[2048,2,4]{0,2,1:T(4,128)S(1)} %all_to_all.33), kind=kOutput, calls=%fused_computation.105 | convolution fusion | flops 32506880 | bytes 41984 | tf_op jit(solution)/shard_map/nk,nj->kj/dot_general | solution.py:61
  118.0 39.1 %all-gather = f32[64,256,4]{1,2,0:T(4,128)S(1)} all-gather(f32[2,256,4]{1,2,0:T(4,128)S(1)} %pad_maximum_fusion.2), channel_id=2, replica_groups=mesh['clip'=4,'slab_0'=32,'slab_1'=2] {'slab_0'}, dimensions={0}, use_global_device_ids=true | all-gather | bytes 270336 | tf_op jit(solution)/shard_map/all_gather | solution.py:32
  157.1 16.5 %all-gather.1 = f32[64,2,256,4]{2,3,1,0:T(4,128)S(1)} all-gather(f32[32,2,256,4]{2,3,1,0:T(4,128)S(1)} %bitcast.202), channel_id=3, replica_groups=mesh['clip'=4,'slab_0'=32,'slab_1'=2] {'slab_1'}, dimensions={0}, use_global_device_ids=true | all-gather | bytes 786432 | tf_op jit(solution)/shard_map/all_gather | solution.py:32
  174.4 3.3 fusion.2
  177.7 3.3 fusion
  181.3 3.3 fusion.101
  184.6 11.7 %fusion.41 = f32[16,32,2048]{2,1,0:T(8,128)S(1)} fusion(f32[16,32,256]{2,1,0:T(8,128)S(1)} %fusion.101, s32[256]{0:T(256)S(1)} %iota_add_fusion), kind=kOutput, calls=%fused_computation.46 | convolution fusion | flops 3228565504 | bytes 4719616 | tf_op jit(solution)/shard_map/sxk,yk->sxy/dot_general | solution.py:61
  196.3 11.6 %fusion.31 = f32[16,32,2048]{2,1,0:T(8,128)S(1)} fusion(f32[16,32,256]{2,1,0:T(8,128)S(1)} %fusion.101, s32[256]{0:T(256)S(1)} %iota_add_fusion), kind=kOutput, calls=%fused_computation.36 | convolution fusion | flops 3228565504 | bytes 4719616 | tf_op jit(solution)/shard_map/sxk,yk->sxy/dot_general | solution.py:61
  207.9 3.3 fusion.107
  211.2 12.2 %subtract_multiply_fusion = f32[16,32,2048]{2,1,0:T(8,128)S(1)} fusion(f32[16,32,2048]{2,1,0:T(8,128)S(1)} %fusion.41, f32[16,32,256]{2,1,0:T(8,128)S(1)} %fusion.107, s32[256]{0:T(256)S(1)} %iota_add_fusion), kind=kOutput, calls=%fused_computation.13 | convolution fusion | flops 3230662656 | bytes 8913920 | tf_op jit(solution)/shard_map/sxk,yk->sxy/dot_general | solution.py:61
  223.4 13.7 %multiply_add_fusion = (f32[16,32,2048]{2,1,0:T(8,128)S(1)}, f32[16,32,2048]{2,1,0:T(8,128)}) fusion(f32[16,32,2048]{2,1,0:T(8,128)S(1)} %subtract_multiply_fusion, f32[16,32,2048]{2,1,0:T(8,128)S(1)} %fusion.31, f32[16,32,256]{2,1,0:T(8,128)S(1)} %fusion.107, s32[256]{0:T(256)S(1)} %iota_add_fusion), kind=kOutput, calls=%fused_computation.11 | convolution fusion | flops 3233808384 | bytes 17302528 | tf_op jit(solution)/shard_map/sxk,yk->sxy/dot_general | solution.py:61
  237.1 5.0 fusion.12
  242.2 0.8 fusion.176
  242.9 6.7 %fusion.137 = f32[16]{0:T(128)S(1)} fusion(f32[16,32,2048]{2,1,0:T(8,128)S(1)} %get-tuple-element.18, f32[32,2048,1]{1,0,2:T(8,128)S(1)} %bitcast.200), kind=kOutput, calls=%fused_computation.108 | convolution fusion | flops 12582912 | bytes 4456512 | tf_op jit(solution)/shard_map/sxy,xy->s/dot_general | solution.py:61
  249.6 1.3 pad_maximum_fusion.4
  251.0 29.3 %all_to_all.42 = f32[64,1,18]{2,1,0:T(1,128)S(1)} all-to-all(f32[64,1,18]{2,1,0:T(1,128)S(1)} %broadcast_in_dim.2), channel_id=1, replica_groups=mesh['clip'=4,'slab_0'=32,'slab_1'=2] {'slab_0','slab_1'}, dimensions={0} | all-to-all | bytes 9216 | tf_op jit(solution)/shard_map/all_to_all | solution.py:45
  280.3 0.6 fusion.322
  280.9 1.3 multiply_divide_fusion
  282.2 13.6 %fusion.16 = f32[16,32,256]{2,1,0:T(8,128)S(1)} fusion(f32[16,32,2048]{2,1,0:T(8,128)} %copy-done.2, f32[32,2048]{1,0:T(8,128)S(1)} %get-tuple-element.5, f32[16]{0:T(128)S(1)} %get-tuple-element.15, s32[256]{0:T(256)S(1)} %iota_add_fusion), kind=kOutput, calls=%fused_computation.20 | convolution fusion | flops 3231711232 | bytes 4981824 | tf_op jit(solution)/shard_map/sxy,yk->sxk/dot_general | solution.py:61
  295.9 11.5 %fusion.14 = f32[16,32,256]{2,1,0:T(8,128)S(1)} fusion(f32[16,32,2048]{2,1,0:T(8,128)S(1)} %copy-done.3, f32[32,2048]{1,0:T(8,128)S(1)} %get-tuple-element.5, f32[16]{0:T(128)S(1)} %get-tuple-element.15, s32[256]{0:T(256)S(1)} %iota_add_fusion), kind=kOutput, calls=%fused_computation.19 | convolution fusion | flops 3231711232 | bytes 4981824 | tf_op jit(solution)/shard_map/sxy,yk->sxk/dot_general | solution.py:61
  307.4 11.6 %fusion.93 = f32[16,32,1,256]{3,1,0,2:T(8,128)S(1)} fusion(f32[16,32,256]{2,1,0:T(8,128)S(1)} %fusion.16, f32[16,32,2048]{2,1,0:T(8,128)S(1)} %copy-done.1, f32[32,2048]{1,0:T(8,128)S(1)} %get-tuple-element.5, f32[16]{0:T(128)S(1)} %get-tuple-element.15, s32[256]{0:T(256)S(1)} %iota_add_fusion), kind=kOutput, calls=%fused_computation.86 | convolution fusion | flops 3231842304 | bytes 5506112 | tf_op jit(solution)/shard_map/sxy,yk->sxk/dot_general | solution.py:61
  319.0 11.7 %fusion.88 = f32[16,32,1,256]{3,1,0,2:T(8,128)S(1)} fusion(f32[16,32,256]{2,1,0:T(8,128)S(1)} %fusion.14, f32[16,32,2048]{2,1,0:T(8,128)S(1)} %copy-done.1, f32[32,2048]{1,0:T(8,128)S(1)} %get-tuple-element.5, f32[16]{0:T(128)S(1)} %get-tuple-element.15, s32[256]{0:T(256)S(1)} %iota_add_fusion), kind=kOutput, calls=%fused_computation.85 | convolution fusion | flops 3231842304 | bytes 5506112 | tf_op jit(solution)/shard_map/sxy,yk->sxk/dot_general | solution.py:61
  330.8 4.5 copy.87
  335.4 4.7 reshape.180
  340.0 6.3 %all-to-all-start.2 = ((f32[64,1,4096]{2,1,0:T(1,128)}), f32[64,1,4096]{2,1,0:T(1,128)S(1)}, u32[]{:S(2)}, u32[]{:S(2)}) async-start(f32[64,1,4096]{2,1,0:T(1,128)} %reshape.180), calls=%async_computation.2 | async-start | bytes 2097152 | tf_op jit(solution)/shard_map/all_to_all | solution.py:149
  347.7 107.2 %all-to-all-done.2 = f32[64,1,4096]{2,1,0:T(1,128)S(1)} async-done(((f32[64,1,4096]{2,1,0:T(1,128)}), f32[64,1,4096]{2,1,0:T(1,128)S(1)}, u32[]{:S(2)}, u32[]{:S(2)}) %all-to-all-start.2) | async-done | bytes 1048608 | tf_op jit(solution)/shard_map/all_to_all | solution.py:149
  454.9 3.3 reduce.2
  458.1 2.7 reshape.181
  460.8 6.6 %copy.89 = f32[16,64,32,2,4]{2,1,0,4,3:T(8,128)} copy(f32[16,64,32,2,4]{2,0,3,4,1:T(8,128)} %bitcast.197) | data formatting | bytes 2097152 | tf_op jit(solution)/shard_map/all_to_all | solution.py:149
  467.4 3.8 all_to_all.38
  471.3 8.9 %fusion.27 = f32[16,4,256]{2,0,1:T(8,128)S(1)} fusion(s32[256]{0:T(256)S(1)} %iota_add_fusion, f32[16,2048,2,4]{1,0,3,2:T(8,128)S(1)} %all_to_all.38), kind=kOutput, calls=%fused_computation.32 | convolution fusion | flops 409993216 | bytes 590848 | tf_op jit(solution)/shard_map/nk,snj->skj/dot_general | solution.py:61
  480.1 9.3 %fusion.25 = f32[16,4,256]{2,0,1:T(8,128)S(1)} fusion(s32[256]{0:T(256)S(1)} %iota_add_fusion, f32[16,2048,2,4]{1,0,3,2:T(8,128)S(1)} %all_to_all.38), kind=kOutput, calls=%fused_computation.30 | convolution fusion | flops 409993216 | bytes 590848 | tf_op jit(solution)/shard_map/nk,snj->skj/dot_general | solution.py:61
  489.4 9.0 %fusion.131 = f32[256,4]{0,1:T(4,128)S(1)} fusion(f32[16,4,256]{2,0,1:T(8,128)S(1)} %fusion.27, s32[256]{0:T(256)S(1)} %iota_add_fusion, f32[16,2048,2,4]{1,0,3,2:T(8,128)S(1)} %all_to_all.38, s32[]{:T(128)S(6)} %mul.307, s32[16,4]{0,1:T(4,128)S(1)} %add_multiply_fusion.3, s32[16,256]{1,0:T(8,128)S(1)} %get-tuple-element.10), kind=kOutput, calls=%fused_computation.98 | convolution fusion | flops 410074112 | bytes 613380 | tf_op jit(solution)/shard_map/nk,snj->skj/dot_general | solution.py:61
  498.4 9.0 %fusion.128 = f32[256,4]{0,1:T(4,128)S(1)} fusion(f32[16,4,256]{2,0,1:T(8,128)S(1)} %fusion.25, s32[256]{0:T(256)S(1)} %iota_add_fusion, f32[16,2048,2,4]{1,0,3,2:T(8,128)S(1)} %all_to_all.38, s32[]{:T(128)S(6)} %mul.307, s32[16,4]{0,1:T(4,128)S(1)} %add_multiply_fusion.3, s32[16,256]{1,0:T(8,128)S(1)} %get-tuple-element.10), kind=kOutput, calls=%fused_computation.97 | convolution fusion | flops 410074112 | bytes 613380 | tf_op jit(solution)/shard_map/nk,snj->skj/dot_general | solution.py:61
  507.4 56.4 %all_gather.19 = f32[2,256,256]{1,0,2:T(2,128)S(1)} all-gather(f32[2,256,4]{1,0,2:T(2,128)S(1)} %copy.90), channel_id=1, replica_groups=mesh['clip'=4,'slab_0'=32,'slab_1'=2] {'slab_0','slab_1'}, dimensions={2}, use_global_device_ids=true | all-gather | bytes 532480 | tf_op jit(solution)/shard_map/all_gather | solution.py:160
  566.0 9.3 %fusion.147 = f32[32,2048]{1,0:T(8,128)S(1)} fusion(f32[32,256]{1,0:T(8,128)S(1)} %convolution_subtract_fusion.1, s32[256]{0:T(256)S(1)} %iota_add_fusion), kind=kOutput, calls=%fused_computation.112 | convolution fusion | flops 208666624 | bytes 295936 | tf_op jit(solution)/shard_map/xk,yk->xy/dot_general | solution.py:61
  575.3 11.0 %convolution_subtract_fusion = f32[32,2048]{1,0:T(8,128)} fusion(f32[32,2048]{1,0:T(8,128)S(1)} %fusion.147, f32[32,256]{1,0:T(8,128)S(1)} %convolution_add_fusion, s32[256]{0:T(256)S(1)} %iota_add_fusion), kind=kOutput, calls=%fused_computation.26 | convolution fusion | flops 208732160 | bytes 558080 | tf_op jit(solution)/shard_map/xk,yk->xy/dot_general | solution.py:61
  (50 shorter events, 5.4 us)
Async XLA Ops:
  0.6 1.0 copy-start
  10.4 45.6 %copy-start.6 = (f32[8]{0:T(128)S(1)}, f32[8]{0:T(128)}, u32[]{:S(2)}) copy-start(f32[8]{0:T(128)} %param.10) | copy-start | bytes 100
  10.4 45.6 %copy-start.7 = (s32[16]{0:T(128)S(1)}, s32[16]{0:T(128)}, u32[]{:S(2)}) copy-start(s32[16]{0:T(128)} %param.9) | copy-start | bytes 196
  10.5 46.3 %copy-start.5 = (s32[16,2]{0,1:T(2,128)S(1)}, s32[16,2]{0,1:T(2,128)}, u32[]{:S(2)}) copy-start(s32[16,2]{0,1:T(2,128)} %param.8) | copy-start | bytes 388
  20.7 59.8 %all-to-all-start = ((f32[64,1,256]{2,1,0:T(1,128)}), f32[64,1,256]{2,1,0:T(1,128)S(1)}, u32[]{:S(2)}, u32[]{:S(2)}) async-start(f32[64,1,256]{2,1,0:T(1,128)} %reshape.178), calls=%async_computation | async-start | bytes 131072 | tf_op jit(solution)/shard_map/all_to_all | solution.py:93
  223.4 13.7 %copy-start.2 = (f32[16,32,2048]{2,1,0:T(8,128)}, f32[16,32,2048]{2,1,0:T(8,128)S(1)}, u32[]{:S(2)}) copy-start(f32[16,32,2048]{2,1,0:T(8,128)S(1)} %subtract_multiply_fusion) | copy-start | bytes 12582916
  237.1 5.1 copy-start.4
  282.2 13.6 %copy-start.3 = (f32[16,32,2048]{2,1,0:T(8,128)S(1)}, f32[16,32,2048]{2,1,0:T(8,128)}, u32[]{:S(2)}) copy-start(f32[16,32,2048]{2,1,0:T(8,128)} %copy-done.2) | copy-start | bytes 12582916
  295.8 11.6 %copy-start.1 = (f32[16,32,2048]{2,1,0:T(8,128)S(1)}, f32[16,32,2048]{2,1,0:T(8,128)}, u32[]{:S(2)}) copy-start(f32[16,32,2048]{2,1,0:T(8,128)} %get-tuple-element.19) | copy-start | bytes 12582916
  340.0 114.8 %all-to-all-start.2 = ((f32[64,1,4096]{2,1,0:T(1,128)}), f32[64,1,4096]{2,1,0:T(1,128)S(1)}, u32[]{:S(2)}, u32[]{:S(2)}) async-start(f32[64,1,4096]{2,1,0:T(1,128)} %reshape.180), calls=%async_computation.2 | async-start | bytes 2097152 | tf_op jit(solution)/shard_map/all_to_all | solution.py:149
where the time goes:
time: 597 us; the launch traced here: 588 us
  matrix products  234 us (39%)
  blocking collectives  141 us (24%)
  waiting for transfers between devices  131 us (22%)
  starting transfers between devices  41.1 us (7%)
  local copies, waits for them, and re-layouts  27.3 us (5%)
  other arithmetic  9.16 us (2%)
    dot_general x27, matrix products, contract(): return jnp.einsum(form, left, right, precision=highest)  211 us
    all_to_all x1, waiting for transfers between devices, on_device(): lax.all_to_all(stacked, SLAB, split_axis=3, concat_axis=1, tiled=True)  107 us
    all_gather x1, blocking collectives, on_device(): block_cols = lax.all_gather(pull_cols, SLAB, axis=2, tiled=True)  56.4 us
    all_gather x2, blocking collectives, all_blocks(): parts = lax.all_gather(parts, axes[k])  55.7 us
    all_to_all x1, starting transfers between devices, on_device(): lax.all_to_all(row_spectrum, SLAB, split_axis=2, concat_axis=0, tiled=True)  34.7 us
    all_to_all x1, blocking collectives, copy_for_each(): return lax.all_to_all(copies, axis, split_axis=0, concat_axis=0, tiled=True)  29.3 us
    all_to_all x1, waiting for transfers between devices, on_device(): lax.all_to_all(row_spectrum, SLAB, split_axis=2, concat_axis=0, tiled=True)  23.5 us
  transfers between devices with their start and end apart: 2, of which 2 were waited for; matrix products, arithmetic and copies ran while one was open for 0% of the time, Pallas kernels for 0%

commit v1 on v0

v1 whole, which is shorter than its diff:
```python
import functools

import numpy as np
import jax
import jax.numpy as jnp
from jax import lax
from jax.experimental import pallas as pl
from jax.experimental.pallas import tpu as pltpu
from jax.sharding import Mesh
from jax.sharding import PartitionSpec as P

K = 256
HALF = K // 2
GRID = 61
NG = 8
COARSE = 2 * K
PARCEL = 9 * 128
RING = "slab_0"
CORE = "slab_1"
SLAB = (RING, CORE)
CLIP_SLAB = ("clip", RING, CORE)

steepness = 8.0
threshold = 0.3
shift_scale = 45

f32 = jnp.float32
bf16 = jnp.bfloat16
NN = (((1,), (0,)), ((), ()))
NT = (((1,), (1,)), ((), ()))
TN = (((0,), (0,)), ((), ()))


def mm(a, b, dims=NN):
    return lax.dot_general(a, b, dims, preferred_element_type=f32)


def pieces(a):
    high = a.astype(bf16)
    return high, (a - high.astype(f32)).astype(bf16)


def mm3(a, b, dims=NN):
    return mm(a[0], b[0], dims) + mm(a[1], b[0], dims) + mm(a[0], b[1], dims)


def host_pieces(table):
    high = table.astype(np.float32).astype(jnp.bfloat16)
    low = (table - high.astype(np.float64)).astype(np.float32).astype(jnp.bfloat16)
    return np.asarray(high), np.asarray(low)


def turns(left, right, length):
    angle = 2.0 * np.pi * (np.outer(left, right) % length) / length
    return np.cos(angle), np.sin(angle)


def groups_of(e):
    return (e - 1) % 4, (3 - e) % 4


def lane_index(shape):
    return lax.broadcasted_iota(jnp.int32, shape, len(shape) - 1)


def row_index(shape):
    return lax.broadcasted_iota(jnp.int32, shape, 0)


def swapped(a, rows):
    lanes = a.shape[1]
    first = (lane_index(a.shape) // rows) % 2 == 0
    return jnp.where(first, pltpu.roll(a, lanes - rows, 1), -pltpu.roll(a, rows, 1))


def twiddle(cos_ref, sin_ref, m):
    owners = cos_ref.shape[0] - 8
    cos, sin = cos_ref[:owners], sin_ref[:owners]
    cos_m, sin_m = cos_ref[owners + m : owners + m + 1], sin_ref[owners + m : owners + m + 1]
    return cos * cos_m - sin * sin_m, sin * cos_m + cos * sin_m


def rows_kernel(mask_ref, high_ref, low_ref, out_ref):
    rows, length = mask_ref.shape
    quarter = length // 4
    m0, m1, m2, m3 = (mask_ref[:, q * quarter : (q + 1) * quarter] for q in range(4))
    even, odd = m0 + m2, m1 + m3
    stack = jnp.concatenate([even + odd, even - odd, m0 - m2, m1 - m3], 0)
    stack = pieces(stack)
    both = mm3((high_ref[...], low_ref[...]), stack, NT)
    cos, sin = both[:HALF], both[HALF:]
    c0, c2, ca, cb = (cos[:, i * rows : (i + 1) * rows] for i in range(4))
    s0, s2, sa, sb = (sin[:, i * rows : (i + 1) * rows] for i in range(4))
    owners = HALF // 2
    odd_row = row_index((owners, rows)) % 2 == 1
    lo, hi = slice(0, owners), slice(owners, HALF)
    ones = jnp.ones((owners, quarter), bf16)
    sums = (mm(ones, stack[0], NT) + mm(ones, stack[1], NT))[:, :rows]
    out_ref[:, :] = jnp.concatenate(
        [
            jnp.where(odd_row, c2[lo], ca[lo] - sb[lo]),
            jnp.where(odd_row, -s2[lo], -sa[lo] - cb[lo]),
            jnp.where(odd_row, c0[hi], ca[hi] + sb[hi]),
            jnp.where(odd_row, -s0[hi], cb[hi] - sa[hi]),
            sums,
            jnp.zeros((owners, 3 * rows), f32),
        ],
        1,
    )


def columns_kernel(in_ref, dft_high_ref, dft_low_ref, cos_ref, sin_ref, piece_ref, zero_ref):
    owners, lanes = in_ref.shape
    rows = lanes // 8
    a = in_ref[...]
    z = mm3((dft_high_ref[...], dft_low_ref[...]), pieces(jnp.concatenate([a, swapped(a, rows)], 0)))
    turned = swapped(z, rows)
    blocks = []
    for m in range(5):
        cos, sin = twiddle(cos_ref, sin_ref, m)
        cos = jnp.concatenate([cos, cos], 1)
        sin = jnp.concatenate([sin, sin], 1)
        blocks.append(z * cos + turned * sin)
    high, low = pieces(jnp.concatenate(blocks, 0))
    pick = (row_index((8, lanes)) == lane_index((8, lanes)) // rows).astype(f32).astype(bf16)
    sums = mm(pick, high, NT) + mm(pick, low, NT)
    copies = piece_ref.shape[0]
    lane = lane_index((copies, 128))
    tail = jnp.zeros((copies, 128), f32)
    for q in range(4):
        piece_ref[:, q * K : (q + 1) * K] = jnp.broadcast_to(sums[q : q + 1, :K], (copies, K))
        tail = jnp.where(lane == q, sums[q : q + 1, K : K + 1], tail)
    piece_ref[:, 4 * K :] = tail
    zero_ref[...] = sums[:, :K]


def image_kernel(
    shift_ref,
    share_ref,
    radius_ref,
    around_ref,
    zero_ref,
    local_p_ref,
    local_m_ref,
    local_pt_ref,
    local_mt_ref,
    field_high_ref,
    field_low_ref,
    spread_high_ref,
    spread_low_ref,
    target_ref,
    out_ref,
    plus_ref,
    minus_ref,
    lift_ref,
    field_ref,
    back_high_ref,
    back_low_ref,
    settled_ref,
    pull_p_ref,
    pull_m_ref,
    sums_ref,
):
    sources = shift_ref.shape[0]
    rows = target_ref.shape[0]
    half = 2 * rows
    norming = 1.0 / (target_ref.shape[1] * target_ref.shape[1])
    radius_sq = radius_ref[0] * radius_ref[0]
    wide = around_ref[...]
    body = jnp.concatenate([wide[:, : 2 * K], wide[:, 2 * K : 4 * K]], 0)
    spectrum = body.T
    tail = wide[:, 4 * K :].T
    zero = zero_ref[...].T
    lane = lane_index((1, HALF))
    ring = HALF // 4
    frequency = 4 * (lane % ring) + lane // ring + 1
    last = lane == HALF - 1
    frequency_p = jnp.where(last, 0, frequency)
    across = row_index((K, 1)) - HALF
    across_m = jnp.where(across == -HALF, HALF, across)
    last_col = lane_index((K, HALF)) == HALF - 1
    first_row = row_index((K, HALF)) == 0
    for part in range(2):
        block = spectrum[part * K : (part + 1) * K]
        plus = jnp.where(last_col, zero[:, 4 + part : 5 + part], block)
        edge = jnp.concatenate([tail[part : part + 1], tail[2 + part : 3 + part]], 1)
        minus = jnp.where(first_row, edge, block)
        for ref, value in ((plus_ref, plus), (minus_ref, minus)):
            high, low = pieces(value)
            ref[part * K : (part + 1) * K, :HALF] = high
            ref[part * K : (part + 1) * K, HALF:] = low

    def passes(s):
        s0 = shift_ref[s, 0]
        s1 = shift_ref[s, 1]
        a = across + s0
        b = frequency_p + s1
        plus = a * a <= radius_sq - b * b
        a = s0 - across_m
        b = s1 - frequency
        minus = a * a <= radius_sq - b * b
        return jnp.where(plus, 1.0, 0.0), jnp.where(minus, 1.0, 0.0)

    block = HALF // 4
    in_block = [lane_index((rows, HALF)) // block == i for i in range(4)]

    def place(choose):
        out = None
        for i in range(4):
            value, group = choose(i)
            value = pltpu.roll(value, (i - group) % 4 * block, 1) if i != group else value
            out = value if out is None else jnp.where(in_block[i], value, out)
        return out

    def lift(s, carry):
        parts = []
        for spec_ref, table_ref, passed in zip((plus_ref, minus_ref), (local_p_ref, local_m_ref), passes(s)):
            passed = passed.astype(bf16)
            passed = jnp.concatenate([passed, passed], 0)
            passed = jnp.concatenate([passed, passed], 1)
            out = mm(table_ref[...], spec_ref[...] * passed)
            out = (out[:half, :HALF] + out[half:, :HALF] + out[:half, HALF:]) * norming
            parts += [out[:rows], out[rows:]]
        at_rows = pl.ds(pl.multiple_of(s * rows, rows), rows)
        for e in range(4):
            groups = groups_of(e)
            high, low = pieces(place(lambda i: (parts[i], groups[i // 2])))
            lift_ref[at_rows, e * 2 * HALF : e * 2 * HALF + HALF] = high
            lift_ref[at_rows, e * 2 * HALF + HALF : (e + 1) * 2 * HALF] = low
        return carry

    lax.fori_loop(0, sources, lift, 0)
    field_tables = [
        (field_high_ref[e * HALF : (e + 1) * HALF], field_low_ref[e * HALF : (e + 1) * HALF]) for e in range(4)
    ]
    for e, (high, low) in enumerate(field_tables):
        lanes = slice(e * 2 * HALF, (e + 1) * 2 * HALF)
        packed = lift_ref[:, lanes]
        field_ref[:, lanes] = mm(packed, jnp.concatenate([high, high], 0)) + mm(packed[:, :HALF], low)

    def lane_blocks(at_rows):
        return [field_ref[at_rows, i * HALF : (i + 1) * HALF] for i in range(8)]

    def expose(s, total):
        at_rows = pl.ds(pl.multiple_of(s * rows, rows), rows)
        r0, i0, r1, i1, r2, i2, r3, i3 = lane_blocks(at_rows)
        real = [r0 + r2 + (r1 + r3), r0 - r2 - (i1 - i3), r0 + r2 - (r1 + r3), r0 - r2 + (i1 - i3)]
        imag = [i0 + i2 + (i1 + i3), i0 - i2 + (r1 - r3), i0 + i2 - (i1 + i3), i0 - i2 - (r1 - r3)]
        out = []
        for q in range(4):
            field_ref[at_rows, 2 * q * HALF : (2 * q + 1) * HALF] = real[q]
            field_ref[at_rows, (2 * q + 1) * HALF : (2 * q + 2) * HALF] = imag[q]
            out.append(total[q] + share_ref[s] * (real[q] * real[q] + imag[q] * imag[q]))
        return tuple(out)

    coarse = lax.fori_loop(0, sources, expose, (jnp.zeros((rows, HALF), f32),) * 4)
    spread = spread_high_ref[...], spread_low_ref[...]
    quarter = COARSE // 4
    spread = [tuple(t[at : at + n] for t in spread) for at, n in ((0, quarter), (quarter, quarter), (2 * quarter, 2 * quarter))]
    i0, i1, i2, i3 = coarse
    even, odd = i0 + i2, i1 + i3
    a, b = i0 - i2, i1 - i3
    e = mm3(pieces(even + odd), spread[0])
    f = mm3(pieces(even - odd), spread[1])
    rs = mm3(pieces(jnp.concatenate([jnp.concatenate([a, -b], 1), jnp.concatenate([b, a], 1)], 0)), spread[2])
    up, down = e + f, e - f
    r, t = rs[:rows], rs[rows:]
    fine = target_ref.shape[1] // 4
    slopes = []
    squares = jnp.zeros((rows, fine), f32)
    for q, intensity in enumerate((up + r, down + t, up - r, down - t)):
        resist = 1.0 / (1.0 + jnp.exp(-steepness * (intensity - threshold)))
        misfit = resist - target_ref[:, q * fine : (q + 1) * fine].astype(f32)
        slopes.append((2.0 * steepness) * misfit * resist * (1.0 - resist))
        squares = squares + misfit * misfit
    s0, s1, s2, s3 = slopes
    even, odd = s0 + s2, s1 + s3
    de = mm3(pieces(even + odd), spread[0], NT)
    df = mm3(pieces(even - odd), spread[1], NT)
    x = mm3(pieces(jnp.concatenate([s0 - s2, s1 - s3], 0)), spread[2], NT)
    da = x[:rows, :quarter] + x[rows:, quarter:]
    db = x[rows:, :quarter] - x[:rows, quarter:]
    up, down = de + df, de - df
    slope_c = [up + da, down + db, up - da, down - db]

    def lane_sum(a):
        a = jnp.sum(a, 0, keepdims=True)
        total = a[:, :128]
        for i in range(1, a.shape[1] // 128):
            total = total + a[:, i * 128 : (i + 1) * 128]
        return total

    sums_ref[...] = jnp.zeros(sums_ref.shape, f32)
    sums_ref[32:33, :] = lane_sum(squares)
    for ref in (pull_p_ref, pull_m_ref):
        ref[...] = jnp.zeros(ref.shape, f32)

    def push(s, carry):
        at_rows = pl.ds(pl.multiple_of(s * rows, rows), rows)
        blocks = lane_blocks(at_rows)
        bright = jnp.zeros((rows, HALF), f32)
        real, imag = [], []
        for q in range(4):
            re, im = blocks[2 * q], blocks[2 * q + 1]
            bright = bright + (re * re + im * im) * slope_c[q]
            factor = (2.0 * norming * share_ref[s]) * slope_c[q]
            real.append(factor * re)
            imag.append(factor * im)
        sums_ref[pl.ds(16 + s, 1), :] = jnp.sum(bright, 0, keepdims=True)
        er, ei, fr, fi = real[0] + real[2], imag[0] + imag[2], real[1] + real[3], imag[1] + imag[3]
        ar, ai, br, bi = real[0] - real[2], imag[0] - imag[2], real[1] - real[3], imag[1] - imag[3]
        turned = [er + fr, ei + fi, ar + bi, ai - br, er - fr, ei - fi, ar - bi, ai + br]
        for i, value in enumerate(turned):
            high, low = pieces(value)
            back_high_ref[at_rows, i * HALF : (i + 1) * HALF] = high
            back_low_ref[at_rows, i * HALF : (i + 1) * HALF] = low
        return carry

    lax.fori_loop(0, sources, push, 0)
    for e, (high, low) in enumerate(field_tables):
        lanes = slice(e * 2 * HALF, (e + 1) * 2 * HALF)
        both = mm(back_high_ref[:, lanes], jnp.concatenate([high, low], 0), NT)
        settled_ref[:, e * HALF : (e + 1) * HALF] = (
            both[:, :HALF] + both[:, HALF:] + mm(back_low_ref[:, lanes], high, NT)
        )

    def pull(s, carry):
        at_rows = pl.ds(pl.multiple_of(s * rows, rows), rows)
        settled = [settled_ref[at_rows, e * HALF : (e + 1) * HALF] for e in range(4)]
        arrays = [
            place(lambda i: (settled[(i + 1) % 4 if k < 2 else (3 - i) % 4], k)) for k in range(4)
        ]
        for pull_ref, table_ref, passed, at in zip(
            (pull_p_ref, pull_m_ref), (local_pt_ref, local_mt_ref), passes(s), (0, 2)
        ):
            high, low = pieces(jnp.concatenate(arrays[at : at + 2], 0))
            out = mm(table_ref[...], jnp.concatenate([high, low, high], 0))
            pull_ref[...] += out * jnp.concatenate([passed, passed], 0)
        return carry

    lax.fori_loop(0, sources, pull, 0)
    plus = pull_p_ref[...]
    minus = pull_m_ref[...]
    owners = HALF // 2
    sums = jnp.sum(sums_ref[...].T, 0, keepdims=True)
    lane = lane_index((owners, 128))
    tail = jnp.where(lane >= 16, sums, 0.0)
    for i in range(8):
        tail = jnp.where(lane == 8 + i, plus[i * owners : (i + 1) * owners, HALF - 1 :], tail)
    edge = jnp.concatenate([minus[:1], minus[K : K + 1], jnp.zeros((6, HALF), f32)], 0).T
    for j in range(2):
        for part in range(2):
            tail = jnp.where(lane == 2 * j + part, edge[j * owners : (j + 1) * owners, part : part + 1], tail)
    out_ref[:, 4 * K :] = tail
    total = jnp.where(lane_index(plus.shape) == HALF - 1, 0.0, plus)
    total = total + jnp.where(row_index(plus.shape) % K == 0, 0.0, minus)
    total = total.T
    out_ref[:, : 2 * K] = total[:owners]
    out_ref[:, 2 * K : 4 * K] = total[owners:]


def owner_kernel(in_ref, high_ref, low_ref, cos_ref, sin_ref, zero_cos_ref, zero_sin_ref, out_ref, sums_ref):
    total = jnp.sum(in_ref[...], 0, keepdims=True)
    tail = total[:, 4 * K :]
    sums_ref[...] = jnp.broadcast_to(tail, sums_ref.shape)
    owners = HALF // 2
    rows = cos_ref.shape[1] // 4
    quantities = [total[:, q * K : (q + 1) * K] for q in range(4)]
    columns = jnp.concatenate(quantities + [jnp.zeros((4, K), f32)], 0).T
    lane = lane_index((owners, 4 * rows))
    where = lane // rows
    z = jnp.zeros((owners, 4 * rows), f32)
    for m in range(5):
        cos, sin = twiddle(cos_ref, sin_ref, m)
        if m < 4:
            part = columns[m * owners : (m + 1) * owners]
            cols = [part[:, q : q + 1] for q in range(4)]
        else:
            top = row_index((owners, 1)) == 0
            cols = [jnp.where(top, tail[:, q : q + 1], 0.0) for q in range(4)]
        straight = jnp.where(where == 0, cols[0], jnp.where(where == 1, cols[1], jnp.where(where == 2, cols[2], cols[3])))
        crossed = jnp.where(where == 0, -cols[1], jnp.where(where == 1, cols[0], jnp.where(where == 2, -cols[3], cols[2])))
        z = z + straight * cos + crossed * sin
    out = mm3((high_ref[...], low_ref[...]), pieces(jnp.concatenate([z, -swapped(z, rows)], 0)))
    const = jnp.zeros((owners, 4 * rows), f32)
    real = jnp.zeros((owners, 4 * rows), f32)
    imag = jnp.zeros((owners, 4 * rows), f32)
    for i in range(4):
        real = jnp.where(where == i, tail[:, 8 + i : 9 + i], real)
        imag = jnp.where(where == i, tail[:, 12 + i : 13 + i], imag)
    const = real * zero_cos_ref[...] - imag * zero_sin_ref[...]
    const = const + pltpu.roll(const, 2 * rows, 1)
    const = const + pltpu.roll(const, rows, 1)
    out_ref[:, : 4 * rows] = out
    out_ref[:, 4 * rows :] = const


def grad_kernel(in_ref, high_ref, low_ref, out_ref):
    rows, length = out_ref.shape
    quarter = length // 4
    owners = in_ref.shape[0]
    a = in_ref[...]
    odd_row = row_index((owners, rows)) % 2 == 1
    none = jnp.zeros((owners, rows), f32)
    real0, imag0, real1, imag1 = (a[:, i * rows : (i + 1) * rows] for i in range(4))
    top = jnp.concatenate(
        [none, jnp.where(odd_row, real0, 0.0), jnp.where(odd_row, 0.0, real0), jnp.where(odd_row, 0.0, -imag0)], 1
    )
    top_sin = jnp.concatenate(
        [none, jnp.where(odd_row, -imag0, 0.0), jnp.where(odd_row, 0.0, -imag0), jnp.where(odd_row, 0.0, -real0)], 1
    )
    low = jnp.concatenate(
        [jnp.where(odd_row, real1, 0.0), none, jnp.where(odd_row, 0.0, real1), jnp.where(odd_row, 0.0, imag1)], 1
    )
    low_sin = jnp.concatenate(
        [jnp.where(odd_row, -imag1, 0.0), none, jnp.where(odd_row, 0.0, -imag1), jnp.where(odd_row, 0.0, real1)], 1
    )
    stack = jnp.concatenate([top, low, top_sin, low_sin], 0).T
    both = mm3(pieces(stack), (high_ref[...], low_ref[...]))
    const = jnp.sum(a[:, 4 * rows :].T, 1, keepdims=True)[:rows]
    e = both[:rows] + const
    f = both[rows : 2 * rows]
    g = both[2 * rows : 3 * rows]
    h = both[3 * rows :]
    up, down = e + f, e - f
    out_ref[:, :quarter] = up + g
    out_ref[:, quarter : 2 * quarter] = down + h
    out_ref[:, 2 * quarter : 3 * quarter] = up - g
    out_ref[:, 3 * quarter :] = down - h


def tables(rows, length, ring):
    owners = HALF // 2
    z = np.arange(ring)
    by_owner = np.stack([4 * z + c + 1 for c in range(2)], 1).reshape(-1)
    slots = np.concatenate([by_owner, by_owner + 2])
    cos, sin = turns(slots, np.arange(length // 4), length)
    row_table = np.concatenate([cos, sin], 0)
    cos, sin = turns(np.arange(owners), np.arange(owners), owners)
    dft = np.concatenate([cos, sin], 1)
    across = np.concatenate([np.arange(owners), owners * np.arange(8) - HALF])
    cos, sin = turns(across, np.arange(rows), length)
    turning = np.tile(cos, (1, 4)).astype(np.float32), np.tile(sin, (1, 4)).astype(np.float32)
    samples = (length // COARSE) * np.arange(COARSE)
    lanes = np.concatenate([4 * z + g + 1 for g in range(4)])
    first = np.concatenate([lanes[:-1], [0]])
    cos_p, sin_p = turns(first, samples[: COARSE // 4], length)
    cos_m, sin_m = turns(lanes, samples[: COARSE // 4], length)
    field = []
    for e in range(4):
        p, m = (slice(g * ring, (g + 1) * ring) for g in groups_of(e))
        real = np.concatenate([cos_p[p], -sin_p[p], cos_m[m], -sin_m[m]], 0)
        imag = np.concatenate([sin_p[p], cos_p[p], -sin_m[m], -cos_m[m]], 0)
        field.append(np.concatenate([real, imag], 1))
    field = np.concatenate(field, 0)
    tones = np.arange(1, COARSE // 2 + 1)
    share = np.where(tones == COARSE // 2, 1.0, 2.0)
    pixels = np.arange(length)
    kernel = (1.0 + np.cos(2.0 * np.pi * (np.outer(pixels, tones) % length) / length) @ share) / COARSE
    near, fine = samples[: COARSE // 4, None], pixels[None, : length // 4]
    h0, h1, h2, h3 = (kernel[(fine + p * (length // 4) - near) % length] for p in range(4))
    spread = np.concatenate([(h0 + h1 + h2 + h3) / 4, (h0 - h1 + h2 - h3) / 4, (h0 - h2) / 2, (h1 - h3) / 2], 0)
    return host_pieces(row_table), host_pieces(dft), turning, host_pieces(field), host_pieces(spread)


def call(kernel, out_shape, scratch=(), n_scalar=0, n_in=0, interpret=False, flops=0):
    vmem = pl.BlockSpec(memory_space=pltpu.VMEM)
    smem = pl.BlockSpec(memory_space=pltpu.SMEM)
    multi = isinstance(out_shape, (tuple, list))
    return pl.pallas_call(
        kernel,
        out_shape=out_shape,
        in_specs=[smem] * n_scalar + [vmem] * n_in,
        out_specs=[vmem] * len(out_shape) if multi else vmem,
        scratch_shapes=list(scratch),
        compiler_params=pltpu.CompilerParams(vmem_limit_bytes=56 * 1024 * 1024),
        interpret=interpret,
    )


INTERPRET = False


def on_device(mask_field, target_print, source_points, source_groups, group_logits, pupil_radius):
    rows, length = mask_field.shape
    ring = lax.axis_size(RING)
    pair = lax.axis_size(CORE)
    owners = ring * pair
    sources = source_points.shape[0]
    row_table, dft, turning, field, spread = tables(rows, length, ring)
    device = lax.axis_index(SLAB)
    norming = 1.0 / (length * length)
    cutoff = pupil_radius[0]
    shifted = (source_points - GRID // 2) * cutoff // shift_scale
    shape = functools.partial(jax.ShapeDtypeStruct, dtype=f32)
    run = functools.partial(call, interpret=INTERPRET)

    def swap_all(parcels, axes):
        return lax.all_to_all(parcels, axes, split_axis=0, concat_axis=0, tiled=True)

    parcels = run(rows_kernel, shape((owners, 8 * rows)), n_in=3)(mask_field, *row_table)
    arrived = swap_all(parcels, SLAB)
    piece, zero = run(columns_kernel, (shape((ring, PARCEL)), shape((8, K))), n_in=5)(arrived, *dft, *turning)
    around = swap_all(piece, RING)
    around = lax.all_gather(around, CORE).reshape(owners, PARCEL)

    onehot = (source_groups[:, None] == jnp.arange(NG, dtype=jnp.int32)[None, :]).astype(f32)
    weights = jnp.exp(jnp.sum(onehot * group_logits[None, :], 1))
    total_weight = jnp.sum(weights)
    weight_share = weights / total_weight
    across = jnp.arange(K, dtype=jnp.int32) - HALF
    across_m = jnp.where(across == -HALF, HALF, across)
    here = device * rows + jnp.arange(rows, dtype=jnp.int32)

    def local(freq):
        angle = jnp.mod(here[:, None] * freq[None, :], length).astype(f32) * (2.0 * np.pi / length)
        c, s = jnp.cos(angle), jnp.sin(angle)
        table = jnp.concatenate([jnp.concatenate([c, -s], 1), jnp.concatenate([s, c], 1)], 0)
        rounded = lax.reduce_precision(table, 8, 7)
        high, low = rounded.astype(bf16), (table - rounded).astype(bf16)
        return jnp.concatenate([high, low], 0), jnp.concatenate([high.T, high.T, low.T], 1)

    local_p, local_pt = local(across)
    local_m, local_mt = local(across_m)
    vmem = pltpu.VMEM
    out = run(
        image_kernel,
        shape((owners, PARCEL)),
        n_scalar=3,
        n_in=11,
        scratch=[
            vmem((2 * K, 2 * HALF), bf16),
            vmem((2 * K, 2 * HALF), bf16),
            vmem((sources * rows, 8 * HALF), bf16),
            vmem((sources * rows, 2 * COARSE), f32),
            vmem((sources * rows, 2 * COARSE), bf16),
            vmem((sources * rows, 2 * COARSE), bf16),
            vmem((sources * rows, 4 * HALF), f32),
            vmem((2 * K, HALF), f32),
            vmem((2 * K, HALF), f32),
            vmem((128, 128), f32),
        ],
    )(
        shifted,
        weight_share,
        pupil_radius,
        around,
        zero,
        local_p,
        local_m,
        local_pt,
        local_mt,
        *field,
        *spread,
        target_print,
    )
    parcels = out.reshape(pair, ring, PARCEL)
    mine = swap_all(parcels, CORE).sum(0)
    mine = swap_all(mine, RING)
    place = lax.axis_index(CORE) * ring + lax.axis_index(RING)
    own_across = place - HALF + owners * jnp.arange(K // owners, dtype=jnp.int32)
    pixels = jnp.arange(length, dtype=jnp.int32).reshape(owners, 1, rows)
    angle = jnp.mod(own_across[None, :, None] * pixels, length).astype(f32) * (2.0 * np.pi / length)
    zero_cos = jnp.cos(angle).reshape(owners, -1)
    zero_sin = jnp.sin(angle).reshape(owners, -1)
    parcels, sums = run(owner_kernel, (shape((owners, 8 * rows)), shape((8, 128))), n_in=7)(
        mine, *dft, *turning, zero_cos, zero_sin
    )
    arrived = swap_all(parcels, SLAB)
    mask_grad = run(grad_kernel, shape((rows, length)), n_in=3)(arrived, *row_table)
    per_source = sums[0, 16 : 16 + sources]
    squares = sums[0, 32]
    loss_value = (squares * norming).reshape(1)
    against = jnp.sum(weight_share * per_source)
    source_pull = weights * (per_source - against) / total_weight
    group_grad = jnp.sum(onehot * source_pull[:, None], 0) * norming
    return (loss_value, mask_grad, group_grad)


def solution(mesh):
    cores = 2
    ring = mesh.shape["slab"] // cores
    split = Mesh(mesh.devices.reshape(mesh.shape["clip"], ring, cores), CLIP_SLAB)
    return jax.shard_map(
        on_device,
        mesh=split,
        in_specs=(
            P(CLIP_SLAB, None),
            P(CLIP_SLAB, None),
            P("clip", None),
            P("clip"),
            P("clip"),
            P("clip"),
        ),
        out_specs=(P("clip"), P(CLIP_SLAB, None), P("clip")),
        check_vma=False,
    )
```

time: 597 us -> 214 us (0.36); the launches traced: 588 us -> 213 us
  matrix products: 234 us -> 0 us
  blocking collectives: 141 us -> 9.92 us
  waiting for transfers between devices: 131 us -> 98.9 us
  Pallas kernels: 0 us -> 28.7 us
  local copies, waits for them, and re-layouts: 27.3 us -> 11.7 us
  starting transfers between devices: 41.1 us -> 50.4 us
    dot_general x30 -> x0, matrix products: 234 us -> none  [the longest x27 211 us: contract(): return jnp.einsum(form, left, right, precision=highest)]
    all_gather x3 -> x1, blocking collectives: 112 us -> 4.88 us  [on_device(): around = lax.all_gather(around, CORE).reshape(owners, PARCEL)]
    all_to_all x2 -> x4, waiting for transfers between devices: 131 us -> 98.9 us  [swap_all(): lax.all_to_all(parcels, axes, split_axis=0, concat_axis=0, tiled=True)]
    pallas_call x0 -> x5, Pallas kernels: none -> 28.7 us  [the longest x1 19.6 us: on_device(): run(image_kernel, shape((owners, PARCEL)), n_scalar=3, n_in=11, scratch=[...]
    all_to_all x1, blocking collectives: 29.3 us -> 5.04 us  [swap_all(): lax.all_to_all(parcels, axes, split_axis=0, concat_axis=0, tiled=True)]
    all_to_all x2 -> x4, starting transfers between devices: 41.1 us -> 50.4 us  [swap_all(): lax.all_to_all(parcels, axes, split_axis=0, concat_axis=0, tiled=True)]
    unnamed x20 -> x9, local copies, waits for them, and re-layouts: 9.49 us -> 2.5 us
  transfers between devices with their start and end apart: 2 -> 4, of which waited for: 2 -> 4; matrix products, arithmetic and copies ran while one was open for 0% -> 5% of each run, Pallas kernels for 0% -> 0%
where the time goes in v1:
time: 214 us; the launch traced here: 213 us
  waiting for transfers between devices  98.9 us (46%)
  starting transfers between devices  50.4 us (24%)
  Pallas kernels  28.7 us (13%)
  local copies, waits for them, and re-layouts  11.7 us (5%)
  other arithmetic  10.3 us (5%)
  blocking collectives  9.92 us (5%)
  between operations  3.27 us (2%)
    all_to_all x4, waiting for transfers between devices, swap_all(): lax.all_to_all(parcels, axes, split_axis=0, concat_axis=0, tiled=True)  98.9 us
    all_to_all x4, starting transfers between devices, swap_all(): lax.all_to_all(parcels, axes, split_axis=0, concat_axis=0, tiled=True)  50.4 us
    pallas_call x1, Pallas kernels, on_device(): run(image_kernel, shape((owners, PARCEL)), n_scalar=3, n_in=11, scratch=[...  19.6 us
    all_to_all x5, local copies, waits for them, and re-layouts, swap_all(): lax.all_to_all(parcels, axes, split_axis=0, concat_axis=0, tiled=True)  5.55 us
    all_to_all x1, blocking collectives, swap_all(): lax.all_to_all(parcels, axes, split_axis=0, concat_axis=0, tiled=True)  5.04 us
    all_gather x1, blocking collectives, on_device(): around = lax.all_gather(around, CORE).reshape(owners, PARCEL)  4.88 us
  transfers between devices with their start and end apart: 4, of which 4 were waited for; matrix products, arithmetic and copies ran while one was open for 5% of the time, Pallas kernels for 0%

profile of v1, /device:TPU:37, one launch (start us, length us, event | category | flops | bytes accessed | tf_op | source)
XLA Modules:
  0.0 213.2 jit_solution(12988242465760577225)
XLA Ops:
  0.6 2.4 %shard_map.175 = f32[64,256]{1,0:T(8,128)} custom-call(f32[32,2048]{1,0:T(8,128)} %mask_ref.1, bf16[256,512]{1,0:T(8,128)(2,1)} %constant.97.clone.high_ref, bf16[256,512]{1,0:T(8,128)(2,1)} %constant.98.clone.low_ref), custom_call_target="tpu_custom_call" | custom-call | tf_op jit(solution)/shard_map/pallas_call | solution.py:501
  3.0 1.5 copy.55
  4.5 34.3 %all-to-all-start = ((f32[64,1,256]{2,1,0:T(1,128)}), f32[64,1,256]{2,1,0:T(1,128)S(1)}, u32[]{:S(2)}, u32[]{:S(2)}) async-start(f32[64,1,256]{2,1,0:T(1,128)} %copy.55), calls=%async_computation | async-start | bytes 131072 | tf_op jit(solution)/shard_map/all_to_all | solution.py:499
  38.9 0.3 fusion.16
  39.3 0.1 copy.60
  39.4 0.1 copy.61
  39.6 0.1 copy.58
  39.7 0.1 copy.59
  39.8 0.1 reduce-precision_convert_fusion
  40.0 0.1 pad_maximum_fusion.5
  40.1 0.1 reduce-precision_convert_fusion.1
  40.2 24.1 %all-to-all-done = f32[64,1,256]{2,1,0:T(1,128)S(1)} async-done(((f32[64,1,256]{2,1,0:T(1,128)}), f32[64,1,256]{2,1,0:T(1,128)S(1)}, u32[]{:S(2)}, u32[]{:S(2)}) %all-to-all-start) | async-done | bytes 65568 | tf_op jit(solution)/shard_map/all_to_all | solution.py:499
  64.3 0.6 copy.74
  64.9 2.2 %shard_map.176 = (f32[32,1152]{1,0:T(8,128)}, f32[8,256]{1,0:T(8,128)}) custom-call(f32[64,256]{1,0:T(8,128)} %bitcast.39, bf16[64,128]{1,0:T(8,128)(2,1)} %constant.99.clone.dft_high_ref.high_ref, bf16[64,128]{1,0:T(8,128)(2,1)} %constant.100.clone.dft_low_ref.low_ref, f32[72,128]{1,0:T(8,128)} %constant.101.clone.cos_ref, f32[72,128]{1,0:T(8,128)} %constant.102.clone.sin_ref), custom_call_target="tpu_custom_call" | custom-call | tf_op jit(solution)/shard_map/pallas_call | solution.py:503
  67.1 1.7 copy.56
  68.8 4.8 %all-to-all-start.1 = ((f32[32,1,1152]{2,1,0:T(1,128)}), f32[32,1,1152]{2,1,0:T(1,128)S(1)}, u32[]{:S(2)}, u32[]{:S(2)}) async-start(f32[32,1,1152]{2,1,0:T(1,128)} %copy.56), calls=%async_computation.1 | async-start | bytes 294912 | tf_op jit(solution)/shard_map/all_to_all | solution.py:499
  73.6 0.1 pad_maximum_fusion.4
  73.7 0.8 copy.63.local_m_ref
  74.5 0.8 copy.62.local_p_ref
  76.0 0.1 copy.54
  76.1 0.6 copy-done.1
  76.6 0.1 select_reduce_fusion.1
  76.7 0.6 exponential_reduce_fusion
  77.3 0.8 pad_maximum_fusion.3.local_mt_ref
  78.2 0.9 pad_maximum_fusion.2.local_pt_ref
  79.0 1.1 broadcast_divide_fusion.share_ref
  80.2 0.6 add_select_fusion.3.shift_ref
  80.8 22.9 %all-to-all-done.1 = f32[32,1,1152]{2,1,0:T(1,128)S(1)} async-done(((f32[32,1,1152]{2,1,0:T(1,128)}), f32[32,1,1152]{2,1,0:T(1,128)S(1)}, u32[]{:S(2)}, u32[]{:S(2)}) %all-to-all-start.1) | async-done | bytes 147488 | tf_op jit(solution)/shard_map/all_to_all | solution.py:499
  103.7 4.9 %all-gather = f32[64,1,1152]{2,0,1:T(8,128)} all-gather(f32[32,1,1152]{2,0,1:T(8,128)S(1)} %copy.57), channel_id=2, replica_groups=mesh['clip'=4,'slab_0'=32,'slab_1'=2] {'slab_1'}, dimensions={0}, use_global_device_ids=true | all-gather | bytes 442368 | tf_op jit(solution)/shard_map/all_gather | solution.py:505
  108.6 19.6 %shard_map.177 = f32[64,1152]{1,0:T(8,128)} custom-call(s32[16,2]{1,0:T(8,128)} %add_select_fusion.3.shift_ref, f32[16]{0:T(128)} %broadcast_divide_fusion.share_ref, s32[1]{0:T(128)} %copy.75.radius_ref, f32[64,1152]{1,0:T(8,128)} %bitcast.31, f32[8,256]{1,0:T(8,128)} %get-tuple-element.8.zero_ref, bf16[128,512]{1,0:T(8,128)(2,1)} %copy.62.local_p_ref, ...), custom_call_target="tpu_custom_call" | custom-call | tf_op jit(solution)/shard_map/pallas_call | solution.py:526
  128.2 5.0 %all_to_all.47 = f32[2,32,1152]{2,1,0:T(8,128)S(1)} all-to-all(f32[2,32,1152]{2,1,0:T(8,128)} %bitcast.32), channel_id=1, replica_groups=mesh['clip'=4,'slab_0'=32,'slab_1'=2] {'slab_1'}, dimensions={0} | all-to-all | bytes 589824 | tf_op jit(solution)/shard_map/all_to_all | solution.py:499
  133.3 0.8 all_to_all.36
  134.0 4.8 %all-to-all-start.3 = ((f32[32,1,1152]{2,1,0:T(1,128)}), f32[32,1,1152]{2,1,0:T(1,128)S(1)}, u32[]{:S(2)}, u32[]{:S(2)}) async-start(f32[32,1,1152]{2,1,0:T(1,128)} %all_to_all.36), calls=%async_computation.3 | async-start | bytes 294912 | tf_op jit(solution)/shard_map/all_to_all | solution.py:499
  138.9 0.1 mul.130
  139.1 0.8 fusion.18
  139.8 30.4 %all-to-all-done.3 = f32[32,1,1152]{2,1,0:T(1,128)S(1)} async-done(((f32[32,1,1152]{2,1,0:T(1,128)}), f32[32,1,1152]{2,1,0:T(1,128)S(1)}, u32[]{:S(2)}, u32[]{:S(2)}) %all-to-all-start.3) | async-done | bytes 147488 | tf_op jit(solution)/shard_map/all_to_all | solution.py:499
  170.2 0.7 copy.72
  170.9 2.4 %shard_map.178 = (f32[64,256]{1,0:T(8,128)}, f32[8,128]{1,0:T(8,128)}) custom-call(f32[32,1152]{1,0:T(8,128)} %bitcast.37, bf16[64,128]{1,0:T(8,128)(2,1)} %constant.99.clone.dft_high_ref.high_ref, bf16[64,128]{1,0:T(8,128)(2,1)} %constant.100.clone.dft_low_ref.low_ref, f32[72,128]{1,0:T(8,128)} %constant.101.clone.cos_ref, ...), custom_call_target="tpu_custom_call" | custom-call | tf_op jit(solution)/shard_map/pallas_call | solution.py:566
  173.3 1.9 fusion.20
  175.2 1.3 slice.6
  176.5 1.5 copy.65
  178.0 6.5 %all-to-all-start.4 = ((f32[64,1,256]{2,1,0:T(1,128)}), f32[64,1,256]{2,1,0:T(1,128)S(1)}, u32[]{:S(2)}, u32[]{:S(2)}) async-start(f32[64,1,256]{2,1,0:T(1,128)} %copy.65), calls=%async_computation.4 | async-start | bytes 131072 | tf_op jit(solution)/shard_map/all_to_all | solution.py:499
  185.2 1.9 fusion.22
  187.1 0.1 select_reduce_fusion
  187.2 0.5 broadcast_multiply_fusion
  187.7 21.5 %all-to-all-done.4 = f32[64,1,256]{2,1,0:T(1,128)S(1)} async-done(((f32[64,1,256]{2,1,0:T(1,128)}), f32[64,1,256]{2,1,0:T(1,128)S(1)}, u32[]{:S(2)}, u32[]{:S(2)}) %all-to-all-start.4) | async-done | bytes 65568 | tf_op jit(solution)/shard_map/all_to_all | solution.py:499
  209.3 0.6 copy.73
  209.9 2.2 %shard_map.179 = f32[32,2048]{1,0:T(8,128)} custom-call(f32[64,256]{1,0:T(8,128)} %bitcast.40, bf16[256,512]{1,0:T(8,128)(2,1)} %constant.97.clone.high_ref, bf16[256,512]{1,0:T(8,128)(2,1)} %constant.98.clone.low_ref), custom_call_target="tpu_custom_call" | custom-call | tf_op jit(solution)/shard_map/pallas_call | solution.py:570
  (17 shorter events, 0.3 us)
Async XLA Ops:
  4.5 59.8 %all-to-all-start = ((f32[64,1,256]{2,1,0:T(1,128)}), f32[64,1,256]{2,1,0:T(1,128)S(1)}, u32[]{:S(2)}, u32[]{:S(2)}) async-start(f32[64,1,256]{2,1,0:T(1,128)} %copy.55), calls=%async_computation | async-start | bytes 131072 | tf_op jit(solution)/shard_map/all_to_all | solution.py:499
  68.8 34.9 %all-to-all-start.1 = ((f32[32,1,1152]{2,1,0:T(1,128)}), f32[32,1,1152]{2,1,0:T(1,128)S(1)}, u32[]{:S(2)}, u32[]{:S(2)}) async-start(f32[32,1,1152]{2,1,0:T(1,128)} %copy.56), calls=%async_computation.1 | async-start | bytes 294912 | tf_op jit(solution)/shard_map/all_to_all | solution.py:499
  75.3 0.7 copy-start
  75.9 0.7 copy-start.1
  76.0 0.7 copy-start.2
  134.0 36.2 %all-to-all-start.3 = ((f32[32,1,1152]{2,1,0:T(1,128)}), f32[32,1,1152]{2,1,0:T(1,128)S(1)}, u32[]{:S(2)}, u32[]{:S(2)}) async-start(f32[32,1,1152]{2,1,0:T(1,128)} %all_to_all.36), calls=%async_computation.3 | async-start | bytes 294912 | tf_op jit(solution)/shard_map/all_to_all | solution.py:499
  178.0 31.3 %all-to-all-start.4 = ((f32[64,1,256]{2,1,0:T(1,128)}), f32[64,1,256]{2,1,0:T(1,128)S(1)}, u32[]{:S(2)}, u32[]{:S(2)}) async-start(f32[64,1,256]{2,1,0:T(1,128)} %copy.65), calls=%async_computation.4 | async-start | bytes 131072 | tf_op jit(solution)/shard_map/all_to_all | solution.py:499

commit v2 on v1

--- a/solution.py
+++ b/solution.py
@@ -80,7 +80,7 @@
     return cos * cos_m - sin * sin_m, sin * cos_m + cos * sin_m
 
 
-def rows_kernel(mask_ref, high_ref, low_ref, out_ref):
+def rows_kernel(mask_ref, high_ref, low_ref, out_ref, sums_ref):
     rows, length = mask_ref.shape
     quarter = length // 4
     m0, m1, m2, m3 = (mask_ref[:, q * quarter : (q + 1) * quarter] for q in range(4))
@@ -94,52 +94,53 @@
     owners = HALF // 2
     odd_row = row_index((owners, rows)) % 2 == 1
     lo, hi = slice(0, owners), slice(owners, HALF)
-    ones = jnp.ones((owners, quarter), bf16)
-    sums = (mm(ones, stack[0], NT) + mm(ones, stack[1], NT))[:, :rows]
-    out_ref[:, :] = jnp.concatenate(
+    ones = jnp.ones((8, quarter), bf16)
+    sums_ref[...] = (mm(ones, stack[0], NT) + mm(ones, stack[1], NT))[:1]
+    parcels = jnp.concatenate(
         [
             jnp.where(odd_row, c2[lo], ca[lo] - sb[lo]),
             jnp.where(odd_row, -s2[lo], -sa[lo] - cb[lo]),
             jnp.where(odd_row, c0[hi], ca[hi] + sb[hi]),
             jnp.where(odd_row, -s0[hi], cb[hi] - sa[hi]),
-            sums,
-            jnp.zeros((owners, 3 * rows), f32),
         ],
         1,
     )
-
-
-def columns_kernel(in_ref, dft_high_ref, dft_low_ref, cos_ref, sin_ref, piece_ref, zero_ref):
-    owners, lanes = in_ref.shape
-    rows = lanes // 8
-    a = in_ref[...]
+    out_ref[...] = parcels.reshape(out_ref.shape)
+
+
+def columns_kernel(in_ref, own_sums_ref, dft_high_ref, dft_low_ref, cos_ref, sin_ref, piece_ref):
+    owners, _, lanes = in_ref.shape
+    rows = lanes // 4
+    a = in_ref[...].reshape(owners, lanes)
     z = mm3((dft_high_ref[...], dft_low_ref[...]), pieces(jnp.concatenate([a, swapped(a, rows)], 0)))
     turned = swapped(z, rows)
     blocks = []
     for m in range(5):
         cos, sin = twiddle(cos_ref, sin_ref, m)
-        cos = jnp.concatenate([cos, cos], 1)
-        sin = jnp.concatenate([sin, sin], 1)
         blocks.append(z * cos + turned * sin)
     high, low = pieces(jnp.concatenate(blocks, 0))
     pick = (row_index((8, lanes)) == lane_index((8, lanes)) // rows).astype(f32).astype(bf16)
     sums = mm(pick, high, NT) + mm(pick, low, NT)
     copies = piece_ref.shape[0]
-    lane = lane_index((copies, 128))
-    tail = jnp.zeros((copies, 128), f32)
+    lane = lane_index((1, 128))
+    tail = jnp.where(lane // rows == 1, pltpu.roll(own_sums_ref[...], rows, 1), 0.0)
     for q in range(4):
-        piece_ref[:, q * K : (q + 1) * K] = jnp.broadcast_to(sums[q : q + 1, :K], (copies, K))
         tail = jnp.where(lane == q, sums[q : q + 1, K : K + 1], tail)
-    piece_ref[:, 4 * K :] = tail
-    zero_ref[...] = sums[:, :K]
+    row = jnp.concatenate([sums[q : q + 1, :K] for q in range(4)] + [tail], 1)
+    piece_ref[...] = jnp.broadcast_to(row.reshape(1, 1, PARCEL), (copies, 1, PARCEL))
 
 
 def image_kernel(
     shift_ref,
     share_ref,
     radius_ref,
-    around_ref,
-    zero_ref,
+    core_ref,
+    mine_ref,
+    theirs_ref,
+    turn_high_ref,
+    turn_low_ref,
+    cos_ref,
+    sin_ref,
     local_p_ref,
     local_m_ref,
     local_pt_ref,
@@ -149,7 +150,8 @@
     spread_high_ref,
     spread_low_ref,
     target_ref,
-    out_ref,
+    out_mine_ref,
+    out_theirs_ref,
     plus_ref,
     minus_ref,
     lift_ref,
@@ -166,13 +168,24 @@
     half = 2 * rows
     norming = 1.0 / (target_ref.shape[1] * target_ref.shape[1])
     radius_sq = radius_ref[0] * radius_ref[0]
-    wide = around_ref[...]
+    first_core = core_ref[0] == 0
+    ring = mine_ref.shape[0]
+    mine = mine_ref[...].reshape(ring, PARCEL)
+    theirs = theirs_ref[...].reshape(ring, PARCEL)
+    wide = jnp.concatenate([jnp.where(first_core, mine, theirs), jnp.where(first_core, theirs, mine)], 0)
     body = jnp.concatenate([wide[:, : 2 * K], wide[:, 2 * K : 4 * K]], 0)
     spectrum = body.T
     tail = wide[:, 4 * K :].T
-    zero = zero_ref[...].T
+    turn = turn_high_ref[...], turn_low_ref[...]
+    owners = 2 * ring
+    z = mm3(turn, pieces(wide[:, 4 * K + rows : 4 * K + 2 * rows]), TN)
+    z_real, z_imag = z[:owners], -z[owners:]
+    turns_of = [tuple(t[:, :rows] for t in twiddle(cos_ref, sin_ref, m)) for m in range(4)]
+    zero = [
+        jnp.concatenate([jnp.sum(z_real * c + z_imag * n, 1, keepdims=True) for c, n in turns_of], 0),
+        jnp.concatenate([jnp.sum(z_imag * c - z_real * n, 1, keepdims=True) for c, n in turns_of], 0),
+    ]
     lane = lane_index((1, HALF))
-    ring = HALF // 4
     frequency = 4 * (lane % ring) + lane // ring + 1
     last = lane == HALF - 1
     frequency_p = jnp.where(last, 0, frequency)
@@ -182,7 +195,7 @@
     first_row = row_index((K, HALF)) == 0
     for part in range(2):
         block = spectrum[part * K : (part + 1) * K]
-        plus = jnp.where(last_col, zero[:, 4 + part : 5 + part], block)
+        plus = jnp.where(last_col, zero[part], block)
         edge = jnp.concatenate([tail[part : part + 1], tail[2 + part : 3 + part]], 1)
         minus = jnp.where(first_row, edge, block)
         for ref, value in ((plus_ref, plus), (minus_ref, minus)):
@@ -291,7 +304,7 @@
         return total
 
     sums_ref[...] = jnp.zeros(sums_ref.shape, f32)
-    sums_ref[32:33, :] = lane_sum(squares)
+    sums_ref[8:9, :] = lane_sum(squares)
     for ref in (pull_p_ref, pull_m_ref):
         ref[...] = jnp.zeros(ref.shape, f32)
 
@@ -341,28 +354,35 @@
     lax.fori_loop(0, sources, pull, 0)
     plus = pull_p_ref[...]
     minus = pull_m_ref[...]
-    owners = HALF // 2
+    y_real = jnp.zeros((owners, rows), f32)
+    y_imag = jnp.zeros((owners, rows), f32)
+    for m, (c, n) in enumerate(turns_of):
+        real = plus[m * owners : (m + 1) * owners, HALF - 1 :]
+        imag = plus[K + m * owners : K + (m + 1) * owners, HALF - 1 :]
+        y_real = y_real + (real * c - imag * n)
+        y_imag = y_imag + (real * n + imag * c)
+    level = mm3(turn, pieces(jnp.concatenate([y_real, -y_imag], 0)))
     sums = jnp.sum(sums_ref[...].T, 0, keepdims=True)
     lane = lane_index((owners, 128))
-    tail = jnp.where(lane >= 16, sums, 0.0)
-    for i in range(8):
-        tail = jnp.where(lane == 8 + i, plus[i * owners : (i + 1) * owners, HALF - 1 :], tail)
+    level = jnp.concatenate([level] * 4, 1)
+    tail = jnp.where(lane // rows == 1, level, sums)
     edge = jnp.concatenate([minus[:1], minus[K : K + 1], jnp.zeros((6, HALF), f32)], 0).T
     for j in range(2):
         for part in range(2):
             tail = jnp.where(lane == 2 * j + part, edge[j * owners : (j + 1) * owners, part : part + 1], tail)
-    out_ref[:, 4 * K :] = tail
     total = jnp.where(lane_index(plus.shape) == HALF - 1, 0.0, plus)
     total = total + jnp.where(row_index(plus.shape) % K == 0, 0.0, minus)
     total = total.T
-    out_ref[:, : 2 * K] = total[:owners]
-    out_ref[:, 2 * K : 4 * K] = total[owners:]
-
-
-def owner_kernel(in_ref, high_ref, low_ref, cos_ref, sin_ref, zero_cos_ref, zero_sin_ref, out_ref, sums_ref):
-    total = jnp.sum(in_ref[...], 0, keepdims=True)
+    row = jnp.concatenate([total[:owners], total[owners:], tail], 1)
+    low, high = row[:ring], row[ring:]
+    out_mine_ref[...] = jnp.where(first_core, low, high).reshape(out_mine_ref.shape)
+    out_theirs_ref[...] = jnp.where(first_core, high, low).reshape(out_theirs_ref.shape)
+
+
+def owner_kernel(in_ref, high_ref, low_ref, cos_ref, sin_ref, out_ref, sums_ref):
+    total = jnp.sum(in_ref[...], 0)
     tail = total[:, 4 * K :]
-    sums_ref[...] = jnp.broadcast_to(tail, sums_ref.shape)
+    sums_ref[...] = tail
     owners = HALF // 2
     rows = cos_ref.shape[1] // 4
     quantities = [total[:, q * K : (q + 1) * K] for q in range(4)]
@@ -382,24 +402,14 @@
         crossed = jnp.where(where == 0, -cols[1], jnp.where(where == 1, cols[0], jnp.where(where == 2, -cols[3], cols[2])))
         z = z + straight * cos + crossed * sin
     out = mm3((high_ref[...], low_ref[...]), pieces(jnp.concatenate([z, -swapped(z, rows)], 0)))
-    const = jnp.zeros((owners, 4 * rows), f32)
-    real = jnp.zeros((owners, 4 * rows), f32)
-    imag = jnp.zeros((owners, 4 * rows), f32)
-    for i in range(4):
-        real = jnp.where(where == i, tail[:, 8 + i : 9 + i], real)
-        imag = jnp.where(where == i, tail[:, 12 + i : 13 + i], imag)
-    const = real * zero_cos_ref[...] - imag * zero_sin_ref[...]
-    const = const + pltpu.roll(const, 2 * rows, 1)
-    const = const + pltpu.roll(const, rows, 1)
-    out_ref[:, : 4 * rows] = out
-    out_ref[:, 4 * rows :] = const
-
-
-def grad_kernel(in_ref, high_ref, low_ref, out_ref):
+    out_ref[...] = out.reshape(out_ref.shape)
+
+
+def grad_kernel(in_ref, sums_ref, share_ref, group_ref, high_ref, low_ref, out_ref, loss_ref, group_out_ref):
     rows, length = out_ref.shape
     quarter = length // 4
     owners = in_ref.shape[0]
-    a = in_ref[...]
+    a = in_ref[...].reshape(owners, 4 * rows)
     odd_row = row_index((owners, rows)) % 2 == 1
     none = jnp.zeros((owners, rows), f32)
     real0, imag0, real1, imag1 = (a[:, i * rows : (i + 1) * rows] for i in range(4))
@@ -417,7 +427,8 @@
     )
     stack = jnp.concatenate([top, low, top_sin, low_sin], 0).T
     both = mm3(pieces(stack), (high_ref[...], low_ref[...]))
-    const = jnp.sum(a[:, 4 * rows :].T, 1, keepdims=True)[:rows]
+    sums = sums_ref[...]
+    const = jnp.broadcast_to(sums, (8, 128)).T[rows : 2 * rows, :1]
     e = both[:rows] + const
     f = both[rows : 2 * rows]
     g = both[2 * rows : 3 * rows]
@@ -427,6 +438,12 @@
     out_ref[:, quarter : 2 * quarter] = down + h
     out_ref[:, 2 * quarter : 3 * quarter] = up - g
     out_ref[:, 3 * quarter :] = down - h
+    norming = 1.0 / (length * length)
+    loss_ref[...] = sums[:, 8:9] * norming
+    share = share_ref[...]
+    against = jnp.sum(share * sums, 1, keepdims=True)
+    pull = share * (sums - against) * norming
+    group_out_ref[...] = jnp.sum((group_ref[...] * pull).T, 0, keepdims=True)
 
 
 def tables(rows, length, ring):
@@ -438,6 +455,8 @@
     row_table = np.concatenate([cos, sin], 0)
     cos, sin = turns(np.arange(owners), np.arange(owners), owners)
     dft = np.concatenate([cos, sin], 1)
+    in_order = np.concatenate([2 * z, 2 * z + 1])
+    turn = dft[in_order]
     across = np.concatenate([np.arange(owners), owners * np.arange(8) - HALF])
     cos, sin = turns(across, np.arange(rows), length)
     turning = np.tile(cos, (1, 4)).astype(np.float32), np.tile(sin, (1, 4)).astype(np.float32)
@@ -460,7 +479,7 @@
     near, fine = samples[: COARSE // 4, None], pixels[None, : length // 4]
     h0, h1, h2, h3 = (kernel[(fine + p * (length // 4) - near) % length] for p in range(4))
     spread = np.concatenate([(h0 + h1 + h2 + h3) / 4, (h0 - h1 + h2 - h3) / 4, (h0 - h2) / 2, (h1 - h3) / 2], 0)
-    return host_pieces(row_table), host_pieces(dft), turning, host_pieces(field), host_pieces(spread)
+    return host_pieces(row_table), host_pieces(dft), host_pieces(turn), turning, host_pieces(field), host_pieces(spread)
 
 
 def call(kernel, out_shape, scratch=(), n_scalar=0, n_in=0, interpret=False, flops=0):
@@ -478,6 +497,22 @@
     )
 
 
+def image_scratch(sources, rows):
+    vmem = pltpu.VMEM
+    return [
+        vmem((2 * K, 2 * HALF), bf16),
+        vmem((2 * K, 2 * HALF), bf16),
+        vmem((sources * rows, 8 * HALF), bf16),
+        vmem((sources * rows, 2 * COARSE), f32),
+        vmem((sources * rows, 2 * COARSE), bf16),
+        vmem((sources * rows, 2 * COARSE), bf16),
+        vmem((sources * rows, 4 * HALF), f32),
+        vmem((2 * K, HALF), f32),
+        vmem((2 * K, HALF), f32),
+        vmem((128, 128), f32),
+    ]
+
+
 INTERPRET = False
 
 
@@ -487,7 +522,7 @@
     pair = lax.axis_size(CORE)
     owners = ring * pair
     sources = source_points.shape[0]
-    row_table, dft, turning, field, spread = tables(rows, length, ring)
+    row_table, dft, turn, turning, field, spread = tables(rows, length, ring)
     device = lax.axis_index(SLAB)
     norming = 1.0 / (length * length)
     cutoff = pupil_radius[0]
@@ -498,11 +533,11 @@
     def swap_all(parcels, axes):
         return lax.all_to_all(parcels, axes, split_axis=0, concat_axis=0, tiled=True)
 
-    parcels = run(rows_kernel, shape((owners, 8 * rows)), n_in=3)(mask_field, *row_table)
+    parcels, own_sums = run(rows_kernel, (shape((owners, 1, 4 * rows)), shape((1, 128))), n_in=3)(mask_field, *row_table)
     arrived = swap_all(parcels, SLAB)
-    piece, zero = run(columns_kernel, (shape((ring, PARCEL)), shape((8, K))), n_in=5)(arrived, *dft, *turning)
+    piece = run(columns_kernel, shape((ring, 1, PARCEL)), n_in=6)(arrived, own_sums, *dft, *turning)
     around = swap_all(piece, RING)
-    around = lax.all_gather(around, CORE).reshape(owners, PARCEL)
+    theirs = lax.ppermute(around, CORE, [(i, (i + 1) % pair) for i in range(pair)])
 
     onehot = (source_groups[:, None] == jnp.arange(NG, dtype=jnp.int32)[None, :]).astype(f32)
     weights = jnp.exp(jnp.sum(onehot * group_logits[None, :], 1))
@@ -522,30 +557,21 @@
 
     local_p, local_pt = local(across)
     local_m, local_mt = local(across_m)
-    vmem = pltpu.VMEM
-    out = run(
+    mine, theirs = run(
         image_kernel,
-        shape((owners, PARCEL)),
-        n_scalar=3,
-        n_in=11,
-        scratch=[
-            vmem((2 * K, 2 * HALF), bf16),
-            vmem((2 * K, 2 * HALF), bf16),
-            vmem((sources * rows, 8 * HALF), bf16),
-            vmem((sources * rows, 2 * COARSE), f32),
-            vmem((sources * rows, 2 * COARSE), bf16),
-            vmem((sources * rows, 2 * COARSE), bf16),
-            vmem((sources * rows, 4 * HALF), f32),
-            vmem((2 * K, HALF), f32),
-            vmem((2 * K, HALF), f32),
-            vmem((128, 128), f32),
-        ],
+        (shape((ring, 1, PARCEL)),) * 2,
+        n_scalar=4,
+        n_in=15,
+        scratch=image_scratch(sources, rows),
     )(
         shifted,
         weight_share,
         pupil_radius,
+        lax.axis_index(CORE).reshape(1),
         around,
-        zero,
+        theirs,
+        *turn,
+        *turning,
         local_p,
         local_m,
         local_pt,
@@ -554,27 +580,16 @@
         *spread,
         target_print,
     )
-    parcels = out.reshape(pair, ring, PARCEL)
-    mine = swap_all(parcels, CORE).sum(0)
+    mine = mine + lax.ppermute(theirs, CORE, [(i, (i + 1) % pair) for i in range(pair)])
     mine = swap_all(mine, RING)
-    place = lax.axis_index(CORE) * ring + lax.axis_index(RING)
-    own_across = place - HALF + owners * jnp.arange(K // owners, dtype=jnp.int32)
-    pixels = jnp.arange(length, dtype=jnp.int32).reshape(owners, 1, rows)
-    angle = jnp.mod(own_across[None, :, None] * pixels, length).astype(f32) * (2.0 * np.pi / length)
-    zero_cos = jnp.cos(angle).reshape(owners, -1)
-    zero_sin = jnp.sin(angle).reshape(owners, -1)
-    parcels, sums = run(owner_kernel, (shape((owners, 8 * rows)), shape((8, 128))), n_in=7)(
-        mine, *dft, *turning, zero_cos, zero_sin
-    )
+    parcels, sums = run(owner_kernel, (shape((owners, 1, 4 * rows)), shape((1, 128))), n_in=5)(mine, *dft, *turning)
     arrived = swap_all(parcels, SLAB)
-    mask_grad = run(grad_kernel, shape((rows, length)), n_in=3)(arrived, *row_table)
-    per_source = sums[0, 16 : 16 + sources]
-    squares = sums[0, 32]
-    loss_value = (squares * norming).reshape(1)
-    against = jnp.sum(weight_share * per_source)
-    source_pull = weights * (per_source - against) / total_weight
-    group_grad = jnp.sum(onehot * source_pull[:, None], 0) * norming
-    return (loss_value, mask_grad, group_grad)
+    share_row = jnp.zeros((1, 128), f32).at[0, 16 : 16 + sources].set(weight_share)
+    group_rows = jnp.zeros((NG, 128), f32).at[:, 16 : 16 + sources].set(onehot.T)
+    mask_grad, loss_value, group_grad = run(
+        grad_kernel, (shape((rows, length)), shape((1, 1)), shape((1, NG))), n_in=6
+    )(arrived, sums, share_row, group_rows, *row_table)
+    return (loss_value.reshape(1), mask_grad, group_grad.reshape(NG))
 
 
 def solution(mesh):

time: 214 us -> 197 us (0.921)
  waiting for transfers between devices: 98.9 us -> 65.2 us
  blocking collectives: 9.92 us -> 36.1 us
  local copies, waits for them, and re-layouts: 11.7 us -> 6.14 us
    all_to_all x4 -> x3, waiting for transfers between devices: 98.9 us -> 64 us  [swap_all(): lax.all_to_all(parcels, axes, split_axis=0, concat_axis=0, tiled=True)]
    all_to_all x1, blocking collectives: 5.04 us -> 36.1 us  [swap_all(): lax.all_to_all(parcels, axes, split_axis=0, concat_axis=0, tiled=True)]
    all_to_all x5 -> x0, local copies, waits for them, and re-layouts: 5.55 us -> none  [swap_all(): lax.all_to_all(parcels, axes, split_axis=0, concat_axis=0, tiled=True)]
    all_gather x1 -> x0, blocking collectives: 4.88 us -> none  [on_device(): around = lax.all_gather(around, CORE).reshape(owners, PARCEL)]
    all_to_all x4 -> x3, starting transfers between devices: 50.4 us -> 45.7 us  [swap_all(): lax.all_to_all(parcels, axes, split_axis=0, concat_axis=0, tiled=True)]
    ppermute x0 -> x2, starting transfers between devices: none -> 3.8 us  [the longest x1 3.26 us: on_device(): lax.ppermute(around, CORE, [(i, (i + 1) % pair) for i in range(pair)])]
    another operation x0 -> x5, other arithmetic: none -> 3.75 us
    div x2 -> x0, other arithmetic: 3.03 us -> none  [the longest x1 1.91 us: on_device(): source_pull = weights * (per_source - against) / total_weight]
  transfers between devices with their start and end apart: 4 -> 5, of which waited for: 4 -> 4; matrix products, arithmetic and copies ran while one was open for 5% -> 6% of each run, Pallas kernels for 0% -> 0%
where the time goes in v2:
time: 197 us; the launch traced here: 196 us
  waiting for transfers between devices  65.2 us (33%)
  starting transfers between devices  49.5 us (25%)
  blocking collectives  36.1 us (18%)
  Pallas kernels  29.3 us (15%)
  other arithmetic  8.71 us (4%)
  local copies, waits for them, and re-layouts  6.14 us (3%)
    all_to_all x3, waiting for transfers between devices, swap_all(): lax.all_to_all(parcels, axes, split_axis=0, concat_axis=0, tiled=True)  64 us
    all_to_all x3, starting transfers between devices, swap_all(): lax.all_to_all(parcels, axes, split_axis=0, concat_axis=0, tiled=True)  45.7 us
    all_to_all x1, blocking collectives, swap_all(): lax.all_to_all(parcels, axes, split_axis=0, concat_axis=0, tiled=True)  36.1 us
    pallas_call x1, Pallas kernels, on_device(): run(image_kernel, (shape((ring, 1, PARCEL)),) * 2, n_scalar=4, n_in=15, s...  20.2 us
  transfers between devices with their start and end apart: 5, of which 4 were waited for; matrix products, arithmetic and copies ran while one was open for 6% of the time, Pallas kernels for 0%

profile of v2, /device:TPU:37, one launch (start us, length us, event | category | flops | bytes accessed | tf_op | source)
XLA Modules:
  0.0 196.4 jit_solution(14116353268881104749)
XLA Ops:
  0.6 2.4 %shard_map.193 = (f32[64,1,128]{2,1,0:T(1,128)}, f32[1,128]{1,0:T(1,128)}) custom-call(f32[32,2048]{1,0:T(8,128)} %mask_ref.1, bf16[256,512]{1,0:T(8,128)(2,1)} %constant.132.clone.high_ref, bf16[256,512]{1,0:T(8,128)(2,1)} %constant.133.clone.low_ref), custom_call_target="tpu_custom_call" | custom-call | tf_op jit(solution)/shard_map/pallas_call | solution.py:536
  3.0 34.3 %all-to-all-start = ((f32[64,1,128]{2,1,0:T(1,128)}), f32[64,1,128]{2,1,0:T(1,128)S(1)}, u32[]{:S(2)}, u32[]{:S(2)}) async-start(f32[64,1,128]{2,1,0:T(1,128)} %get-tuple-element.36), calls=%async_computation | async-start | bytes 65536 | tf_op jit(solution)/shard_map/all_to_all | solution.py:534
  37.4 0.3 fusion.13
  37.8 0.1 copy.44
  37.9 0.1 copy.45
  38.0 0.1 copy.42
  38.2 0.1 copy.43
  38.3 0.0 copy-start.4
  39.0 0.0 copy-done.4
  39.0 0.1 copy.41
  39.1 0.6 and_reduce_fusion
  39.7 19.5 %all-to-all-done.in_ref = f32[64,1,128]{2,1,0:T(1,128)S(1)} async-done(((f32[64,1,128]{2,1,0:T(1,128)}), f32[64,1,128]{2,1,0:T(1,128)S(1)}, u32[]{:S(2)}, u32[]{:S(2)}) %all-to-all-start) | async-done | bytes 32800 | tf_op jit(solution)/shard_map/all_to_all | solution.py:534
  59.2 0.6 copy-done.2
  59.8 2.1 %shard_map.194 = f32[32,1,1152]{2,1,0:T(1,128)} custom-call(f32[64,1,128]{2,1,0:T(1,128)} %copy-done.2, f32[1,128]{1,0:T(1,128)} %get-tuple-element.37.own_sums_ref, bf16[64,128]{1,0:T(8,128)(2,1)} %constant.134.clone.dft_high_ref.high_ref, bf16[64,128]{1,0:T(8,128)(2,1)} %constant.135.clone.dft_low_ref.low_ref, f32[72,128]{1,0:T(8,128)} %constant.136.clone.cos_ref, ...), custom_call_target="tpu_custom_call" | custom-call | tf_op jit(solution)/shard_map/pallas_call | solution.py:538
  61.9 4.9 %all-to-all-start.1 = ((f32[32,1,1152]{2,1,0:T(1,128)}), f32[32,1,1152]{2,1,0:T(1,128)S(1)}, u32[]{:S(2)}, u32[]{:S(2)}) async-start(f32[32,1,1152]{2,1,0:T(1,128)} %shard_map.194), calls=%async_computation.1 | async-start | bytes 294912 | tf_op jit(solution)/shard_map/all_to_all | solution.py:534
  66.8 0.0 copy-done.5
  66.8 0.0 copy-done.7
  66.8 0.1 select_reduce_fusion
  66.9 0.6 exponential_reduce_fusion
  67.5 0.1 reduce-precision_convert_fusion
  67.7 0.1 pad_maximum_fusion.5
  67.8 0.8 pad_maximum_fusion.3.local_mt_ref
  68.6 0.1 reduce-precision_convert_fusion.1
  68.8 1.8 fusion.15
  70.6 0.6 add_select_fusion.2.shift_ref
  71.2 25.5 %all-to-all-done.1.mine_ref = f32[32,1,1152]{2,1,0:T(1,128)S(1)} async-done(((f32[32,1,1152]{2,1,0:T(1,128)}), f32[32,1,1152]{2,1,0:T(1,128)S(1)}, u32[]{:S(2)}, u32[]{:S(2)}) %all-to-all-start.1) | async-done | bytes 147488 | tf_op jit(solution)/shard_map/all_to_all | solution.py:534
  96.7 3.3 %collective-permute-start = (f32[32,1,1152]{2,1,0:T(1,128)S(1)}, f32[32,1,1152]{2,1,0:T(1,128)S(1)}, u32[]{:S(2)}, u32[]{:S(2)}) collective-permute-start(f32[32,1,1152]{2,1,0:T(1,128)S(1)} %all-to-all-done.1.mine_ref), channel_id=1, source_target_pairs={{0,1},{1,0},{2,3},{3,2},{4,5},{5,4},{6,7},{7,6},{8,9},{9,8},{10,11... | collective-permute-start | bytes 442376 | tf_op jit(solution)/shard_map/ppermute | solution.py:540
  99.9 0.1 pad_maximum_fusion.4
  100.1 0.8 copy.47.local_m_ref
  100.8 0.8 copy.46.local_p_ref
  101.6 0.9 pad_maximum_fusion.2.local_pt_ref
  102.5 0.0 collective-permute-done.theirs_ref
  102.5 0.6 copy-done.1
  103.1 20.2 %shard_map.195 = (f32[32,1,1152]{2,1,0:T(1,128)}, f32[32,1,1152]{2,1,0:T(1,128)}) custom-call(s32[16,2]{1,0:T(8,128)} %add_select_fusion.2.shift_ref, f32[16]{0:T(128)} %get-tuple-element.46.share_ref, s32[1]{0:T(128)} %copy.49.radius_ref, s32[1]{0:T(128)} %bitcast.1.core_ref, f32[32,1,1152]{2,1,0:T(1,128)} %copy-done, f32[32,1,1152]{2,1,0:T(1,128)} %copy-done.1, ...), custom_call_target="tpu_custom_call" | custom-call | tf_op jit(solution)/shard_map/pallas_call | solution.py:560
  123.3 0.5 collective-permute-start.1
  123.8 1.2 collective-permute-done.1
  125.0 1.1 add.47
  126.1 36.1 %all_to_all.20.in_ref = f32[32,1,1152]{2,1,0:T(1,128)} all-to-all(f32[32,1,1152]{2,1,0:T(1,128)S(1)} %add.47), channel_id=1, replica_groups=mesh['clip'=4,'slab_0'=32,'slab_1'=2] {'slab_0'}, dimensions={0} | all-to-all | bytes 294912 | tf_op jit(solution)/shard_map/all_to_all | solution.py:534
  162.2 2.4 %shard_map.196 = (f32[64,1,128]{2,1,0:T(1,128)}, f32[1,128]{1,0:T(1,128)}) custom-call(f32[32,1,1152]{2,1,0:T(1,128)} %all_to_all.20.in_ref, bf16[64,128]{1,0:T(8,128)(2,1)} %constant.134.clone.dft_high_ref.high_ref, bf16[64,128]{1,0:T(8,128)(2,1)} %constant.135.clone.dft_low_ref.low_ref, f32[72,128]{1,0:T(8,128)} %constant.136.clone.cos_ref, ...), custom_call_target="tpu_custom_call" | custom-call | tf_op jit(solution)/shard_map/pallas_call | solution.py:585
  164.5 6.4 %all-to-all-start.3 = ((f32[64,1,128]{2,1,0:T(1,128)}), f32[64,1,128]{2,1,0:T(1,128)S(1)}, u32[]{:S(2)}, u32[]{:S(2)}) async-start(f32[64,1,128]{2,1,0:T(1,128)} %get-tuple-element.40), calls=%async_computation.3 | async-start | bytes 65536 | tf_op jit(solution)/shard_map/all_to_all | solution.py:534
  171.0 0.6 slice.36
  171.6 0.6 fusion.16
  172.2 0.6 convert_select_fusion
  172.9 0.7 scatter.9.group_ref
  173.5 0.9 scatter.6.share_ref
  174.4 19.1 %all-to-all-done.3.in_ref = f32[64,1,128]{2,1,0:T(1,128)S(1)} async-done(((f32[64,1,128]{2,1,0:T(1,128)}), f32[64,1,128]{2,1,0:T(1,128)S(1)}, u32[]{:S(2)}, u32[]{:S(2)}) %all-to-all-start.3) | async-done | bytes 32800 | tf_op jit(solution)/shard_map/all_to_all | solution.py:534
  193.5 0.6 copy-done.3
  194.1 2.3 %shard_map.197 = (f32[32,2048]{1,0:T(8,128)}, f32[1,1]{1,0:T(1,128)}, f32[1,8]{1,0:T(1,128)}) custom-call(f32[64,1,128]{2,1,0:T(1,128)} %copy-done.3, f32[1,128]{1,0:T(1,128)} %get-tuple-element.41.sums_ref, f32[1,128]{1,0:T(1,128)} %copy-done.6, f32[8,128]{1,0:T(8,128)} %scatter.9.group_ref, bf16[256,512]{1,0:T(8,128)(2,1)} %constant.132.clone.high_ref, ...), custom_call_target="tpu_custom_call" | custom-call | tf_op jit(solution)/shard_map/pallas_call | solution.py:589
  (16 shorter events, 0.1 us)
Async XLA Ops:
  3.0 56.2 %all-to-all-start = ((f32[64,1,128]{2,1,0:T(1,128)}), f32[64,1,128]{2,1,0:T(1,128)S(1)}, u32[]{:S(2)}, u32[]{:S(2)}) async-start(f32[64,1,128]{2,1,0:T(1,128)} %get-tuple-element.36), calls=%async_computation | async-start | bytes 65536 | tf_op jit(solution)/shard_map/all_to_all | solution.py:534
  38.3 0.7 copy-start.4
  59.2 0.6 copy-start.2
  61.9 4.9 %copy-start.5 = (s32[16]{0:T(128)S(1)}, s32[16]{0:T(128)}, u32[]{:S(2)}) copy-start(s32[16]{0:T(128)} %param.25) | copy-start | bytes 196
  61.9 4.9 %copy-start.7 = (f32[8]{0:T(128)S(1)}, f32[8]{0:T(128)}, u32[]{:S(2)}) copy-start(f32[8]{0:T(128)} %param.26) | copy-start | bytes 100
  61.9 34.8 %all-to-all-start.1 = ((f32[32,1,1152]{2,1,0:T(1,128)}), f32[32,1,1152]{2,1,0:T(1,128)S(1)}, u32[]{:S(2)}, u32[]{:S(2)}) async-start(f32[32,1,1152]{2,1,0:T(1,128)} %shard_map.194), calls=%async_computation.1 | async-start | bytes 294912 | tf_op jit(solution)/shard_map/all_to_all | solution.py:534
  96.7 3.4 %copy-start = (f32[32,1,1152]{2,1,0:T(1,128)}, f32[32,1,1152]{2,1,0:T(1,128)S(1)}, u32[]{:S(2)}) copy-start(f32[32,1,1152]{2,1,0:T(1,128)S(1)} %all-to-all-done.1.mine_ref) | copy-start | bytes 442372
  96.7 5.8 %collective-permute-start = (f32[32,1,1152]{2,1,0:T(1,128)S(1)}, f32[32,1,1152]{2,1,0:T(1,128)S(1)}, u32[]{:S(2)}, u32[]{:S(2)}) collective-permute-start(f32[32,1,1152]{2,1,0:T(1,128)S(1)} %all-to-all-done.1.mine_ref), channel_id=1, source_target_pairs={{0,1},{1,0},{2,3},{3,2},{4,5},{5,4},{6,7},{7,6},{8,9},{9,8},{10,11... | collective-permute-start | bytes 442376 | tf_op jit(solution)/shard_map/ppermute | solution.py:540
  102.5 0.6 copy-start.1
  123.3 1.8 collective-permute-start.1
  164.5 29.0 %all-to-all-start.3 = ((f32[64,1,128]{2,1,0:T(1,128)}), f32[64,1,128]{2,1,0:T(1,128)S(1)}, u32[]{:S(2)}, u32[]{:S(2)}) async-start(f32[64,1,128]{2,1,0:T(1,128)} %get-tuple-element.40), calls=%async_computation.3 | async-start | bytes 65536 | tf_op jit(solution)/shard_map/all_to_all | solution.py:534
  174.4 19.1 %copy-start.6 = (f32[1,128]{1,0:T(1,128)}, f32[1,128]{1,0:T(1,128)S(1)}, u32[]{:S(2)}) copy-start(f32[1,128]{1,0:T(1,128)S(1)} %scatter.6.share_ref) | copy-start | bytes 1540
  193.5 0.6 copy-start.3

commit v3 on v2

--- a/solution.py
+++ b/solution.py
@@ -108,7 +108,35 @@
     out_ref[...] = parcels.reshape(out_ref.shape)
 
 
-def columns_kernel(in_ref, own_sums_ref, dft_high_ref, dft_low_ref, cos_ref, sin_ref, piece_ref):
+def local_kernel(
+    cos_ref, sin_ref, kernel_ref, plus_ref, minus_ref, plus_t_ref, minus_t_ref, spread_high_ref, spread_low_ref, ready_ref
+):
+    cos = cos_ref[...]
+    edge = lane_index(cos.shape) == 0
+    for out_ref, out_t_ref, sin in (
+        (plus_ref, plus_t_ref, sin_ref[...]),
+        (minus_ref, minus_t_ref, jnp.where(edge, -sin_ref[...], sin_ref[...])),
+    ):
+        table = jnp.concatenate([jnp.concatenate([cos, -sin], 1), jnp.concatenate([sin, cos], 1)], 0)
+        high, low = pieces(table)
+        out_ref[...] = jnp.concatenate([high, low], 0)
+        high, low = pieces(table.T)
+        out_t_ref[...] = jnp.concatenate([high, high, low], 1)
+    ready_ref[...] = cos[:8, :128]
+    length = kernel_ref.shape[1]
+    near, fine = COARSE // 4, length // 4
+    at = pltpu.roll(
+        jnp.broadcast_to(kernel_ref[...], (near, length)), 0, 1, stride=length // COARSE, stride_axis=0
+    )
+    h0, h1, h2, h3 = (at[:, p * fine : (p + 1) * fine] for p in range(4))
+    even, odd = h0 + h2, h1 + h3
+    for i, table in enumerate(((even + odd) / 4, (even - odd) / 4, (h0 - h2) / 2, (h1 - h3) / 2)):
+        high, low = pieces(table)
+        spread_high_ref[i * near : (i + 1) * near] = high
+        spread_low_ref[i * near : (i + 1) * near] = low
+
+
+def columns_kernel(in_ref, own_sums_ref, dft_high_ref, dft_low_ref, cos_ref, sin_ref, ready_ref, piece_ref):
     owners, _, lanes = in_ref.shape
     rows = lanes // 4
     a = in_ref[...].reshape(owners, lanes)
@@ -242,7 +270,7 @@
             lift_ref[at_rows, e * 2 * HALF + HALF : (e + 1) * 2 * HALF] = low
         return carry
 
-    lax.fori_loop(0, sources, lift, 0)
+    lax.fori_loop(0, sources, lift, 0, unroll=16)
     field_tables = [
         (field_high_ref[e * HALF : (e + 1) * HALF], field_low_ref[e * HALF : (e + 1) * HALF]) for e in range(4)
     ]
@@ -266,7 +294,7 @@
             out.append(total[q] + share_ref[s] * (real[q] * real[q] + imag[q] * imag[q]))
         return tuple(out)
 
-    coarse = lax.fori_loop(0, sources, expose, (jnp.zeros((rows, HALF), f32),) * 4)
+    coarse = lax.fori_loop(0, sources, expose, (jnp.zeros((rows, HALF), f32),) * 4, unroll=2)
     spread = spread_high_ref[...], spread_low_ref[...]
     quarter = COARSE // 4
     spread = [tuple(t[at : at + n] for t in spread) for at, n in ((0, quarter), (quarter, quarter), (2 * quarter, 2 * quarter))]
@@ -329,7 +357,7 @@
             back_low_ref[at_rows, i * HALF : (i + 1) * HALF] = low
         return carry
 
-    lax.fori_loop(0, sources, push, 0)
+    lax.fori_loop(0, sources, push, 0, unroll=2)
     for e, (high, low) in enumerate(field_tables):
         lanes = slice(e * 2 * HALF, (e + 1) * 2 * HALF)
         both = mm(back_high_ref[:, lanes], jnp.concatenate([high, low], 0), NT)
@@ -351,7 +379,7 @@
             pull_ref[...] += out * jnp.concatenate([passed, passed], 0)
         return carry
 
-    lax.fori_loop(0, sources, pull, 0)
+    lax.fori_loop(0, sources, pull, 0, unroll=16)
     plus = pull_p_ref[...]
     minus = pull_m_ref[...]
     y_real = jnp.zeros((owners, rows), f32)
@@ -476,13 +504,11 @@
     share = np.where(tones == COARSE // 2, 1.0, 2.0)
     pixels = np.arange(length)
     kernel = (1.0 + np.cos(2.0 * np.pi * (np.outer(pixels, tones) % length) / length) @ share) / COARSE
-    near, fine = samples[: COARSE // 4, None], pixels[None, : length // 4]
-    h0, h1, h2, h3 = (kernel[(fine + p * (length // 4) - near) % length] for p in range(4))
-    spread = np.concatenate([(h0 + h1 + h2 + h3) / 4, (h0 - h1 + h2 - h3) / 4, (h0 - h2) / 2, (h1 - h3) / 2], 0)
-    return host_pieces(row_table), host_pieces(dft), host_pieces(turn), turning, host_pieces(field), host_pieces(spread)
-
-
-def call(kernel, out_shape, scratch=(), n_scalar=0, n_in=0, interpret=False, flops=0):
+    spread = kernel.reshape(1, length).astype(np.float32)
+    return host_pieces(row_table), host_pieces(dft), host_pieces(turn), turning, host_pieces(field), spread
+
+
+def call(kernel, out_shape, scratch=(), n_scalar=0, n_in=0, mib=12, interpret=False):
     vmem = pl.BlockSpec(memory_space=pltpu.VMEM)
     smem = pl.BlockSpec(memory_space=pltpu.SMEM)
     multi = isinstance(out_shape, (tuple, list))
@@ -492,7 +518,7 @@
         in_specs=[smem] * n_scalar + [vmem] * n_in,
         out_specs=[vmem] * len(out_shape) if multi else vmem,
         scratch_shapes=list(scratch),
-        compiler_params=pltpu.CompilerParams(vmem_limit_bytes=56 * 1024 * 1024),
+        compiler_params=pltpu.CompilerParams(vmem_limit_bytes=mib * 1024 * 1024),
         interpret=interpret,
     )
 
@@ -535,7 +561,16 @@
 
     parcels, own_sums = run(rows_kernel, (shape((owners, 1, 4 * rows)), shape((1, 128))), n_in=3)(mask_field, *row_table)
     arrived = swap_all(parcels, SLAB)
-    piece = run(columns_kernel, shape((ring, 1, PARCEL)), n_in=6)(arrived, own_sums, *dft, *turning)
+    across = jnp.arange(K, dtype=jnp.int32) - HALF
+    here = device * rows + jnp.arange(rows, dtype=jnp.int32)
+    angle = jnp.mod(here[:, None] * across[None, :], length).astype(f32) * (2.0 * np.pi / length)
+    sizes = ((4 * rows, 2 * K),) * 2 + ((2 * K, 6 * rows),) * 2 + ((COARSE, length // 4),) * 2
+    local_p, local_m, local_pt, local_mt, *spread, ready = run(
+        local_kernel,
+        tuple(jax.ShapeDtypeStruct(t, bf16) for t in sizes) + (shape((8, 128)),),
+        n_in=3,
+    )(jnp.cos(angle), jnp.sin(angle), spread)
+    piece = run(columns_kernel, shape((ring, 1, PARCEL)), n_in=7)(arrived, own_sums, *dft, *turning, ready)
     around = swap_all(piece, RING)
     theirs = lax.ppermute(around, CORE, [(i, (i + 1) % pair) for i in range(pair)])
 
@@ -543,25 +578,12 @@
     weights = jnp.exp(jnp.sum(onehot * group_logits[None, :], 1))
     total_weight = jnp.sum(weights)
     weight_share = weights / total_weight
-    across = jnp.arange(K, dtype=jnp.int32) - HALF
-    across_m = jnp.where(across == -HALF, HALF, across)
-    here = device * rows + jnp.arange(rows, dtype=jnp.int32)
-
-    def local(freq):
-        angle = jnp.mod(here[:, None] * freq[None, :], length).astype(f32) * (2.0 * np.pi / length)
-        c, s = jnp.cos(angle), jnp.sin(angle)
-        table = jnp.concatenate([jnp.concatenate([c, -s], 1), jnp.concatenate([s, c], 1)], 0)
-        rounded = lax.reduce_precision(table, 8, 7)
-        high, low = rounded.astype(bf16), (table - rounded).astype(bf16)
-        return jnp.concatenate([high, low], 0), jnp.concatenate([high.T, high.T, low.T], 1)
-
-    local_p, local_pt = local(across)
-    local_m, local_mt = local(across_m)
     mine, theirs = run(
         image_kernel,
         (shape((ring, 1, PARCEL)),) * 2,
         n_scalar=4,
         n_in=15,
+        mib=28,
         scratch=image_scratch(sources, rows),
     )(
         shifted,

time: 197 us -> 181 us (0.919)
  Pallas kernels: 29.3 us -> 16 us
  other arithmetic: 8.71 us -> 4.32 us
  waiting for transfers between devices: 65.2 us -> 69.5 us
    pallas_call x2 -> x3, Pallas kernels: 22.3 us -> 12.1 us  [the longest x1 10.4 us: on_device(): run(image_kernel, (shape((ring, 1, PARCEL)),) * 2, n_scalar=4, n_in=15, m...]
    all_to_all x3, waiting for transfers between devices: 64 us -> 68.1 us  [swap_all(): lax.all_to_all(parcels, axes, split_axis=0, concat_axis=0, tiled=True)]
    concatenate x6 -> x0, local copies, waits for them, and re-layouts: 2.04 us -> none  [the longest x2 1.53 us: local(): jnp.concatenate([high, low], 0)]
  transfers between devices with their start and end apart: 5 -> 5, of which waited for: 4 -> 4; matrix products, arithmetic and copies ran while one was open for 6% -> 3% of each run, Pallas kernels for 0% -> 0%
where the time goes in v3:
time: 181 us
  waiting for transfers between devices  69.5 us (38%)
  starting transfers between devices  48.8 us (27%)
  blocking collectives  35.7 us (20%)
  Pallas kernels  16 us (9%)
  local copies, waits for them, and re-layouts  5.03 us (3%)
  other arithmetic  4.32 us (2%)
    all_to_all x3, waiting for transfers between devices, swap_all(): lax.all_to_all(parcels, axes, split_axis=0, concat_axis=0, tiled=True)  68.1 us
    all_to_all x3, starting transfers between devices, swap_all(): lax.all_to_all(parcels, axes, split_axis=0, concat_axis=0, tiled=True)  45.4 us
    all_to_all x1, blocking collectives, swap_all(): lax.all_to_all(parcels, axes, split_axis=0, concat_axis=0, tiled=True)  35.7 us
    pallas_call x1, Pallas kernels, on_device(): run(image_kernel, (shape((ring, 1, PARCEL)),) * 2, n_scalar=4, n_in=15, m...  10.4 us
  transfers between devices with their start and end apart: 5, of which 4 were waited for; matrix products, arithmetic and copies ran while one was open for 3% of the time, Pallas kernels for 0%

profile of v3, /device:TPU:37, one launch (start us, length us, event | category | flops | bytes accessed | tf_op | source)
XLA Modules:
  0.0 180.9 jit_solution(337067072563447305)
XLA Ops:
  0.6 0.0 copy-start
  0.6 0.9 copy-done
  1.6 0.9 copy-done.2
  2.5 0.9 copy-done.6
  3.5 1.3 shard_map.184
  4.8 34.3 %all-to-all-start = ((f32[64,1,128]{2,1,0:T(1,128)}), f32[64,1,128]{2,1,0:T(1,128)S(1)}, u32[]{:S(2)}, u32[]{:S(2)}) async-start(f32[64,1,128]{2,1,0:T(1,128)} %get-tuple-element.43), calls=%async_computation | async-start | bytes 65536 | tf_op jit(solution)/shard_map/all_to_all | solution.py:560
  39.1 0.0 copy-start.14
  39.1 0.0 copy-start.10
  39.1 0.0 copy-start.11
  39.2 0.2 fusion.3
  39.4 0.4 copy-done.14
  39.8 0.4 shard_map.185
  40.2 20.8 %all-to-all-done.in_ref = f32[64,1,128]{2,1,0:T(1,128)S(1)} async-done(((f32[64,1,128]{2,1,0:T(1,128)}), f32[64,1,128]{2,1,0:T(1,128)S(1)}, u32[]{:S(2)}, u32[]{:S(2)}) %all-to-all-start) | async-done | bytes 32800 | tf_op jit(solution)/shard_map/all_to_all | solution.py:560
  61.0 0.0 copy-done.10
  61.1 0.0 copy-done.4
  61.1 0.0 copy-done.5
  61.1 0.0 copy-start.7
  61.1 0.0 copy-start.8
  61.1 1.3 shard_map.186
  62.3 4.8 %all-to-all-start.1 = ((f32[32,1,1152]{2,1,0:T(1,128)}), f32[32,1,1152]{2,1,0:T(1,128)S(1)}, u32[]{:S(2)}, u32[]{:S(2)}) async-start(f32[32,1,1152]{2,1,0:T(1,128)} %shard_map.186), calls=%async_computation.1 | async-start | bytes 294912 | tf_op jit(solution)/shard_map/all_to_all | solution.py:560
  67.1 0.0 copy-start.15
  67.8 0.0 copy-done.15
  67.8 0.1 copy.24
  67.9 0.6 and_reduce_fusion
  68.6 0.0 copy-done.16
  68.6 0.0 copy-done.17
  68.6 0.1 select_reduce_fusion
  68.7 0.6 exponential_reduce_fusion
  69.3 27.7 %all-to-all-done.1.mine_ref = f32[32,1,1152]{2,1,0:T(1,128)S(1)} async-done(((f32[32,1,1152]{2,1,0:T(1,128)}), f32[32,1,1152]{2,1,0:T(1,128)S(1)}, u32[]{:S(2)}, u32[]{:S(2)}) %all-to-all-start.1) | async-done | bytes 147488 | tf_op jit(solution)/shard_map/all_to_all | solution.py:560
  97.0 3.3 %collective-permute-start = (f32[32,1,1152]{2,1,0:T(1,128)S(1)}, f32[32,1,1152]{2,1,0:T(1,128)S(1)}, u32[]{:S(2)}, u32[]{:S(2)}) collective-permute-start(f32[32,1,1152]{2,1,0:T(1,128)S(1)} %all-to-all-done.1.mine_ref), channel_id=1, source_target_pairs={{0,1},{1,0},{2,3},{3,2},{4,5},{5,4},{6,7},{7,6},{8,9},{9,8},{10,11... | collective-permute-start | bytes 442376 | tf_op jit(solution)/shard_map/ppermute | solution.py:575
  100.3 1.3 fusion.6
  101.6 0.0 collective-permute-done.theirs_ref
  101.6 10.4 %shard_map.187 = (f32[32,1,1152]{2,1,0:T(1,128)S(1)}, f32[32,1,1152]{2,1,0:T(1,128)S(1)}) custom-call(s32[16,2]{1,0:T(8,128)S(1)} %add_select_fusion.1.shift_ref, f32[16]{0:T(128)S(1)} %get-tuple-element.60.share_ref, s32[1]{0:T(128)} %copy.26.radius_ref, s32[1]{0:T(128)} %bitcast.1.core_ref, f32[32,1,1152]{2,1,0:T(1,128)S(1)} %all-to-all-done.1.mine_ref, ...), custom_call_target="tpu_custom_call" | custom-call | tf_op jit(solution)/shard_map/pallas_call | solution.py:581
  112.0 0.2 collective-permute-start.1
  112.2 1.3 collective-permute-done.1
  113.5 0.2 add.39
  113.7 0.0 copy-start.1
  113.7 0.0 copy-start.3
  113.7 35.7 %all_to_all.20.in_ref = f32[32,1,1152]{2,1,0:T(1,128)S(1)} all-to-all(f32[32,1,1152]{2,1,0:T(1,128)S(1)} %add.39), channel_id=1, replica_groups=mesh['clip'=4,'slab_0'=32,'slab_1'=2] {'slab_0'}, dimensions={0} | all-to-all | bytes 294912 | tf_op jit(solution)/shard_map/all_to_all | solution.py:560
  149.4 1.4 shard_map.188
  150.8 6.3 %all-to-all-start.3 = ((f32[64,1,128]{2,1,0:T(1,128)}), f32[64,1,128]{2,1,0:T(1,128)S(1)}, u32[]{:S(2)}, u32[]{:S(2)}) async-start(f32[64,1,128]{2,1,0:T(1,128)} %get-tuple-element.54), calls=%async_computation.3 | async-start | bytes 65536 | tf_op jit(solution)/shard_map/all_to_all | solution.py:560
  157.1 0.6 slice.36
  157.7 0.6 fusion.7
  158.3 0.6 convert_select_fusion
  159.0 0.1 scatter.9.group_ref
  159.1 0.9 scatter.6.share_ref
  160.0 19.6 %all-to-all-done.3.in_ref = f32[64,1,128]{2,1,0:T(1,128)S(1)} async-done(((f32[64,1,128]{2,1,0:T(1,128)}), f32[64,1,128]{2,1,0:T(1,128)S(1)}, u32[]{:S(2)}, u32[]{:S(2)}) %all-to-all-start.3) | async-done | bytes 32800 | tf_op jit(solution)/shard_map/all_to_all | solution.py:560
  179.6 1.2 shard_map.189
  (23 shorter events, 0.1 us)
Async XLA Ops:
  0.6 1.0 copy-start
  1.6 0.9 copy-start.2
  2.5 0.9 copy-start.6
  3.5 98.1 %copy-start.9 = (bf16[512,256]{1,0:T(8,128)(2,1)S(1)}, bf16[512,256]{1,0:T(8,128)(2,1)}, u32[]{:S(2)}) copy-start(bf16[512,256]{1,0:T(8,128)(2,1)} %constant.132.clone.field_low_ref) | copy-start | bytes 786436
  4.8 56.3 %all-to-all-start = ((f32[64,1,128]{2,1,0:T(1,128)}), f32[64,1,128]{2,1,0:T(1,128)S(1)}, u32[]{:S(2)}, u32[]{:S(2)}) async-start(f32[64,1,128]{2,1,0:T(1,128)} %get-tuple-element.43), calls=%async_computation | async-start | bytes 65536 | tf_op jit(solution)/shard_map/all_to_all | solution.py:560
  39.1 0.7 copy-start.14
  39.1 21.9 %copy-start.10 = (bf16[64,128]{1,0:T(8,128)(2,1)S(1)}, bf16[64,128]{1,0:T(8,128)(2,1)}, u32[]{:S(2)}) copy-start(bf16[64,128]{1,0:T(8,128)(2,1)} %constant.125.clone.dft_high_ref.high_ref) | copy-start | bytes 49156
  39.1 21.9 %copy-start.11 = (bf16[64,128]{1,0:T(8,128)(2,1)S(1)}, bf16[64,128]{1,0:T(8,128)(2,1)}, u32[]{:S(2)}) copy-start(bf16[64,128]{1,0:T(8,128)(2,1)} %constant.126.clone.dft_low_ref.low_ref) | copy-start | bytes 49156
  39.8 21.2 %copy-start.4 = (f32[72,128]{1,0:T(8,128)S(1)}, f32[72,128]{1,0:T(8,128)}, u32[]{:S(2)}) copy-start(f32[72,128]{1,0:T(8,128)} %constant.127.clone.cos_ref) | copy-start | bytes 110596
  39.8 21.2 %copy-start.5 = (f32[72,128]{1,0:T(8,128)S(1)}, f32[72,128]{1,0:T(8,128)}, u32[]{:S(2)}) copy-start(f32[72,128]{1,0:T(8,128)} %constant.128.clone.sin_ref) | copy-start | bytes 110596
  61.1 40.5 %copy-start.7 = (s32[32,2048]{1,0:T(8,128)S(1)}, s32[32,2048]{1,0:T(8,128)}, u32[]{:S(2)}) copy-start(s32[32,2048]{1,0:T(8,128)} %target_ref.1) | copy-start | bytes 786436
  61.1 40.5 %copy-start.8 = (bf16[512,256]{1,0:T(8,128)(2,1)S(1)}, bf16[512,256]{1,0:T(8,128)(2,1)}, u32[]{:S(2)}) copy-start(bf16[512,256]{1,0:T(8,128)(2,1)} %constant.131.clone.field_high_ref) | copy-start | bytes 786436
  62.3 34.7 %all-to-all-start.1 = ((f32[32,1,1152]{2,1,0:T(1,128)}), f32[32,1,1152]{2,1,0:T(1,128)S(1)}, u32[]{:S(2)}, u32[]{:S(2)}) async-start(f32[32,1,1152]{2,1,0:T(1,128)} %shard_map.186), calls=%async_computation.1 | async-start | bytes 294912 | tf_op jit(solution)/shard_map/all_to_all | solution.py:560
  67.1 0.7 copy-start.15
  67.9 0.7 copy-start.16
  67.9 0.7 copy-start.17
  69.3 32.3 %copy-start.12 = (bf16[64,128]{1,0:T(8,128)(2,1)S(1)}, bf16[64,128]{1,0:T(8,128)(2,1)}, u32[]{:S(2)}) copy-start(bf16[64,128]{1,0:T(8,128)(2,1)} %constant.129.clone.turn_high_ref) | copy-start | bytes 49156
  69.3 32.3 %copy-start.13 = (bf16[64,128]{1,0:T(8,128)(2,1)S(1)}, bf16[64,128]{1,0:T(8,128)(2,1)}, u32[]{:S(2)}) copy-start(bf16[64,128]{1,0:T(8,128)(2,1)} %constant.130.clone.turn_low_ref) | copy-start | bytes 49156
  97.0 4.6 %collective-permute-start = (f32[32,1,1152]{2,1,0:T(1,128)S(1)}, f32[32,1,1152]{2,1,0:T(1,128)S(1)}, u32[]{:S(2)}, u32[]{:S(2)}) collective-permute-start(f32[32,1,1152]{2,1,0:T(1,128)S(1)} %all-to-all-done.1.mine_ref), channel_id=1, source_target_pairs={{0,1},{1,0},{2,3},{3,2},{4,5},{5,4},{6,7},{7,6},{8,9},{9,8},{10,11... | collective-permute-start | bytes 442376 | tf_op jit(solution)/shard_map/ppermute | solution.py:575
  112.0 1.5 collective-permute-start.1
  113.7 65.9 %copy-start.1 = (bf16[256,512]{1,0:T(8,128)(2,1)S(1)}, bf16[256,512]{1,0:T(8,128)(2,1)}, u32[]{:S(2)}) copy-start(bf16[256,512]{1,0:T(8,128)(2,1)} %constant.122.clone.high_ref) | copy-start | bytes 786436
  113.7 65.9 %copy-start.3 = (bf16[256,512]{1,0:T(8,128)(2,1)S(1)}, bf16[256,512]{1,0:T(8,128)(2,1)}, u32[]{:S(2)}) copy-start(bf16[256,512]{1,0:T(8,128)(2,1)} %constant.123.clone.low_ref) | copy-start | bytes 786436
  150.8 28.8 %all-to-all-start.3 = ((f32[64,1,128]{2,1,0:T(1,128)}), f32[64,1,128]{2,1,0:T(1,128)S(1)}, u32[]{:S(2)}, u32[]{:S(2)}) async-start(f32[64,1,128]{2,1,0:T(1,128)} %get-tuple-element.54), calls=%async_computation.3 | async-start | bytes 65536 | tf_op jit(solution)/shard_map/all_to_all | solution.py:560

commit v4 on v3

--- a/solution.py
+++ b/solution.py
@@ -14,11 +14,13 @@
 GRID = 61
 NG = 8
 COARSE = 2 * K
-PARCEL = 9 * 128
-RING = "slab_0"
-CORE = "slab_1"
-SLAB = (RING, CORE)
-CLIP_SLAB = ("clip", RING, CORE)
+FAR = 4
+SPECTRA = K * K // 16
+FAR_AXIS = "slab_0"
+NEAR = "slab_1"
+CORE = "slab_2"
+SLAB = (FAR_AXIS, NEAR, CORE)
+CLIP_SLAB = ("clip", *SLAB)
 
 steepness = 8.0
 threshold = 0.3
@@ -80,7 +82,7 @@
     return cos * cos_m - sin * sin_m, sin * cos_m + cos * sin_m
 
 
-def rows_kernel(mask_ref, high_ref, low_ref, out_ref, sums_ref):
+def rows_kernel(mask_ref, high_ref, low_ref, out_ref):
     rows, length = mask_ref.shape
     quarter = length // 4
     m0, m1, m2, m3 = (mask_ref[:, q * quarter : (q + 1) * quarter] for q in range(4))
@@ -91,21 +93,21 @@
     cos, sin = both[:HALF], both[HALF:]
     c0, c2, ca, cb = (cos[:, i * rows : (i + 1) * rows] for i in range(4))
     s0, s2, sa, sb = (sin[:, i * rows : (i + 1) * rows] for i in range(4))
-    owners = HALF // 2
-    odd_row = row_index((owners, rows)) % 2 == 1
-    lo, hi = slice(0, owners), slice(owners, HALF)
     ones = jnp.ones((8, quarter), bf16)
-    sums_ref[...] = (mm(ones, stack[0], NT) + mm(ones, stack[1], NT))[:1]
-    parcels = jnp.concatenate(
-        [
-            jnp.where(odd_row, c2[lo], ca[lo] - sb[lo]),
-            jnp.where(odd_row, -s2[lo], -sa[lo] - cb[lo]),
-            jnp.where(odd_row, c0[hi], ca[hi] + sb[hi]),
-            jnp.where(odd_row, -s0[hi], cb[hi] - sa[hi]),
-        ],
-        1,
-    )
-    out_ref[...] = parcels.reshape(out_ref.shape)
+    sums = (mm(ones, stack[0], NT) + mm(ones, stack[1], NT))[:1, :rows]
+    group = HALF // 4
+    g0, g1, g2, g3 = (slice(g * group, (g + 1) * group) for g in range(4))
+    real = [ca[g0] - sb[g0], c2[g1], ca[g2] + sb[g2], c0[g3]]
+    imag = [-sa[g0] - cb[g0], -s2[g1], cb[g2] - sa[g2], -s0[g3]]
+    owners = out_ref.shape[0] // FAR
+    slots = group // owners
+    blocks = []
+    for re, im in zip(real, imag):
+        for t in range(slots):
+            blocks += [re[t * owners : (t + 1) * owners], im[t * owners : (t + 1) * owners]]
+    blocks += [jnp.broadcast_to(sums, (owners, rows)), jnp.zeros((owners, 3 * rows), f32)]
+    parcels = jnp.concatenate(blocks, 1)
+    out_ref[...] = jnp.concatenate([parcels] * FAR, 0).reshape(out_ref.shape)
 
 
 def local_kernel(
@@ -136,26 +138,28 @@
         spread_low_ref[i * near : (i + 1) * near] = low
 
 
-def columns_kernel(in_ref, own_sums_ref, dft_high_ref, dft_low_ref, cos_ref, sin_ref, ready_ref, piece_ref):
-    owners, _, lanes = in_ref.shape
-    rows = lanes // 4
-    a = in_ref[...].reshape(owners, lanes)
+def columns_kernel(in_ref, dft_high_ref, dft_low_ref, cos_ref, sin_ref, ready_ref, piece_ref):
+    devices, _, lanes = in_ref.shape
+    rows = cos_ref.shape[1] // 4
+    lanes -= 4 * rows
+    a = in_ref[...].reshape(devices, lanes + 4 * rows)[:, :lanes]
     z = mm3((dft_high_ref[...], dft_low_ref[...]), pieces(jnp.concatenate([a, swapped(a, rows)], 0)))
     turned = swapped(z, rows)
     blocks = []
     for m in range(5):
-        cos, sin = twiddle(cos_ref, sin_ref, m)
+        cos, sin = (jnp.concatenate([t] * (lanes // (4 * rows)), 1) for t in twiddle(cos_ref, sin_ref, m))
         blocks.append(z * cos + turned * sin)
     high, low = pieces(jnp.concatenate(blocks, 0))
-    pick = (row_index((8, lanes)) == lane_index((8, lanes)) // rows).astype(f32).astype(bf16)
+    count = lanes // rows
+    pick = (row_index((count, lanes)) == lane_index((count, lanes)) // rows).astype(f32).astype(bf16)
     sums = mm(pick, high, NT) + mm(pick, low, NT)
     copies = piece_ref.shape[0]
     lane = lane_index((1, 128))
-    tail = jnp.where(lane // rows == 1, pltpu.roll(own_sums_ref[...], rows, 1), 0.0)
-    for q in range(4):
+    tail = jnp.zeros((1, 128), f32)
+    for q in range(count):
         tail = jnp.where(lane == q, sums[q : q + 1, K : K + 1], tail)
-    row = jnp.concatenate([sums[q : q + 1, :K] for q in range(4)] + [tail], 1)
-    piece_ref[...] = jnp.broadcast_to(row.reshape(1, 1, PARCEL), (copies, 1, PARCEL))
+    row = jnp.concatenate([sums[q : q + 1, :K] for q in range(count)] + [tail], 1)
+    piece_ref[...] = jnp.broadcast_to(row.reshape(1, 1, row.shape[1]), (copies, 1, row.shape[1]))
 
 
 def image_kernel(
@@ -165,6 +169,9 @@
     core_ref,
     mine_ref,
     theirs_ref,
+    arrived_ref,
+    dft_high_ref,
+    dft_low_ref,
     turn_high_ref,
     turn_low_ref,
     cos_ref,
@@ -197,24 +204,30 @@
     norming = 1.0 / (target_ref.shape[1] * target_ref.shape[1])
     radius_sq = radius_ref[0] * radius_ref[0]
     first_core = core_ref[0] == 0
-    ring = mine_ref.shape[0]
-    mine = mine_ref[...].reshape(ring, PARCEL)
-    theirs = theirs_ref[...].reshape(ring, PARCEL)
+    near = mine_ref.shape[0]
+    mine = mine_ref[...].reshape(near, SPECTRA + 128)
+    theirs = theirs_ref[...].reshape(near, SPECTRA + 128)
     wide = jnp.concatenate([jnp.where(first_core, mine, theirs), jnp.where(first_core, theirs, mine)], 0)
-    body = jnp.concatenate([wide[:, : 2 * K], wide[:, 2 * K : 4 * K]], 0)
+    owners = 2 * near
+    slots = HALF // owners
+    body = jnp.concatenate([wide[:, t * 2 * K : (t + 1) * 2 * K] for t in range(slots)], 0)
     spectrum = body.T
-    tail = wide[:, 4 * K :].T
-    turn = turn_high_ref[...], turn_low_ref[...]
-    owners = 2 * ring
-    z = mm3(turn, pieces(wide[:, 4 * K + rows : 4 * K + 2 * rows]), TN)
-    z_real, z_imag = z[:owners], -z[owners:]
+    tail = [
+        jnp.concatenate([wide[:, SPECTRA + 2 * t + part : SPECTRA + 2 * t + part + 1] for t in range(slots)], 0)
+        for part in range(2)
+    ]
+    tail = jnp.concatenate(tail + [jnp.zeros((HALF, 6), f32)], 1).T
+    devices = arrived_ref.shape[0]
+    row_sums = arrived_ref[...].reshape(devices, arrived_ref.shape[2])[:, arrived_ref.shape[2] - 4 * rows :]
+    z = mm3((dft_high_ref[...], dft_low_ref[...]), pieces(row_sums[:, :rows]), TN)
+    z_real, z_imag = z[:devices], -z[devices:]
     turns_of = [tuple(t[:, :rows] for t in twiddle(cos_ref, sin_ref, m)) for m in range(4)]
     zero = [
         jnp.concatenate([jnp.sum(z_real * c + z_imag * n, 1, keepdims=True) for c, n in turns_of], 0),
         jnp.concatenate([jnp.sum(z_imag * c - z_real * n, 1, keepdims=True) for c, n in turns_of], 0),
     ]
     lane = lane_index((1, HALF))
-    frequency = 4 * (lane % ring) + lane // ring + 1
+    frequency = 4 * (lane % (HALF // 4)) + lane // (HALF // 4) + 1
     last = lane == HALF - 1
     frequency_p = jnp.where(last, 0, frequency)
     across = row_index((K, 1)) - HALF
@@ -224,8 +237,7 @@
     for part in range(2):
         block = spectrum[part * K : (part + 1) * K]
         plus = jnp.where(last_col, zero[part], block)
-        edge = jnp.concatenate([tail[part : part + 1], tail[2 + part : 3 + part]], 1)
-        minus = jnp.where(first_row, edge, block)
+        minus = jnp.where(first_row, tail[part : part + 1], block)
         for ref, value in ((plus_ref, plus), (minus_ref, minus)):
             high, low = pieces(value)
             ref[part * K : (part + 1) * K, :HALF] = high
@@ -332,7 +344,7 @@
         return total
 
     sums_ref[...] = jnp.zeros(sums_ref.shape, f32)
-    sums_ref[8:9, :] = lane_sum(squares)
+    sums_ref[80:81, :] = lane_sum(squares)
     for ref in (pull_p_ref, pull_m_ref):
         ref[...] = jnp.zeros(ref.shape, f32)
 
@@ -347,7 +359,7 @@
             factor = (2.0 * norming * share_ref[s]) * slope_c[q]
             real.append(factor * re)
             imag.append(factor * im)
-        sums_ref[pl.ds(16 + s, 1), :] = jnp.sum(bright, 0, keepdims=True)
+        sums_ref[pl.ds(64 + s, 1), :] = jnp.sum(bright, 0, keepdims=True)
         er, ei, fr, fi = real[0] + real[2], imag[0] + imag[2], real[1] + real[3], imag[1] + imag[3]
         ar, ai, br, bi = real[0] - real[2], imag[0] - imag[2], real[1] - real[3], imag[1] - imag[3]
         turned = [er + fr, ei + fi, ar + bi, ai - br, er - fr, ei - fi, ar - bi, ai + br]
@@ -382,81 +394,86 @@
     lax.fori_loop(0, sources, pull, 0, unroll=16)
     plus = pull_p_ref[...]
     minus = pull_m_ref[...]
-    y_real = jnp.zeros((owners, rows), f32)
-    y_imag = jnp.zeros((owners, rows), f32)
+    y_real = jnp.zeros((devices, rows), f32)
+    y_imag = jnp.zeros((devices, rows), f32)
     for m, (c, n) in enumerate(turns_of):
-        real = plus[m * owners : (m + 1) * owners, HALF - 1 :]
-        imag = plus[K + m * owners : K + (m + 1) * owners, HALF - 1 :]
+        real = plus[m * devices : (m + 1) * devices, HALF - 1 :]
+        imag = plus[K + m * devices : K + (m + 1) * devices, HALF - 1 :]
         y_real = y_real + (real * c - imag * n)
         y_imag = y_imag + (real * n + imag * c)
+    turn = turn_high_ref[...], turn_low_ref[...]
     level = mm3(turn, pieces(jnp.concatenate([y_real, -y_imag], 0)))
+    level = jnp.concatenate([level[f * owners : (f + 1) * owners] for f in range(FAR)], 1)
     sums = jnp.sum(sums_ref[...].T, 0, keepdims=True)
     lane = lane_index((owners, 128))
-    level = jnp.concatenate([level] * 4, 1)
-    tail = jnp.where(lane // rows == 1, level, sums)
+    tail = jnp.broadcast_to(sums, (owners, 128))
     edge = jnp.concatenate([minus[:1], minus[K : K + 1], jnp.zeros((6, HALF), f32)], 0).T
-    for j in range(2):
+    for t in range(slots):
         for part in range(2):
-            tail = jnp.where(lane == 2 * j + part, edge[j * owners : (j + 1) * owners, part : part + 1], tail)
+            tail = jnp.where(lane == 2 * t + part, edge[t * owners : (t + 1) * owners, part : part + 1], tail)
     total = jnp.where(lane_index(plus.shape) == HALF - 1, 0.0, plus)
     total = total + jnp.where(row_index(plus.shape) % K == 0, 0.0, minus)
     total = total.T
-    row = jnp.concatenate([total[:owners], total[owners:], tail], 1)
-    low, high = row[:ring], row[ring:]
+    row = jnp.concatenate([total[t * owners : (t + 1) * owners] for t in range(slots)] + [tail, level], 1)
+    low, high = row[:near], row[near:]
     out_mine_ref[...] = jnp.where(first_core, low, high).reshape(out_mine_ref.shape)
     out_theirs_ref[...] = jnp.where(first_core, high, low).reshape(out_theirs_ref.shape)
 
 
-def owner_kernel(in_ref, high_ref, low_ref, cos_ref, sin_ref, out_ref, sums_ref):
+def owner_kernel(own_ref, in_ref, high_ref, low_ref, cos_ref, sin_ref, out_ref):
     total = jnp.sum(in_ref[...], 0)
-    tail = total[:, 4 * K :]
-    sums_ref[...] = tail
-    owners = HALF // 2
+    tail = total[:, SPECTRA : SPECTRA + 128]
+    devices = out_ref.shape[0]
     rows = cos_ref.shape[1] // 4
-    quantities = [total[:, q * K : (q + 1) * K] for q in range(4)]
-    columns = jnp.concatenate(quantities + [jnp.zeros((4, K), f32)], 0).T
-    lane = lane_index((owners, 4 * rows))
-    where = lane // rows
-    z = jnp.zeros((owners, 4 * rows), f32)
+    count = SPECTRA // K
+    owners = devices // FAR
+    columns = jnp.concatenate([total[:, q * K : (q + 1) * K] for q in range(count)], 0).T
+    where = lane_index((devices, 4 * rows)) // rows
+    top = row_index((devices, 1)) == 0
+    z = [jnp.zeros((devices, 4 * rows), f32)] * (count // 4)
     for m in range(5):
         cos, sin = twiddle(cos_ref, sin_ref, m)
-        if m < 4:
-            part = columns[m * owners : (m + 1) * owners]
-            cols = [part[:, q : q + 1] for q in range(4)]
-        else:
-            top = row_index((owners, 1)) == 0
-            cols = [jnp.where(top, tail[:, q : q + 1], 0.0) for q in range(4)]
-        straight = jnp.where(where == 0, cols[0], jnp.where(where == 1, cols[1], jnp.where(where == 2, cols[2], cols[3])))
-        crossed = jnp.where(where == 0, -cols[1], jnp.where(where == 1, cols[0], jnp.where(where == 2, -cols[3], cols[2])))
-        z = z + straight * cos + crossed * sin
+        for i in range(count // 4):
+            if m < 4:
+                part = columns[m * devices : (m + 1) * devices]
+                cols = [part[:, q : q + 1] for q in range(4 * i, 4 * i + 4)]
+            else:
+                cols = [jnp.where(top, tail[:, q : q + 1], 0.0) for q in range(4 * i, 4 * i + 4)]
+            straight = jnp.where(where < 2, jnp.where(where == 0, cols[0], cols[1]), jnp.where(where == 2, cols[2], cols[3]))
+            crossed = jnp.where(where < 2, jnp.where(where == 0, -cols[1], cols[0]), jnp.where(where == 2, -cols[3], cols[2]))
+            z[i] = z[i] + straight * cos + crossed * sin
+    z = jnp.concatenate(z, 1)
     out = mm3((high_ref[...], low_ref[...]), pieces(jnp.concatenate([z, -swapped(z, rows)], 0)))
-    out_ref[...] = out.reshape(out_ref.shape)
-
-
-def grad_kernel(in_ref, sums_ref, share_ref, group_ref, high_ref, low_ref, out_ref, loss_ref, group_out_ref):
+    device = row_index((devices, rows))
+    level = jnp.zeros((devices, rows), f32)
+    for f in range(FAR):
+        at = SPECTRA + 128 + f * rows
+        level = jnp.where(device // owners == f, total[:, at : at + rows], level)
+    level = jnp.where(device % owners == own_ref[0], level, 0.0)
+    extra = jnp.concatenate([level, jnp.broadcast_to(tail[:, rows:] * (1.0 / owners), (devices, 3 * rows))], 1)
+    out_ref[...] = jnp.concatenate([out, extra], 1).reshape(out_ref.shape)
+
+
+def grad_kernel(in_ref, share_ref, group_ref, high_ref, low_ref, out_ref, loss_ref, group_out_ref):
     rows, length = out_ref.shape
     quarter = length // 4
-    owners = in_ref.shape[0]
-    a = in_ref[...].reshape(owners, 4 * rows)
-    odd_row = row_index((owners, rows)) % 2 == 1
+    devices, _, lanes = in_ref.shape
+    owners = devices // FAR
+    a = in_ref[...].reshape(devices, lanes)
+    parts = [a[f * owners : (f + 1) * owners] for f in range(FAR)]
+    a = (parts[0] + parts[1]) + (parts[2] + parts[3])
     none = jnp.zeros((owners, rows), f32)
-    real0, imag0, real1, imag1 = (a[:, i * rows : (i + 1) * rows] for i in range(4))
-    top = jnp.concatenate(
-        [none, jnp.where(odd_row, real0, 0.0), jnp.where(odd_row, 0.0, real0), jnp.where(odd_row, 0.0, -imag0)], 1
-    )
-    top_sin = jnp.concatenate(
-        [none, jnp.where(odd_row, -imag0, 0.0), jnp.where(odd_row, 0.0, -imag0), jnp.where(odd_row, 0.0, -real0)], 1
-    )
-    low = jnp.concatenate(
-        [jnp.where(odd_row, real1, 0.0), none, jnp.where(odd_row, 0.0, real1), jnp.where(odd_row, 0.0, imag1)], 1
-    )
-    low_sin = jnp.concatenate(
-        [jnp.where(odd_row, -imag1, 0.0), none, jnp.where(odd_row, 0.0, -imag1), jnp.where(odd_row, 0.0, real1)], 1
-    )
-    stack = jnp.concatenate([top, low, top_sin, low_sin], 0).T
+    slots = HALF // owners
+    by_cos, by_sin = [], []
+    for t in range(slots):
+        re, im = a[:, 2 * t * rows : (2 * t + 1) * rows], a[:, (2 * t + 1) * rows : (2 * t + 2) * rows]
+        group = t * owners // (HALF // 4)
+        by_cos += [jnp.concatenate(([none, none, re, -im], [none, re, none, none], [none, none, re, im], [re, none, none, none])[group], 1)]
+        by_sin += [jnp.concatenate(([none, none, -im, -re], [none, -im, none, none], [none, none, -im, re], [-im, none, none, none])[group], 1)]
+    stack = jnp.concatenate(by_cos + by_sin, 0).T
     both = mm3(pieces(stack), (high_ref[...], low_ref[...]))
-    sums = sums_ref[...]
-    const = jnp.broadcast_to(sums, (8, 128)).T[rows : 2 * rows, :1]
+    sums = jnp.sum(a[:, 2 * slots * rows :], 0, keepdims=True)
+    const = jnp.broadcast_to(sums, (8, 128)).T[:rows, :1]
     e = both[:rows] + const
     f = both[rows : 2 * rows]
     g = both[2 * rows : 3 * rows]
@@ -467,35 +484,38 @@
     out_ref[:, 2 * quarter : 3 * quarter] = up - g
     out_ref[:, 3 * quarter :] = down - h
     norming = 1.0 / (length * length)
-    loss_ref[...] = sums[:, 8:9] * norming
+    loss_ref[...] = sums[:, 80:81] * norming
     share = share_ref[...]
     against = jnp.sum(share * sums, 1, keepdims=True)
     pull = share * (sums - against) * norming
     group_out_ref[...] = jnp.sum((group_ref[...] * pull).T, 0, keepdims=True)
 
 
-def tables(rows, length, ring):
-    owners = HALF // 2
-    z = np.arange(ring)
-    by_owner = np.stack([4 * z + c + 1 for c in range(2)], 1).reshape(-1)
-    slots = np.concatenate([by_owner, by_owner + 2])
+def tables(rows, length, near):
+    devices = 2 * near * FAR
+    owner = np.arange(2 * near)
+    t = np.arange(HALF // len(owner))[:, None]
+    place = t * len(owner) + (owner % 2) * near + owner // 2
+    slots = (4 * (place % (HALF // 4)) + place // (HALF // 4) + 1).reshape(-1)
     cos, sin = turns(slots, np.arange(length // 4), length)
     row_table = np.concatenate([cos, sin], 0)
-    cos, sin = turns(np.arange(owners), np.arange(owners), owners)
+    cos, sin = turns(np.arange(devices), np.arange(devices), devices)
     dft = np.concatenate([cos, sin], 1)
-    in_order = np.concatenate([2 * z, 2 * z + 1])
+    n = np.arange(near)
+    in_order = np.concatenate([2 * near * f + 2 * n + c for f in range(FAR) for c in range(2)])
     turn = dft[in_order]
-    across = np.concatenate([np.arange(owners), owners * np.arange(8) - HALF])
+    across = np.concatenate([np.arange(devices), devices * np.arange(8) - HALF])
     cos, sin = turns(across, np.arange(rows), length)
     turning = np.tile(cos, (1, 4)).astype(np.float32), np.tile(sin, (1, 4)).astype(np.float32)
     samples = (length // COARSE) * np.arange(COARSE)
-    lanes = np.concatenate([4 * z + g + 1 for g in range(4)])
+    group = HALF // 4
+    lanes = np.concatenate([4 * np.arange(group) + g + 1 for g in range(4)])
     first = np.concatenate([lanes[:-1], [0]])
     cos_p, sin_p = turns(first, samples[: COARSE // 4], length)
     cos_m, sin_m = turns(lanes, samples[: COARSE // 4], length)
     field = []
     for e in range(4):
-        p, m = (slice(g * ring, (g + 1) * ring) for g in groups_of(e))
+        p, m = (slice(g * group, (g + 1) * group) for g in groups_of(e))
         real = np.concatenate([cos_p[p], -sin_p[p], cos_m[m], -sin_m[m]], 0)
         imag = np.concatenate([sin_p[p], cos_p[p], -sin_m[m], -cos_m[m]], 0)
         field.append(np.concatenate([real, imag], 1))
@@ -544,11 +564,11 @@
 
 def on_device(mask_field, target_print, source_points, source_groups, group_logits, pupil_radius):
     rows, length = mask_field.shape
-    ring = lax.axis_size(RING)
+    near = lax.axis_size(NEAR)
     pair = lax.axis_size(CORE)
-    owners = ring * pair
+    devices = FAR * near * pair
     sources = source_points.shape[0]
-    row_table, dft, turn, turning, field, spread = tables(rows, length, ring)
+    row_table, dft, turn, turning, field, spread = tables(rows, length, near)
     device = lax.axis_index(SLAB)
     norming = 1.0 / (length * length)
     cutoff = pupil_radius[0]
@@ -559,7 +579,8 @@
     def swap_all(parcels, axes):
         return lax.all_to_all(parcels, axes, split_axis=0, concat_axis=0, tiled=True)
 
-    parcels, own_sums = run(rows_kernel, (shape((owners, 1, 4 * rows)), shape((1, 128))), n_in=3)(mask_field, *row_table)
+    width = 2 * HALF // (near * pair) * rows + 4 * rows
+    parcels = run(rows_kernel, shape((devices, 1, width)), n_in=3, mib=56)(mask_field, *row_table)
     arrived = swap_all(parcels, SLAB)
     across = jnp.arange(K, dtype=jnp.int32) - HALF
     here = device * rows + jnp.arange(rows, dtype=jnp.int32)
@@ -570,8 +591,8 @@
         tuple(jax.ShapeDtypeStruct(t, bf16) for t in sizes) + (shape((8, 128)),),
         n_in=3,
     )(jnp.cos(angle), jnp.sin(angle), spread)
-    piece = run(columns_kernel, shape((ring, 1, PARCEL)), n_in=7)(arrived, own_sums, *dft, *turning, ready)
-    around = swap_all(piece, RING)
+    piece = run(columns_kernel, shape((near, 1, SPECTRA + 128)), n_in=6)(arrived, *dft, *turning, ready)
+    around = swap_all(piece, NEAR)
     theirs = lax.ppermute(around, CORE, [(i, (i + 1) % pair) for i in range(pair)])
 
     onehot = (source_groups[:, None] == jnp.arange(NG, dtype=jnp.int32)[None, :]).astype(f32)
@@ -580,9 +601,9 @@
     weight_share = weights / total_weight
     mine, theirs = run(
         image_kernel,
-        (shape((ring, 1, PARCEL)),) * 2,
+        (shape((near, 1, SPECTRA + 256)),) * 2,
         n_scalar=4,
-        n_in=15,
+        n_in=18,
         mib=28,
         scratch=image_scratch(sources, rows),
     )(
@@ -592,6 +613,8 @@
         lax.axis_index(CORE).reshape(1),
         around,
         theirs,
+        arrived,
+        *dft,
         *turn,
         *turning,
         local_p,
@@ -603,21 +626,22 @@
         target_print,
     )
     mine = mine + lax.ppermute(theirs, CORE, [(i, (i + 1) % pair) for i in range(pair)])
-    mine = swap_all(mine, RING)
-    parcels, sums = run(owner_kernel, (shape((owners, 1, 4 * rows)), shape((1, 128))), n_in=5)(mine, *dft, *turning)
+    mine = swap_all(mine, NEAR)
+    own = (lax.axis_index(NEAR) * pair + lax.axis_index(CORE)).reshape(1)
+    parcels = run(owner_kernel, shape((devices, 1, width)), n_scalar=1, n_in=5)(own, mine, *dft, *turning)
     arrived = swap_all(parcels, SLAB)
-    share_row = jnp.zeros((1, 128), f32).at[0, 16 : 16 + sources].set(weight_share)
-    group_rows = jnp.zeros((NG, 128), f32).at[:, 16 : 16 + sources].set(onehot.T)
+    share_row = jnp.zeros((1, 128), f32).at[0, 64 : 64 + sources].set(weight_share)
+    group_rows = jnp.zeros((NG, 128), f32).at[:, 64 : 64 + sources].set(onehot.T)
     mask_grad, loss_value, group_grad = run(
-        grad_kernel, (shape((rows, length)), shape((1, 1)), shape((1, NG))), n_in=6
-    )(arrived, sums, share_row, group_rows, *row_table)
+        grad_kernel, (shape((rows, length)), shape((1, 1)), shape((1, NG))), n_in=5
+    )(arrived, share_row, group_rows, *row_table)
     return (loss_value.reshape(1), mask_grad, group_grad.reshape(NG))
 
 
 def solution(mesh):
     cores = 2
-    ring = mesh.shape["slab"] // cores
-    split = Mesh(mesh.devices.reshape(mesh.shape["clip"], ring, cores), CLIP_SLAB)
+    near = mesh.shape["slab"] // cores // FAR
+    split = Mesh(mesh.devices.reshape(mesh.shape["clip"], FAR, near, cores), CLIP_SLAB)
     return jax.shard_map(
         on_device,
         mesh=split,

time: 181 us -> 166 us (0.917)
  blocking collectives: 35.7 us -> 14.5 us
  starting transfers between devices: 48.8 us -> 53 us
  local copies, waits for them, and re-layouts: 5.03 us -> 2.21 us
  Pallas kernels: 16 us -> 18.4 us
  waiting for transfers between devices: 69.5 us -> 71.8 us
    all_to_all x1, blocking collectives: 35.7 us -> 14.5 us  [swap_all(): lax.all_to_all(parcels, axes, split_axis=0, concat_axis=0, tiled=True)]
    all_to_all x3, starting transfers between devices: 45.4 us -> 50.1 us  [swap_all(): lax.all_to_all(parcels, axes, split_axis=0, concat_axis=0, tiled=True)]
    unnamed x36 -> x30, local copies, waits for them, and re-layouts: 3.4 us -> 0.58 us
    all_to_all x3, waiting for transfers between devices: 68.1 us -> 70.5 us  [swap_all(): lax.all_to_all(parcels, axes, split_axis=0, concat_axis=0, tiled=True)]
    pallas_call x4, Pallas kernels: 14.3 us -> 16.7 us  [the longest x1 10.5 us: on_device(): run(image_kernel, (shape((near, 1, SPECTRA + 256)),) * 2, n_scalar=4, n_i...]
where the time goes in v4:
time: 166 us
  waiting for transfers between devices  71.8 us (43%)
  starting transfers between devices  53 us (32%)
  Pallas kernels  18.4 us (11%)
  blocking collectives  14.5 us (9%)
  other arithmetic  4.29 us (3%)
  local copies, waits for them, and re-layouts  2.21 us (1%)
    all_to_all x3, waiting for transfers between devices, swap_all(): lax.all_to_all(parcels, axes, split_axis=0, concat_axis=0, tiled=True)  70.5 us
    all_to_all x3, starting transfers between devices, swap_all(): lax.all_to_all(parcels, axes, split_axis=0, concat_axis=0, tiled=True)  50.1 us
    all_to_all x1, blocking collectives, swap_all(): lax.all_to_all(parcels, axes, split_axis=0, concat_axis=0, tiled=True)  14.5 us
    pallas_call x1, Pallas kernels, on_device(): run(image_kernel, (shape((near, 1, SPECTRA + 256)),) * 2, n_scalar=4, n_i...  10.5 us
  transfers between devices with their start and end apart: 5, of which 4 were waited for; matrix products, arithmetic and copies ran while one was open for 3% of the time, Pallas kernels for 0%

profile of v4, /device:TPU:37, one launch (start us, length us, event | category | flops | bytes accessed | tf_op | source)
XLA Modules:
  0.0 165.7 jit_solution(20030924431226415)
XLA Ops:
  0.6 2.4 %shard_map.184 = f32[64,1,640]{2,1,0:T(1,128)} custom-call(f32[32,2048]{1,0:T(8,128)} %mask_ref.1, bf16[256,512]{1,0:T(8,128)(2,1)} %constant.130.clone.high_ref, bf16[256,512]{1,0:T(8,128)(2,1)} %constant.131.clone.low_ref), custom_call_target="tpu_custom_call" | custom-call | tf_op jit(solution)/shard_map/pallas_call | solution.py:583
  3.0 34.5 %all-to-all-start = ((f32[64,1,640]{2,1,0:T(1,128)}), f32[64,1,640]{2,1,0:T(1,128)S(1)}, u32[]{:S(2)}, u32[]{:S(2)}) async-start(f32[64,1,640]{2,1,0:T(1,128)} %shard_map.184), calls=%async_computation | async-start | bytes 327680 | tf_op jit(solution)/shard_map/all_to_all | solution.py:580
  37.5 0.0 copy-start.11
  37.5 0.0 copy-start.7
  37.5 0.0 copy-start.8
  37.5 0.2 fusion.3
  37.8 0.4 copy-done.11
  38.2 0.4 shard_map.185
  38.6 32.2 %all-to-all-done.in_ref.arrived_ref = f32[64,1,640]{2,1,0:T(1,128)S(1)} async-done(((f32[64,1,640]{2,1,0:T(1,128)}), f32[64,1,640]{2,1,0:T(1,128)S(1)}, u32[]{:S(2)}, u32[]{:S(2)}) %all-to-all-start) | async-done | bytes 163872 | tf_op jit(solution)/shard_map/all_to_all | solution.py:580
  70.8 0.0 copy-done.7
  70.8 0.0 copy-done.8
  70.8 0.0 copy-done.2
  70.8 0.0 copy-done.3
  70.8 0.0 copy-start.5
  70.8 1.5 shard_map.186
  72.3 3.7 %all-to-all-start.1 = ((f32[8,1,4224]{2,1,0:T(1,128)}), f32[8,1,4224]{2,1,0:T(1,128)S(1)}, u32[]{:S(2)}, u32[]{:S(2)}) async-start(f32[8,1,4224]{2,1,0:T(1,128)} %shard_map.186), calls=%async_computation.1 | async-start | bytes 270336 | tf_op jit(solution)/shard_map/all_to_all | solution.py:580
  76.0 0.0 copy-start.12
  76.7 0.0 copy-done.12
  76.7 0.1 copy.24
  76.8 0.6 and_reduce_fusion
  77.4 0.0 copy-done.13
  77.4 0.0 copy-done.14
  77.5 0.1 select_reduce_fusion
  77.5 0.7 exponential_reduce_fusion
  78.2 7.9 %all-to-all-done.1.mine_ref = f32[8,1,4224]{2,1,0:T(1,128)S(1)} async-done(((f32[8,1,4224]{2,1,0:T(1,128)}), f32[8,1,4224]{2,1,0:T(1,128)S(1)}, u32[]{:S(2)}, u32[]{:S(2)}) %all-to-all-start.1) | async-done | bytes 135200 | tf_op jit(solution)/shard_map/all_to_all | solution.py:580
  86.2 2.5 %collective-permute-start = (f32[8,1,4224]{2,1,0:T(1,128)S(1)}, f32[8,1,4224]{2,1,0:T(1,128)S(1)}, u32[]{:S(2)}, u32[]{:S(2)}) collective-permute-start(f32[8,1,4224]{2,1,0:T(1,128)S(1)} %all-to-all-done.1.mine_ref), channel_id=1, source_target_pairs={{0,1},{1,0},{2,3},{3,2},{4,5},{5,4},{6,7},{7,6},{8,9},{9,8},{10,11... | collective-permute-start | bytes 405512 | tf_op jit(solution)/shard_map/ppermute | solution.py:596
  88.7 1.2 fusion.6
  90.0 0.0 collective-permute-done.theirs_ref
  90.0 0.0 copy-done.6
  90.0 0.0 copy-done.5
  90.0 0.0 copy-done.4
  90.0 0.0 copy-done.9
  90.0 0.0 copy-done.10
  90.0 10.5 %shard_map.187 = (f32[8,1,4352]{2,1,0:T(1,128)S(1)}, f32[8,1,4352]{2,1,0:T(1,128)S(1)}) custom-call(s32[16,2]{1,0:T(8,128)S(1)} %add_select_fusion.1.shift_ref, f32[16]{0:T(128)S(1)} %get-tuple-element.52.share_ref, s32[1]{0:T(128)} %copy.26.radius_ref, s32[1]{0:T(128)} %bitcast.2.core_ref, f32[8,1,4224]{2,1,0:T(1,128)S(1)} %all-to-all-done.1.mine_ref, ...), custom_call_target="tpu_custom_call" | custom-call | tf_op jit(solution)/shard_map/pallas_call | solution.py:602
  100.5 0.4 collective-permute-start.1
  100.9 1.3 collective-permute-done.1
  102.2 0.1 add.44
  102.3 14.5 %all_to_all.20.in_ref = f32[8,1,4352]{2,1,0:T(1,128)S(1)} all-to-all(f32[8,1,4352]{2,1,0:T(1,128)S(1)} %add.44), channel_id=1, replica_groups=mesh['clip'=4,'slab_0'=4,'slab_1'=8,'slab_2'=2] {'slab_1'}, dimensions={0} | all-to-all | bytes 278528 | tf_op jit(solution)/shard_map/all_to_all | solution.py:580
  116.8 2.4 %shard_map.188 = f32[64,1,640]{2,1,0:T(1,128)} custom-call(s32[1]{0:T(128)} %bitcast.own_ref, f32[8,1,4352]{2,1,0:T(1,128)S(1)} %all_to_all.20.in_ref, bf16[64,128]{1,0:T(8,128)(2,1)S(1)} %copy-done.7, bf16[64,128]{1,0:T(8,128)(2,1)S(1)} %copy-done.8, f32[72,128]{1,0:T(8,128)S(1)} %copy-done.2, f32[72,128]{1,0:T(8,128)S(1)} %copy-done.3), custom_call_target="tpu_custom_call" | custom-call | tf_op jit(solution)/shard_map/pallas_call | solution.py:631
  119.2 11.9 %all-to-all-start.3 = ((f32[64,1,640]{2,1,0:T(1,128)}), f32[64,1,640]{2,1,0:T(1,128)S(1)}, u32[]{:S(2)}, u32[]{:S(2)}) async-start(f32[64,1,640]{2,1,0:T(1,128)} %shard_map.188), calls=%async_computation.3 | async-start | bytes 327680 | tf_op jit(solution)/shard_map/all_to_all | solution.py:580
  131.2 0.6 slice.36
  131.8 0.6 fusion.7
  132.4 0.6 convert_select_fusion
  133.1 0.1 scatter.9.group_ref
  133.2 0.9 scatter.6.share_ref
  134.0 30.5 %all-to-all-done.3.in_ref = f32[64,1,640]{2,1,0:T(1,128)S(1)} async-done(((f32[64,1,640]{2,1,0:T(1,128)}), f32[64,1,640]{2,1,0:T(1,128)S(1)}, u32[]{:S(2)}, u32[]{:S(2)}) %all-to-all-start.3) | async-done | bytes 163872 | tf_op jit(solution)/shard_map/all_to_all | solution.py:580
  164.5 0.0 copy-done.1
  164.5 1.2 shard_map.189
  (17 shorter events, 0.0 us)
Async XLA Ops:
  3.0 87.0 %copy-start.6 = (bf16[512,256]{1,0:T(8,128)(2,1)S(1)}, bf16[512,256]{1,0:T(8,128)(2,1)}, u32[]{:S(2)}) copy-start(bf16[512,256]{1,0:T(8,128)(2,1)} %constant.140.clone.field_low_ref) | copy-start | bytes 786436
  3.0 67.8 %all-to-all-start = ((f32[64,1,640]{2,1,0:T(1,128)}), f32[64,1,640]{2,1,0:T(1,128)S(1)}, u32[]{:S(2)}, u32[]{:S(2)}) async-start(f32[64,1,640]{2,1,0:T(1,128)} %shard_map.184), calls=%async_computation | async-start | bytes 327680 | tf_op jit(solution)/shard_map/all_to_all | solution.py:580
  37.5 0.7 copy-start.11
  37.5 33.3 %copy-start.7 = (bf16[64,128]{1,0:T(8,128)(2,1)S(1)}, bf16[64,128]{1,0:T(8,128)(2,1)}, u32[]{:S(2)}) copy-start(bf16[64,128]{1,0:T(8,128)(2,1)} %constant.133.clone.dft_high_ref.high_ref) | copy-start | bytes 49156
  37.5 33.3 %copy-start.8 = (bf16[64,128]{1,0:T(8,128)(2,1)S(1)}, bf16[64,128]{1,0:T(8,128)(2,1)}, u32[]{:S(2)}) copy-start(bf16[64,128]{1,0:T(8,128)(2,1)} %constant.134.clone.dft_low_ref.low_ref) | copy-start | bytes 49156
  38.2 32.6 %copy-start.2 = (f32[72,128]{1,0:T(8,128)S(1)}, f32[72,128]{1,0:T(8,128)}, u32[]{:S(2)}) copy-start(f32[72,128]{1,0:T(8,128)} %constant.135.clone.cos_ref) | copy-start | bytes 110596
  38.2 32.6 %copy-start.3 = (f32[72,128]{1,0:T(8,128)S(1)}, f32[72,128]{1,0:T(8,128)}, u32[]{:S(2)}) copy-start(f32[72,128]{1,0:T(8,128)} %constant.136.clone.sin_ref) | copy-start | bytes 110596
  70.8 19.2 %copy-start.5 = (bf16[512,256]{1,0:T(8,128)(2,1)S(1)}, bf16[512,256]{1,0:T(8,128)(2,1)}, u32[]{:S(2)}) copy-start(bf16[512,256]{1,0:T(8,128)(2,1)} %constant.139.clone.field_high_ref) | copy-start | bytes 786436
  72.3 17.7 %copy-start.4 = (s32[32,2048]{1,0:T(8,128)S(1)}, s32[32,2048]{1,0:T(8,128)}, u32[]{:S(2)}) copy-start(s32[32,2048]{1,0:T(8,128)} %target_ref.1) | copy-start | bytes 786436
  72.3 13.9 %all-to-all-start.1 = ((f32[8,1,4224]{2,1,0:T(1,128)}), f32[8,1,4224]{2,1,0:T(1,128)S(1)}, u32[]{:S(2)}, u32[]{:S(2)}) async-start(f32[8,1,4224]{2,1,0:T(1,128)} %shard_map.186), calls=%async_computation.1 | async-start | bytes 270336 | tf_op jit(solution)/shard_map/all_to_all | solution.py:580
  76.0 0.7 copy-start.12
  76.8 0.7 copy-start.13
  76.8 0.7 copy-start.14
  78.2 11.8 %copy-start.9 = (bf16[64,128]{1,0:T(8,128)(2,1)S(1)}, bf16[64,128]{1,0:T(8,128)(2,1)}, u32[]{:S(2)}) copy-start(bf16[64,128]{1,0:T(8,128)(2,1)} %constant.137.clone.turn_high_ref) | copy-start | bytes 49156
  78.2 11.8 %copy-start.10 = (bf16[64,128]{1,0:T(8,128)(2,1)S(1)}, bf16[64,128]{1,0:T(8,128)(2,1)}, u32[]{:S(2)}) copy-start(bf16[64,128]{1,0:T(8,128)(2,1)} %constant.138.clone.turn_low_ref) | copy-start | bytes 49156
  86.2 3.8 %collective-permute-start = (f32[8,1,4224]{2,1,0:T(1,128)S(1)}, f32[8,1,4224]{2,1,0:T(1,128)S(1)}, u32[]{:S(2)}, u32[]{:S(2)}) collective-permute-start(f32[8,1,4224]{2,1,0:T(1,128)S(1)} %all-to-all-done.1.mine_ref), channel_id=1, source_target_pairs={{0,1},{1,0},{2,3},{3,2},{4,5},{5,4},{6,7},{7,6},{8,9},{9,8},{10,11... | collective-permute-start | bytes 405512 | tf_op jit(solution)/shard_map/ppermute | solution.py:596
  100.5 1.7 %collective-permute-start.1 = (f32[8,1,4352]{2,1,0:T(1,128)S(1)}, f32[8,1,4352]{2,1,0:T(1,128)S(1)}, u32[]{:S(2)}, u32[]{:S(2)}) collective-permute-start(f32[8,1,4352]{2,1,0:T(1,128)S(1)} %get-tuple-element.47), channel_id=1, source_target_pairs={{0,1},{1,0},{2,3},{3,2},{4,5},{5,4},{6,7},{7,6},{8,9},{9,8},{10,11... | collective-permute-start | bytes 417800 | tf_op jit(solution)/shard_map/ppermute | solution.py:628
  116.8 47.7 %copy-start.1 = (bf16[256,512]{1,0:T(8,128)(2,1)S(1)}, bf16[256,512]{1,0:T(8,128)(2,1)}, u32[]{:S(2)}) copy-start(bf16[256,512]{1,0:T(8,128)(2,1)} %constant.131.clone.low_ref) | copy-start | bytes 786436
  119.2 45.3 %copy-start = (bf16[256,512]{1,0:T(8,128)(2,1)S(1)}, bf16[256,512]{1,0:T(8,128)(2,1)}, u32[]{:S(2)}) copy-start(bf16[256,512]{1,0:T(8,128)(2,1)} %constant.130.clone.high_ref) | copy-start | bytes 786436
  119.2 45.3 %all-to-all-start.3 = ((f32[64,1,640]{2,1,0:T(1,128)}), f32[64,1,640]{2,1,0:T(1,128)S(1)}, u32[]{:S(2)}, u32[]{:S(2)}) async-start(f32[64,1,640]{2,1,0:T(1,128)} %shard_map.188), calls=%async_computation.3 | async-start | bytes 327680 | tf_op jit(solution)/shard_map/all_to_all | solution.py:580

commit v5 on v4

--- a/solution.py
+++ b/solution.py
@@ -138,7 +138,7 @@
         spread_low_ref[i * near : (i + 1) * near] = low
 
 
-def columns_kernel(in_ref, dft_high_ref, dft_low_ref, cos_ref, sin_ref, ready_ref, piece_ref):
+def columns_kernel(in_ref, dft_high_ref, dft_low_ref, cos_ref, sin_ref, ready_ref, share_ref, piece_ref):
     devices, _, lanes = in_ref.shape
     rows = cos_ref.shape[1] // 4
     lanes -= 4 * rows
@@ -306,7 +306,7 @@
             out.append(total[q] + share_ref[s] * (real[q] * real[q] + imag[q] * imag[q]))
         return tuple(out)
 
-    coarse = lax.fori_loop(0, sources, expose, (jnp.zeros((rows, HALF), f32),) * 4, unroll=2)
+    coarse = lax.fori_loop(0, sources, expose, (jnp.zeros((rows, HALF), f32),) * 4, unroll=16)
     spread = spread_high_ref[...], spread_low_ref[...]
     quarter = COARSE // 4
     spread = [tuple(t[at : at + n] for t in spread) for at, n in ((0, quarter), (quarter, quarter), (2 * quarter, 2 * quarter))]
@@ -369,7 +369,7 @@
             back_low_ref[at_rows, i * HALF : (i + 1) * HALF] = low
         return carry
 
-    lax.fori_loop(0, sources, push, 0, unroll=2)
+    lax.fori_loop(0, sources, push, 0, unroll=16)
     for e, (high, low) in enumerate(field_tables):
         lanes = slice(e * 2 * HALF, (e + 1) * 2 * HALF)
         both = mm(back_high_ref[:, lanes], jnp.concatenate([high, low], 0), NT)
@@ -428,21 +428,24 @@
     count = SPECTRA // K
     owners = devices // FAR
     columns = jnp.concatenate([total[:, q * K : (q + 1) * K] for q in range(count)], 0).T
-    where = lane_index((devices, 4 * rows)) // rows
-    top = row_index((devices, 1)) == 0
-    z = [jnp.zeros((devices, 4 * rows), f32)] * (count // 4)
+    edge = jnp.where(row_index((8, count)) == 0, tail[:, :count], 0.0)
+    columns = jnp.concatenate(pieces(jnp.concatenate([columns, edge], 0)), 1)
+    lanes = count * rows
+    have = row_index((2 * count, lanes)) % count
+    want = lane_index((2 * count, lanes)) // rows
+    straight = jnp.where(have == want, 1.0, 0.0)
+    partner = jnp.where(want % 2 == 0, want + 1, want - 1)
+    crossed = jnp.where(have == partner, jnp.where(want % 2 == 0, -1.0, 1.0), 0.0)
+    straight = mm(columns, straight.astype(bf16))
+    crossed = mm(columns, crossed.astype(bf16))
+    z = jnp.zeros((devices, lanes), f32)
     for m in range(5):
-        cos, sin = twiddle(cos_ref, sin_ref, m)
-        for i in range(count // 4):
-            if m < 4:
-                part = columns[m * devices : (m + 1) * devices]
-                cols = [part[:, q : q + 1] for q in range(4 * i, 4 * i + 4)]
-            else:
-                cols = [jnp.where(top, tail[:, q : q + 1], 0.0) for q in range(4 * i, 4 * i + 4)]
-            straight = jnp.where(where < 2, jnp.where(where == 0, cols[0], cols[1]), jnp.where(where == 2, cols[2], cols[3]))
-            crossed = jnp.where(where < 2, jnp.where(where == 0, -cols[1], cols[0]), jnp.where(where == 2, -cols[3], cols[2]))
-            z[i] = z[i] + straight * cos + crossed * sin
-    z = jnp.concatenate(z, 1)
+        cos, sin = (jnp.concatenate([t] * (count // 4), 1) for t in twiddle(cos_ref, sin_ref, m))
+        if m < 4:
+            z = z + straight[m * devices : (m + 1) * devices] * cos + crossed[m * devices : (m + 1) * devices] * sin
+        else:
+            last = straight[K:] * cos[:8] + crossed[K:] * sin[:8]
+            z = jnp.concatenate([z[:8] + last, z[8:]], 0)
     out = mm3((high_ref[...], low_ref[...]), pieces(jnp.concatenate([z, -swapped(z, rows)], 0)))
     device = row_index((devices, rows))
     level = jnp.zeros((devices, rows), f32)
@@ -579,6 +582,10 @@
     def swap_all(parcels, axes):
         return lax.all_to_all(parcels, axes, split_axis=0, concat_axis=0, tiled=True)
 
+    onehot = (source_groups[:, None] == jnp.arange(NG, dtype=jnp.int32)[None, :]).astype(f32)
+    weights = jnp.exp(jnp.sum(onehot * group_logits[None, :], 1))
+    total_weight = jnp.sum(weights)
+    weight_share = weights / total_weight
     width = 2 * HALF // (near * pair) * rows + 4 * rows
     parcels = run(rows_kernel, shape((devices, 1, width)), n_in=3, mib=56)(mask_field, *row_table)
     arrived = swap_all(parcels, SLAB)
@@ -591,14 +598,12 @@
         tuple(jax.ShapeDtypeStruct(t, bf16) for t in sizes) + (shape((8, 128)),),
         n_in=3,
     )(jnp.cos(angle), jnp.sin(angle), spread)
-    piece = run(columns_kernel, shape((near, 1, SPECTRA + 128)), n_in=6)(arrived, *dft, *turning, ready)
+    piece = run(columns_kernel, shape((near, 1, SPECTRA + 128)), n_in=7)(
+        arrived, *dft, *turning, ready, weight_share.reshape(1, sources)
+    )
     around = swap_all(piece, NEAR)
     theirs = lax.ppermute(around, CORE, [(i, (i + 1) % pair) for i in range(pair)])
 
-    onehot = (source_groups[:, None] == jnp.arange(NG, dtype=jnp.int32)[None, :]).astype(f32)
-    weights = jnp.exp(jnp.sum(onehot * group_logits[None, :], 1))
-    total_weight = jnp.sum(weights)
-    weight_share = weights / total_weight
     mine, theirs = run(
         image_kernel,
         (shape((near, 1, SPECTRA + 256)),) * 2,

time: 166 us -> 165 us (level)
  transfers between devices with their start and end apart: 5 -> 5, of which waited for: 4 -> 5; matrix products, arithmetic and copies ran while one was open for 3% -> 3% of each run, Pallas kernels for 0% -> 0%
where the time goes in v5:
time: 165 us; the launch traced here: 164 us
  waiting for transfers between devices  71.4 us (43%)
  starting transfers between devices  53.1 us (32%)
  Pallas kernels  17.4 us (11%)
  blocking collectives  14.4 us (9%)
  other arithmetic  4.18 us (3%)
  local copies, waits for them, and re-layouts  2.14 us (1%)
    all_to_all x3, waiting for transfers between devices, swap_all(): lax.all_to_all(parcels, axes, split_axis=0, concat_axis=0, tiled=True)  69.5 us
    all_to_all x3, starting transfers between devices, swap_all(): lax.all_to_all(parcels, axes, split_axis=0, concat_axis=0, tiled=True)  50.1 us
    all_to_all x1, blocking collectives, swap_all(): lax.all_to_all(parcels, axes, split_axis=0, concat_axis=0, tiled=True)  14.4 us
    pallas_call x1, Pallas kernels, on_device(): run(image_kernel, (shape((near, 1, SPECTRA + 256)),) * 2, n_scalar=4, n_i...  10.4 us
  transfers between devices with their start and end apart: 5, of which 5 were waited for; matrix products, arithmetic and copies ran while one was open for 3% of the time, Pallas kernels for 0%

profile of v5, /device:TPU:37, one launch (start us, length us, event | category | flops | bytes accessed | tf_op | source)
XLA Modules:
  0.0 164.2 jit_solution(16683688017743086665)
XLA Ops:
  0.6 2.4 %shard_map.184 = f32[64,1,640]{2,1,0:T(1,128)} custom-call(f32[32,2048]{1,0:T(8,128)} %mask_ref.1, bf16[256,512]{1,0:T(8,128)(2,1)} %constant.130.clone.high_ref, bf16[256,512]{1,0:T(8,128)(2,1)} %constant.131.clone.low_ref), custom_call_target="tpu_custom_call" | custom-call | tf_op jit(solution)/shard_map/pallas_call | solution.py:590
  3.0 34.5 %all-to-all-start = ((f32[64,1,640]{2,1,0:T(1,128)}), f32[64,1,640]{2,1,0:T(1,128)S(1)}, u32[]{:S(2)}, u32[]{:S(2)}) async-start(f32[64,1,640]{2,1,0:T(1,128)} %shard_map.184), calls=%async_computation | async-start | bytes 327680 | tf_op jit(solution)/shard_map/all_to_all | solution.py:583
  37.5 0.0 copy-start.11
  37.5 0.0 copy-start.13
  37.5 0.0 copy-start.14
  37.5 0.0 copy-start.8
  37.6 0.2 fusion.3
  37.8 0.0 copy-start.7
  37.8 0.4 copy-done.11
  38.2 0.4 shard_map.185
  38.6 0.7 and_reduce_fusion
  39.3 0.0 copy-done.13
  39.3 0.0 copy-done.14
  39.3 0.1 select_reduce_fusion
  39.4 0.6 exponential_reduce_fusion
  39.9 1.2 broadcast_select_fusion
  41.1 29.6 %all-to-all-done.in_ref.arrived_ref = f32[64,1,640]{2,1,0:T(1,128)S(1)} async-done(((f32[64,1,640]{2,1,0:T(1,128)}), f32[64,1,640]{2,1,0:T(1,128)S(1)}, u32[]{:S(2)}, u32[]{:S(2)}) %all-to-all-start) | async-done | bytes 163872 | tf_op jit(solution)/shard_map/all_to_all | solution.py:583
  70.8 0.0 copy-done.8
  70.8 0.0 copy-done.7
  70.8 0.0 copy-done.2
  70.8 0.0 copy-done.3
  70.8 0.0 copy-start.4
  70.8 0.0 copy-start.5
  70.8 1.5 shard_map.186
  72.3 3.6 %all-to-all-start.1 = ((f32[8,1,4224]{2,1,0:T(1,128)}), f32[8,1,4224]{2,1,0:T(1,128)S(1)}, u32[]{:S(2)}, u32[]{:S(2)}) async-start(f32[8,1,4224]{2,1,0:T(1,128)} %shard_map.186), calls=%async_computation.1 | async-start | bytes 270336 | tf_op jit(solution)/shard_map/all_to_all | solution.py:583
  75.9 0.0 copy-start.12
  76.6 0.0 copy-done.12
  76.6 0.0 copy-start.10
  76.6 0.1 copy.24
  76.7 9.4 %all-to-all-done.1.mine_ref = f32[8,1,4224]{2,1,0:T(1,128)S(1)} async-done(((f32[8,1,4224]{2,1,0:T(1,128)}), f32[8,1,4224]{2,1,0:T(1,128)S(1)}, u32[]{:S(2)}, u32[]{:S(2)}) %all-to-all-start.1) | async-done | bytes 135200 | tf_op jit(solution)/shard_map/all_to_all | solution.py:583
  86.0 2.5 %collective-permute-start = (f32[8,1,4224]{2,1,0:T(1,128)S(1)}, f32[8,1,4224]{2,1,0:T(1,128)S(1)}, u32[]{:S(2)}, u32[]{:S(2)}) collective-permute-start(f32[8,1,4224]{2,1,0:T(1,128)S(1)} %all-to-all-done.1.mine_ref), channel_id=1, source_target_pairs={{0,1},{1,0},{2,3},{3,2},{4,5},{5,4},{6,7},{7,6},{8,9},{9,8},{10,11... | collective-permute-start | bytes 405512 | tf_op jit(solution)/shard_map/ppermute | solution.py:605
  88.6 1.0 collective-permute-done.theirs_ref
  89.6 0.0 copy-done.5
  89.6 10.4 %shard_map.187 = (f32[8,1,4352]{2,1,0:T(1,128)S(1)}, f32[8,1,4352]{2,1,0:T(1,128)S(1)}) custom-call(s32[16,2]{1,0:T(8,128)S(1)} %add_select_fusion.1.shift_ref, f32[16]{0:T(128)S(1)} %get-tuple-element.52.share_ref, s32[1]{0:T(128)} %copy.26.radius_ref, s32[1]{0:T(128)} %bitcast.2.core_ref, f32[8,1,4224]{2,1,0:T(1,128)S(1)} %all-to-all-done.1.mine_ref, ...), custom_call_target="tpu_custom_call" | custom-call | tf_op jit(solution)/shard_map/pallas_call | solution.py:607
  100.0 0.5 collective-permute-start.1
  100.5 1.0 collective-permute-done.1
  101.5 0.1 add.44
  101.6 14.4 %all_to_all.20.in_ref = f32[8,1,4352]{2,1,0:T(1,128)S(1)} all-to-all(f32[8,1,4352]{2,1,0:T(1,128)S(1)} %add.44), channel_id=1, replica_groups=mesh['clip'=4,'slab_0'=4,'slab_1'=8,'slab_2'=2] {'slab_1'}, dimensions={0} | all-to-all | bytes 278528 | tf_op jit(solution)/shard_map/all_to_all | solution.py:583
  116.0 1.5 shard_map.188
  117.6 12.1 %all-to-all-start.3 = ((f32[64,1,640]{2,1,0:T(1,128)}), f32[64,1,640]{2,1,0:T(1,128)S(1)}, u32[]{:S(2)}, u32[]{:S(2)}) async-start(f32[64,1,640]{2,1,0:T(1,128)} %shard_map.188), calls=%async_computation.3 | async-start | bytes 327680 | tf_op jit(solution)/shard_map/all_to_all | solution.py:583
  129.7 0.6 slice.36
  130.2 0.6 fusion.6
  130.9 0.6 convert_select_fusion
  131.5 0.1 scatter.9.group_ref
  131.6 0.9 scatter.6.share_ref
  132.5 30.5 %all-to-all-done.3.in_ref = f32[64,1,640]{2,1,0:T(1,128)S(1)} async-done(((f32[64,1,640]{2,1,0:T(1,128)}), f32[64,1,640]{2,1,0:T(1,128)S(1)}, u32[]{:S(2)}, u32[]{:S(2)}) %all-to-all-start.3) | async-done | bytes 163872 | tf_op jit(solution)/shard_map/all_to_all | solution.py:583
  163.0 0.0 copy-done.1
  163.0 1.2 shard_map.189
  (17 shorter events, 0.1 us)
Async XLA Ops:
  3.0 86.6 %copy-start.6 = (bf16[512,256]{1,0:T(8,128)(2,1)S(1)}, bf16[512,256]{1,0:T(8,128)(2,1)}, u32[]{:S(2)}) copy-start(bf16[512,256]{1,0:T(8,128)(2,1)} %constant.140.clone.field_low_ref) | copy-start | bytes 786436
  3.0 67.8 %all-to-all-start = ((f32[64,1,640]{2,1,0:T(1,128)}), f32[64,1,640]{2,1,0:T(1,128)S(1)}, u32[]{:S(2)}, u32[]{:S(2)}) async-start(f32[64,1,640]{2,1,0:T(1,128)} %shard_map.184), calls=%async_computation | async-start | bytes 327680 | tf_op jit(solution)/shard_map/all_to_all | solution.py:583
  37.5 0.7 copy-start.11
  37.5 1.8 %copy-start.13 = (s32[16]{0:T(128)S(1)}, s32[16]{0:T(128)}, u32[]{:S(2)}) copy-start(s32[16]{0:T(128)} %param.24) | copy-start | bytes 196
  37.5 1.8 %copy-start.14 = (f32[8]{0:T(128)S(1)}, f32[8]{0:T(128)}, u32[]{:S(2)}) copy-start(f32[8]{0:T(128)} %param.25) | copy-start | bytes 100
  37.5 33.2 %copy-start.8 = (bf16[64,128]{1,0:T(8,128)(2,1)S(1)}, bf16[64,128]{1,0:T(8,128)(2,1)}, u32[]{:S(2)}) copy-start(bf16[64,128]{1,0:T(8,128)(2,1)} %constant.134.clone.dft_low_ref.low_ref) | copy-start | bytes 49156
  37.8 33.0 %copy-start.7 = (bf16[64,128]{1,0:T(8,128)(2,1)S(1)}, bf16[64,128]{1,0:T(8,128)(2,1)}, u32[]{:S(2)}) copy-start(bf16[64,128]{1,0:T(8,128)(2,1)} %constant.133.clone.dft_high_ref.high_ref) | copy-start | bytes 49156
  38.2 32.6 %copy-start.2 = (f32[72,128]{1,0:T(8,128)S(1)}, f32[72,128]{1,0:T(8,128)}, u32[]{:S(2)}) copy-start(f32[72,128]{1,0:T(8,128)} %constant.135.clone.cos_ref) | copy-start | bytes 110596
  38.2 32.6 %copy-start.3 = (f32[72,128]{1,0:T(8,128)S(1)}, f32[72,128]{1,0:T(8,128)}, u32[]{:S(2)}) copy-start(f32[72,128]{1,0:T(8,128)} %constant.136.clone.sin_ref) | copy-start | bytes 110596
  70.8 18.8 %copy-start.4 = (s32[32,2048]{1,0:T(8,128)S(1)}, s32[32,2048]{1,0:T(8,128)}, u32[]{:S(2)}) copy-start(s32[32,2048]{1,0:T(8,128)} %target_ref.1) | copy-start | bytes 786436
  70.8 18.8 %copy-start.5 = (bf16[512,256]{1,0:T(8,128)(2,1)S(1)}, bf16[512,256]{1,0:T(8,128)(2,1)}, u32[]{:S(2)}) copy-start(bf16[512,256]{1,0:T(8,128)(2,1)} %constant.139.clone.field_high_ref) | copy-start | bytes 786436
  72.3 13.7 %all-to-all-start.1 = ((f32[8,1,4224]{2,1,0:T(1,128)}), f32[8,1,4224]{2,1,0:T(1,128)S(1)}, u32[]{:S(2)}, u32[]{:S(2)}) async-start(f32[8,1,4224]{2,1,0:T(1,128)} %shard_map.186), calls=%async_computation.1 | async-start | bytes 270336 | tf_op jit(solution)/shard_map/all_to_all | solution.py:583
  75.9 0.7 copy-start.12
  76.6 13.0 %copy-start.10 = (bf16[64,128]{1,0:T(8,128)(2,1)S(1)}, bf16[64,128]{1,0:T(8,128)(2,1)}, u32[]{:S(2)}) copy-start(bf16[64,128]{1,0:T(8,128)(2,1)} %constant.138.clone.turn_low_ref) | copy-start | bytes 49156
  76.7 12.9 %copy-start.9 = (bf16[64,128]{1,0:T(8,128)(2,1)S(1)}, bf16[64,128]{1,0:T(8,128)(2,1)}, u32[]{:S(2)}) copy-start(bf16[64,128]{1,0:T(8,128)(2,1)} %constant.137.clone.turn_high_ref) | copy-start | bytes 49156
  86.0 3.5 %collective-permute-start = (f32[8,1,4224]{2,1,0:T(1,128)S(1)}, f32[8,1,4224]{2,1,0:T(1,128)S(1)}, u32[]{:S(2)}, u32[]{:S(2)}) collective-permute-start(f32[8,1,4224]{2,1,0:T(1,128)S(1)} %all-to-all-done.1.mine_ref), channel_id=1, source_target_pairs={{0,1},{1,0},{2,3},{3,2},{4,5},{5,4},{6,7},{7,6},{8,9},{9,8},{10,11... | collective-permute-start | bytes 405512 | tf_op jit(solution)/shard_map/ppermute | solution.py:605
  100.0 1.5 collective-permute-start.1
  116.0 46.9 %copy-start.1 = (bf16[256,512]{1,0:T(8,128)(2,1)S(1)}, bf16[256,512]{1,0:T(8,128)(2,1)}, u32[]{:S(2)}) copy-start(bf16[256,512]{1,0:T(8,128)(2,1)} %constant.131.clone.low_ref) | copy-start | bytes 786436
  117.6 45.4 %copy-start = (bf16[256,512]{1,0:T(8,128)(2,1)S(1)}, bf16[256,512]{1,0:T(8,128)(2,1)}, u32[]{:S(2)}) copy-start(bf16[256,512]{1,0:T(8,128)(2,1)} %constant.130.clone.high_ref) | copy-start | bytes 786436
  117.6 45.4 %all-to-all-start.3 = ((f32[64,1,640]{2,1,0:T(1,128)}), f32[64,1,640]{2,1,0:T(1,128)S(1)}, u32[]{:S(2)}, u32[]{:S(2)}) async-start(f32[64,1,640]{2,1,0:T(1,128)} %shard_map.188), calls=%async_computation.3 | async-start | bytes 327680 | tf_op jit(solution)/shard_map/all_to_all | solution.py:583

commit v6 on v5

--- a/solution.py
+++ b/solution.py
@@ -82,7 +82,7 @@
     return cos * cos_m - sin * sin_m, sin * cos_m + cos * sin_m
 
 
-def rows_kernel(mask_ref, high_ref, low_ref, out_ref):
+def rows_kernel(core_ref, mask_ref, high_ref, low_ref, mine_ref, theirs_ref):
     rows, length = mask_ref.shape
     quarter = length // 4
     m0, m1, m2, m3 = (mask_ref[:, q * quarter : (q + 1) * quarter] for q in range(4))
@@ -99,15 +99,29 @@
     g0, g1, g2, g3 = (slice(g * group, (g + 1) * group) for g in range(4))
     real = [ca[g0] - sb[g0], c2[g1], ca[g2] + sb[g2], c0[g3]]
     imag = [-sa[g0] - cb[g0], -s2[g1], cb[g2] - sa[g2], -s0[g3]]
-    owners = out_ref.shape[0] // FAR
+    chips = mine_ref.shape[0] // FAR
+    owners = 2 * chips
     slots = group // owners
     blocks = []
     for re, im in zip(real, imag):
         for t in range(slots):
             blocks += [re[t * owners : (t + 1) * owners], im[t * owners : (t + 1) * owners]]
-    blocks += [jnp.broadcast_to(sums, (owners, rows)), jnp.zeros((owners, 3 * rows), f32)]
     parcels = jnp.concatenate(blocks, 1)
-    out_ref[...] = jnp.concatenate([parcels] * FAR, 0).reshape(out_ref.shape)
+    sums = jnp.broadcast_to(sums, (chips, rows))
+    none = jnp.zeros((chips, rows), f32)
+    first_core = core_ref[0] == 0
+    low, high = parcels[:chips], parcels[chips:]
+    empty = jnp.zeros(low.shape, f32)
+    for out_ref, part in (
+        (mine_ref, [jnp.where(first_core, low, high), empty, sums, none]),
+        (theirs_ref, [empty, jnp.where(first_core, high, low), none, sums]),
+    ):
+        part = jnp.concatenate(part + [none, none], 1)
+        out_ref[...] = jnp.concatenate([part] * FAR, 0).reshape(out_ref.shape)
+
+
+def both_cores(first_core, own, other):
+    return jnp.concatenate([jnp.where(first_core, own, other), jnp.where(first_core, other, own)], 0)
 
 
 def local_kernel(
@@ -138,12 +152,16 @@
         spread_low_ref[i * near : (i + 1) * near] = low
 
 
-def columns_kernel(in_ref, dft_high_ref, dft_low_ref, cos_ref, sin_ref, ready_ref, share_ref, piece_ref):
-    devices, _, lanes = in_ref.shape
+def columns_kernel(core_ref, in_ref, dft_high_ref, dft_low_ref, cos_ref, sin_ref, ready_ref, share_ref, piece_ref):
+    chips, _, lanes = in_ref.shape
     rows = cos_ref.shape[1] // 4
-    lanes -= 4 * rows
-    a = in_ref[...].reshape(devices, lanes + 4 * rows)[:, :lanes]
-    z = mm3((dft_high_ref[...], dft_low_ref[...]), pieces(jnp.concatenate([a, swapped(a, rows)], 0)))
+    lanes = (lanes - 4 * rows) // 2
+    a = in_ref[...].reshape(chips, 2 * lanes + 4 * rows)
+    a = both_cores(core_ref[0] == 0, a[:, :lanes], a[:, lanes : 2 * lanes])
+    turn = dft_high_ref[...], dft_low_ref[...]
+    devices = 2 * chips
+    by_cos, by_sin = (tuple(t[:, i * devices : (i + 1) * devices] for t in turn) for i in range(2))
+    z = mm3(by_cos, pieces(a), TN) + mm3(by_sin, pieces(swapped(a, rows)), TN)
     turned = swapped(z, rows)
     blocks = []
     for m in range(5):
@@ -217,9 +235,11 @@
         for part in range(2)
     ]
     tail = jnp.concatenate(tail + [jnp.zeros((HALF, 6), f32)], 1).T
-    devices = arrived_ref.shape[0]
-    row_sums = arrived_ref[...].reshape(devices, arrived_ref.shape[2])[:, arrived_ref.shape[2] - 4 * rows :]
-    z = mm3((dft_high_ref[...], dft_low_ref[...]), pieces(row_sums[:, :rows]), TN)
+    chips, _, lanes = arrived_ref.shape
+    devices = 2 * chips
+    row_sums = arrived_ref[...].reshape(chips, lanes)[:, lanes - 4 * rows :]
+    row_sums = both_cores(first_core, row_sums[:, :rows], row_sums[:, rows : 2 * rows])
+    z = mm3((dft_high_ref[...], dft_low_ref[...]), pieces(row_sums), TN)
     z_real, z_imag = z[:devices], -z[devices:]
     turns_of = [tuple(t[:, :rows] for t in twiddle(cos_ref, sin_ref, m)) for m in range(4)]
     zero = [
@@ -420,10 +440,11 @@
     out_theirs_ref[...] = jnp.where(first_core, high, low).reshape(out_theirs_ref.shape)
 
 
-def owner_kernel(own_ref, in_ref, high_ref, low_ref, cos_ref, sin_ref, out_ref):
+def owner_kernel(core_ref, near_ref, in_ref, high_ref, low_ref, cos_ref, sin_ref, mine_ref, theirs_ref):
     total = jnp.sum(in_ref[...], 0)
     tail = total[:, SPECTRA : SPECTRA + 128]
-    devices = out_ref.shape[0]
+    chips = mine_ref.shape[0]
+    devices = 2 * chips
     rows = cos_ref.shape[1] // 4
     count = SPECTRA // K
     owners = devices // FAR
@@ -447,24 +468,35 @@
             last = straight[K:] * cos[:8] + crossed[K:] * sin[:8]
             z = jnp.concatenate([z[:8] + last, z[8:]], 0)
     out = mm3((high_ref[...], low_ref[...]), pieces(jnp.concatenate([z, -swapped(z, rows)], 0)))
-    device = row_index((devices, rows))
-    level = jnp.zeros((devices, rows), f32)
+    near = chips // FAR
+    chip = row_index((chips, rows))
+    level = jnp.zeros((chips, rows), f32)
     for f in range(FAR):
         at = SPECTRA + 128 + f * rows
-        level = jnp.where(device // owners == f, total[:, at : at + rows], level)
-    level = jnp.where(device % owners == own_ref[0], level, 0.0)
-    extra = jnp.concatenate([level, jnp.broadcast_to(tail[:, rows:] * (1.0 / owners), (devices, 3 * rows))], 1)
-    out_ref[...] = jnp.concatenate([out, extra], 1).reshape(out_ref.shape)
-
-
-def grad_kernel(in_ref, share_ref, group_ref, high_ref, low_ref, out_ref, loss_ref, group_out_ref):
+        level = jnp.where(chip // near == f, total[:, at : at + rows], level)
+    level = jnp.where(chip % near == near_ref[0], level, 0.0)
+    scalars = jnp.broadcast_to(tail[:, rows:] * (1.0 / owners), (chips, 3 * rows))
+    first_core = core_ref[0] == 0
+    low, high = out[:chips], out[chips:]
+    empty = jnp.zeros(low.shape, f32)
+    mine = jnp.concatenate([jnp.where(first_core, low, high), empty, level, scalars], 1)
+    theirs = jnp.concatenate([empty, jnp.where(first_core, high, low), jnp.zeros((chips, rows), f32), scalars], 1)
+    mine_ref[...] = mine.reshape(mine_ref.shape)
+    theirs_ref[...] = theirs.reshape(theirs_ref.shape)
+
+
+def grad_kernel(core_ref, in_ref, share_ref, group_ref, high_ref, low_ref, out_ref, loss_ref, group_out_ref):
     rows, length = out_ref.shape
     quarter = length // 4
-    devices, _, lanes = in_ref.shape
-    owners = devices // FAR
-    a = in_ref[...].reshape(devices, lanes)
-    parts = [a[f * owners : (f + 1) * owners] for f in range(FAR)]
+    chips, _, lanes = in_ref.shape
+    near = chips // FAR
+    owners = 2 * near
+    a = in_ref[...].reshape(chips, lanes)
+    parts = [a[f * near : (f + 1) * near] for f in range(FAR)]
     a = (parts[0] + parts[1]) + (parts[2] + parts[3])
+    extra = a[:, lanes - 4 * rows :]
+    lanes = (lanes - 4 * rows) // 2
+    a = both_cores(core_ref[0] == 0, a[:, :lanes], a[:, lanes : 2 * lanes])
     none = jnp.zeros((owners, rows), f32)
     slots = HALF // owners
     by_cos, by_sin = [], []
@@ -475,7 +507,7 @@
         by_sin += [jnp.concatenate(([none, none, -im, -re], [none, -im, none, none], [none, none, -im, re], [-im, none, none, none])[group], 1)]
     stack = jnp.concatenate(by_cos + by_sin, 0).T
     both = mm3(pieces(stack), (high_ref[...], low_ref[...]))
-    sums = jnp.sum(a[:, 2 * slots * rows :], 0, keepdims=True)
+    sums = jnp.sum(extra, 0, keepdims=True)
     const = jnp.broadcast_to(sums, (8, 128)).T[:rows, :1]
     e = both[:rows] + const
     f = both[rows : 2 * rows]
@@ -496,10 +528,8 @@
 
 def tables(rows, length, near):
     devices = 2 * near * FAR
-    owner = np.arange(2 * near)
-    t = np.arange(HALF // len(owner))[:, None]
-    place = t * len(owner) + (owner % 2) * near + owner // 2
-    slots = (4 * (place % (HALF // 4)) + place // (HALF // 4) + 1).reshape(-1)
+    place = np.arange(HALF)
+    slots = 4 * (place % (HALF // 4)) + place // (HALF // 4) + 1
     cos, sin = turns(slots, np.arange(length // 4), length)
     row_table = np.concatenate([cos, sin], 0)
     cos, sin = turns(np.arange(devices), np.arange(devices), devices)
@@ -507,6 +537,7 @@
     n = np.arange(near)
     in_order = np.concatenate([2 * near * f + 2 * n + c for f in range(FAR) for c in range(2)])
     turn = dft[in_order]
+    dft = dft[np.concatenate([np.arange(0, devices, 2), np.arange(1, devices, 2)])]
     across = np.concatenate([np.arange(devices), devices * np.arange(8) - HALF])
     cos, sin = turns(across, np.arange(rows), length)
     turning = np.tile(cos, (1, 4)).astype(np.float32), np.tile(sin, (1, 4)).astype(np.float32)
@@ -586,9 +617,16 @@
     weights = jnp.exp(jnp.sum(onehot * group_logits[None, :], 1))
     total_weight = jnp.sum(weights)
     weight_share = weights / total_weight
-    width = 2 * HALF // (near * pair) * rows + 4 * rows
-    parcels = run(rows_kernel, shape((devices, 1, width)), n_in=3, mib=56)(mask_field, *row_table)
-    arrived = swap_all(parcels, SLAB)
+    width = 4 * HALF // (near * pair) * rows + 4 * rows
+    core = lax.axis_index(CORE).reshape(1)
+
+    def swap_rows(mine, theirs):
+        theirs = lax.ppermute(theirs, CORE, [(i, (i + 1) % pair) for i in range(pair)])
+        return swap_all(mine + theirs, (FAR_AXIS, NEAR))
+
+    chips = FAR * near
+    halves = (shape((chips, 1, width)),) * 2
+    arrived = swap_rows(*run(rows_kernel, halves, n_scalar=1, n_in=3, mib=56)(core, mask_field, *row_table))
     across = jnp.arange(K, dtype=jnp.int32) - HALF
     here = device * rows + jnp.arange(rows, dtype=jnp.int32)
     angle = jnp.mod(here[:, None] * across[None, :], length).astype(f32) * (2.0 * np.pi / length)
@@ -598,8 +636,8 @@
         tuple(jax.ShapeDtypeStruct(t, bf16) for t in sizes) + (shape((8, 128)),),
         n_in=3,
     )(jnp.cos(angle), jnp.sin(angle), spread)
-    piece = run(columns_kernel, shape((near, 1, SPECTRA + 128)), n_in=7)(
-        arrived, *dft, *turning, ready, weight_share.reshape(1, sources)
+    piece = run(columns_kernel, shape((near, 1, SPECTRA + 128)), n_scalar=1, n_in=7)(
+        core, arrived, *dft, *turning, ready, weight_share.reshape(1, sources)
     )
     around = swap_all(piece, NEAR)
     theirs = lax.ppermute(around, CORE, [(i, (i + 1) % pair) for i in range(pair)])
@@ -615,7 +653,7 @@
         shifted,
         weight_share,
         pupil_radius,
-        lax.axis_index(CORE).reshape(1),
+        core,
         around,
         theirs,
         arrived,
@@ -632,14 +670,14 @@
     )
     mine = mine + lax.ppermute(theirs, CORE, [(i, (i + 1) % pair) for i in range(pair)])
     mine = swap_all(mine, NEAR)
-    own = (lax.axis_index(NEAR) * pair + lax.axis_index(CORE)).reshape(1)
-    parcels = run(owner_kernel, shape((devices, 1, width)), n_scalar=1, n_in=5)(own, mine, *dft, *turning)
-    arrived = swap_all(parcels, SLAB)
+    arrived = swap_rows(
+        *run(owner_kernel, halves, n_scalar=2, n_in=5)(core, lax.axis_index(NEAR).reshape(1), mine, *dft, *turning)
+    )
     share_row = jnp.zeros((1, 128), f32).at[0, 64 : 64 + sources].set(weight_share)
     group_rows = jnp.zeros((NG, 128), f32).at[:, 64 : 64 + sources].set(onehot.T)
     mask_grad, loss_value, group_grad = run(
-        grad_kernel, (shape((rows, length)), shape((1, 1)), shape((1, NG))), n_in=5
-    )(arrived, share_row, group_rows, *row_table)
+        grad_kernel, (shape((rows, length)), shape((1, 1)), shape((1, NG))), n_scalar=1, n_in=5
+    )(core, arrived, share_row, group_rows, *row_table)
     return (loss_value.reshape(1), mask_grad, group_grad.reshape(NG))
 
 

time: 165 us -> 164 us (level)
  waiting for transfers between devices: 71.4 us -> 68.3 us
  other arithmetic: 4.18 us -> 6.75 us
    all_to_all x3, starting transfers between devices: 50.1 us -> 26.3 us  [swap_all(): lax.all_to_all(parcels, axes, split_axis=0, concat_axis=0, tiled=True)]
    ppermute x0 -> x2, starting transfers between devices: none -> 23.2 us  [swap_rows(): lax.ppermute(theirs, CORE, [(i, (i + 1) % pair) for i in range(pair)])]
    all_to_all x3, waiting for transfers between devices: 69.5 us -> 64.1 us  [swap_all(): lax.all_to_all(parcels, axes, split_axis=0, concat_axis=0, tiled=True)]
    add x0 -> x2, other arithmetic: none -> 2.54 us  [swap_rows(): return swap_all(mine + theirs, (FAR_AXIS, NEAR))]
    ppermute x0 -> x2, waiting for transfers between devices: none -> 2.23 us  [swap_rows(): lax.ppermute(theirs, CORE, [(i, (i + 1) % pair) for i in range(pair)])]
  transfers between devices with their start and end apart: 5 -> 7, of which waited for: 5 -> 7; matrix products, arithmetic and copies ran while one was open for 3% -> 4% of each run, Pallas kernels for 0% -> 0%
where the time goes in v6:
time: 164 us; the launch traced here: 162 us
  waiting for transfers between devices  68.3 us (42%)
  starting transfers between devices  53.7 us (33%)
  Pallas kernels  16.8 us (10%)
  blocking collectives  13.3 us (8%)
  other arithmetic  6.75 us (4%)
  local copies, waits for them, and re-layouts  2.14 us (1%)
    all_to_all x3, waiting for transfers between devices, swap_all(): lax.all_to_all(parcels, axes, split_axis=0, concat_axis=0, tiled=True)  64.1 us
    all_to_all x3, starting transfers between devices, swap_all(): lax.all_to_all(parcels, axes, split_axis=0, concat_axis=0, tiled=True)  26.3 us
    ppermute x2, starting transfers between devices, swap_rows(): lax.ppermute(theirs, CORE, [(i, (i + 1) % pair) for i in range(pair)])  23.2 us
    all_to_all x1, blocking collectives, swap_all(): lax.all_to_all(parcels, axes, split_axis=0, concat_axis=0, tiled=True)  13.3 us
    pallas_call x1, Pallas kernels, on_device(): run(image_kernel, (shape((near, 1, SPECTRA + 256)),) * 2, n_scalar=4, n_i...  10.5 us
    ppermute x1, starting transfers between devices, on_device(): lax.ppermute(around, CORE, [(i, (i + 1) % pair) for i in range(pair)])  3.69 us
  transfers between devices with their start and end apart: 7, of which 7 were waited for; matrix products, arithmetic and copies ran while one was open for 4% of the time, Pallas kernels for 0%

profile of v6, /device:TPU:37, one launch (start us, length us, event | category | flops | bytes accessed | tf_op | source)
XLA Modules:
  0.0 162.5 jit_solution(12746466515717264350)
XLA Ops:
  0.6 2.4 %shard_map.184 = (f32[32,1,1152]{2,1,0:T(1,128)}, f32[32,1,1152]{2,1,0:T(1,128)}) custom-call(s32[1]{0:T(128)} %bitcast.core_ref, f32[32,2048]{1,0:T(8,128)} %mask_ref.1, bf16[256,512]{1,0:T(8,128)(2,1)} %constant.130.clone.high_ref, bf16[256,512]{1,0:T(8,128)(2,1)} %constant.131.clone.low_ref), custom_call_target="tpu_custom_call" | custom-call | tf_op jit(solution)/shard_map/pallas_call | solution.py:629
  3.0 20.4 %collective-permute-start = (f32[32,1,1152]{2,1,0:T(1,128)}, f32[32,1,1152]{2,1,0:T(1,128)S(1)}, u32[]{:S(2)}, u32[]{:S(2)}) collective-permute-start(f32[32,1,1152]{2,1,0:T(1,128)} %get-tuple-element.44), channel_id=1, source_target_pairs={{0,1},{1,0},{2,3},{3,2},{4,5},{5,4},{6,7},{7,6},{8,9},{9,8},{10,11... | collective-permute-start | bytes 442376 | tf_op jit(solution)/shard_map/ppermute | solution.py:624
  23.4 1.2 collective-permute-done
  24.7 1.7 %add.44 = f32[32,1,1152]{2,1,0:T(1,128)} add(f32[32,1,1152]{2,1,0:T(1,128)} %get-tuple-element.43, f32[32,1,1152]{2,1,0:T(1,128)S(1)} %collective-permute-done) | non-fusion elementwise | flops 36864 | bytes 442368 | tf_op jit(solution)/shard_map/add | solution.py:625
  26.4 13.5 %all-to-all-start = ((f32[32,1,1152]{2,1,0:T(1,128)}), f32[32,1,1152]{2,1,0:T(1,128)S(1)}, u32[]{:S(2)}, u32[]{:S(2)}) async-start(f32[32,1,1152]{2,1,0:T(1,128)} %add.44), calls=%async_computation | async-start | bytes 294912 | tf_op jit(solution)/shard_map/all_to_all | solution.py:614
  40.0 0.0 copy-start.11
  40.0 0.0 copy-start.13
  40.0 0.0 copy-start.14
  40.0 0.0 copy-start.8
  40.0 0.2 fusion.3
  40.2 0.0 copy-start.7
  40.2 0.4 copy-done.11
  40.7 0.4 shard_map.185
  41.1 0.6 and_reduce_fusion
  41.7 0.1 select_reduce_fusion
  41.8 0.6 exponential_reduce_fusion
  42.4 1.2 broadcast_select_fusion
  43.6 27.0 %all-to-all-done.in_ref.arrived_ref = f32[32,1,1152]{2,1,0:T(1,128)S(1)} async-done(((f32[32,1,1152]{2,1,0:T(1,128)}), f32[32,1,1152]{2,1,0:T(1,128)S(1)}, u32[]{:S(2)}, u32[]{:S(2)}) %all-to-all-start) | async-done | bytes 147488 | tf_op jit(solution)/shard_map/all_to_all | solution.py:614
  70.6 0.0 copy-done.7
  70.6 0.0 copy-start.4
  70.6 0.0 copy-start.5
  70.6 1.5 shard_map.186
  72.2 3.6 %all-to-all-start.1 = ((f32[8,1,4224]{2,1,0:T(1,128)}), f32[8,1,4224]{2,1,0:T(1,128)S(1)}, u32[]{:S(2)}, u32[]{:S(2)}) async-start(f32[8,1,4224]{2,1,0:T(1,128)} %shard_map.186), calls=%async_computation.1 | async-start | bytes 270336 | tf_op jit(solution)/shard_map/all_to_all | solution.py:614
  75.7 0.0 copy-start.12
  76.4 0.0 copy-done.12
  76.4 0.0 copy-start.10
  76.4 0.1 copy.24
  76.5 9.3 %all-to-all-done.1.mine_ref = f32[8,1,4224]{2,1,0:T(1,128)S(1)} async-done(((f32[8,1,4224]{2,1,0:T(1,128)}), f32[8,1,4224]{2,1,0:T(1,128)S(1)}, u32[]{:S(2)}, u32[]{:S(2)}) %all-to-all-start.1) | async-done | bytes 135200 | tf_op jit(solution)/shard_map/all_to_all | solution.py:614
  85.9 3.7 %collective-permute-start.1 = (f32[8,1,4224]{2,1,0:T(1,128)S(1)}, f32[8,1,4224]{2,1,0:T(1,128)S(1)}, u32[]{:S(2)}, u32[]{:S(2)}) collective-permute-start(f32[8,1,4224]{2,1,0:T(1,128)S(1)} %all-to-all-done.1.mine_ref), channel_id=1, source_target_pairs={{0,1},{1,0},{2,3},{3,2},{4,5},{5,4},{6,7},{7,6},{8,9},{9,8},{10,11... | collective-permute-start | bytes 405512 | tf_op jit(solution)/shard_map/ppermute | solution.py:643
  89.6 1.0 collective-permute-done.1.theirs_ref
  90.6 0.0 copy-done.4
  90.6 10.5 %shard_map.187 = (f32[8,1,4352]{2,1,0:T(1,128)S(1)}, f32[8,1,4352]{2,1,0:T(1,128)S(1)}) custom-call(s32[16,2]{1,0:T(8,128)S(1)} %add_select_fusion.1.shift_ref, f32[16]{0:T(128)S(1)} %get-tuple-element.60.share_ref, s32[1]{0:T(128)} %copy.26.radius_ref, s32[1]{0:T(128)} %bitcast.core_ref, f32[8,1,4224]{2,1,0:T(1,128)S(1)} %all-to-all-done.1.mine_ref, ...), custom_call_target="tpu_custom_call" | custom-call | tf_op jit(solution)/shard_map/pallas_call | solution.py:645
  101.1 0.5 collective-permute-start.2
  101.5 1.0 collective-permute-done.2
  102.5 0.1 add.50
  102.7 13.3 %all_to_all.20.in_ref = f32[8,1,4352]{2,1,0:T(1,128)S(1)} all-to-all(f32[8,1,4352]{2,1,0:T(1,128)S(1)} %add.50), channel_id=1, replica_groups=mesh['clip'=4,'slab_0'=4,'slab_1'=8,'slab_2'=2] {'slab_1'}, dimensions={0} | all-to-all | bytes 278528 | tf_op jit(solution)/shard_map/all_to_all | solution.py:614
  116.0 0.9 shard_map.188
  116.8 2.8 %collective-permute-start.3 = (f32[32,1,1152]{2,1,0:T(1,128)S(1)}, f32[32,1,1152]{2,1,0:T(1,128)S(1)}, u32[]{:S(2)}, u32[]{:S(2)}) collective-permute-start(f32[32,1,1152]{2,1,0:T(1,128)S(1)} %get-tuple-element.55), channel_id=1, source_target_pairs={{0,1},{1,0},{2,3},{3,2},{4,5},{5,4},{6,7},{7,6},{8,9},{9,8},{10,11... | collective-permute-start | bytes 442376 | tf_op jit(solution)/shard_map/ppermute | solution.py:624
  119.6 1.0 collective-permute-done.3
  120.7 0.8 add.51
  121.5 9.2 %all-to-all-start.3 = ((f32[32,1,1152]{2,1,0:T(1,128)}), f32[32,1,1152]{2,1,0:T(1,128)S(1)}, u32[]{:S(2)}, u32[]{:S(2)}) async-start(f32[32,1,1152]{2,1,0:T(1,128)} %add.51), calls=%async_computation.3 | async-start | bytes 294912 | tf_op jit(solution)/shard_map/all_to_all | solution.py:614
  130.6 0.6 slice.36
  131.2 0.6 fusion.6
  131.9 0.6 convert_select_fusion
  132.5 0.1 scatter.9.group_ref
  132.6 0.9 scatter.6.share_ref
  133.5 27.8 %all-to-all-done.3.in_ref = f32[32,1,1152]{2,1,0:T(1,128)S(1)} async-done(((f32[32,1,1152]{2,1,0:T(1,128)}), f32[32,1,1152]{2,1,0:T(1,128)S(1)}, u32[]{:S(2)}, u32[]{:S(2)}) %all-to-all-start.3) | async-done | bytes 147488 | tf_op jit(solution)/shard_map/all_to_all | solution.py:614
  161.3 1.2 shard_map.189
  (23 shorter events, 0.1 us)
Async XLA Ops:
  3.0 21.6 %collective-permute-start = (f32[32,1,1152]{2,1,0:T(1,128)}, f32[32,1,1152]{2,1,0:T(1,128)S(1)}, u32[]{:S(2)}, u32[]{:S(2)}) collective-permute-start(f32[32,1,1152]{2,1,0:T(1,128)} %get-tuple-element.44), channel_id=1, source_target_pairs={{0,1},{1,0},{2,3},{3,2},{4,5},{5,4},{6,7},{7,6},{8,9},{9,8},{10,11... | collective-permute-start | bytes 442376 | tf_op jit(solution)/shard_map/ppermute | solution.py:624
  26.4 64.2 %copy-start.6 = (bf16[512,256]{1,0:T(8,128)(2,1)S(1)}, bf16[512,256]{1,0:T(8,128)(2,1)}, u32[]{:S(2)}) copy-start(bf16[512,256]{1,0:T(8,128)(2,1)} %constant.140.clone.field_low_ref) | copy-start | bytes 786436
  26.4 44.2 %all-to-all-start = ((f32[32,1,1152]{2,1,0:T(1,128)}), f32[32,1,1152]{2,1,0:T(1,128)S(1)}, u32[]{:S(2)}, u32[]{:S(2)}) async-start(f32[32,1,1152]{2,1,0:T(1,128)} %add.44), calls=%async_computation | async-start | bytes 294912 | tf_op jit(solution)/shard_map/all_to_all | solution.py:614
  40.0 0.7 copy-start.11
  40.0 1.7 %copy-start.13 = (s32[16]{0:T(128)S(1)}, s32[16]{0:T(128)}, u32[]{:S(2)}) copy-start(s32[16]{0:T(128)} %param.24) | copy-start | bytes 196
  40.0 1.7 %copy-start.14 = (f32[8]{0:T(128)S(1)}, f32[8]{0:T(128)}, u32[]{:S(2)}) copy-start(f32[8]{0:T(128)} %param.25) | copy-start | bytes 100
  40.0 30.6 %copy-start.8 = (bf16[64,128]{1,0:T(8,128)(2,1)S(1)}, bf16[64,128]{1,0:T(8,128)(2,1)}, u32[]{:S(2)}) copy-start(bf16[64,128]{1,0:T(8,128)(2,1)} %constant.134.clone.dft_low_ref.low_ref) | copy-start | bytes 49156
  40.2 30.4 %copy-start.7 = (bf16[64,128]{1,0:T(8,128)(2,1)S(1)}, bf16[64,128]{1,0:T(8,128)(2,1)}, u32[]{:S(2)}) copy-start(bf16[64,128]{1,0:T(8,128)(2,1)} %constant.133.clone.dft_high_ref.high_ref) | copy-start | bytes 49156
  40.7 29.9 %copy-start.2 = (f32[72,128]{1,0:T(8,128)S(1)}, f32[72,128]{1,0:T(8,128)}, u32[]{:S(2)}) copy-start(f32[72,128]{1,0:T(8,128)} %constant.135.clone.cos_ref) | copy-start | bytes 110596
  40.7 29.9 %copy-start.3 = (f32[72,128]{1,0:T(8,128)S(1)}, f32[72,128]{1,0:T(8,128)}, u32[]{:S(2)}) copy-start(f32[72,128]{1,0:T(8,128)} %constant.136.clone.sin_ref) | copy-start | bytes 110596
  70.6 20.0 %copy-start.4 = (s32[32,2048]{1,0:T(8,128)S(1)}, s32[32,2048]{1,0:T(8,128)}, u32[]{:S(2)}) copy-start(s32[32,2048]{1,0:T(8,128)} %target_ref.1) | copy-start | bytes 786436
  70.6 20.0 %copy-start.5 = (bf16[512,256]{1,0:T(8,128)(2,1)S(1)}, bf16[512,256]{1,0:T(8,128)(2,1)}, u32[]{:S(2)}) copy-start(bf16[512,256]{1,0:T(8,128)(2,1)} %constant.139.clone.field_high_ref) | copy-start | bytes 786436
  72.2 13.7 %all-to-all-start.1 = ((f32[8,1,4224]{2,1,0:T(1,128)}), f32[8,1,4224]{2,1,0:T(1,128)S(1)}, u32[]{:S(2)}, u32[]{:S(2)}) async-start(f32[8,1,4224]{2,1,0:T(1,128)} %shard_map.186), calls=%async_computation.1 | async-start | bytes 270336 | tf_op jit(solution)/shard_map/all_to_all | solution.py:614
  75.7 0.7 copy-start.12
  76.4 14.1 %copy-start.10 = (bf16[64,128]{1,0:T(8,128)(2,1)S(1)}, bf16[64,128]{1,0:T(8,128)(2,1)}, u32[]{:S(2)}) copy-start(bf16[64,128]{1,0:T(8,128)(2,1)} %constant.138.clone.turn_low_ref) | copy-start | bytes 49156
  76.5 14.0 %copy-start.9 = (bf16[64,128]{1,0:T(8,128)(2,1)S(1)}, bf16[64,128]{1,0:T(8,128)(2,1)}, u32[]{:S(2)}) copy-start(bf16[64,128]{1,0:T(8,128)(2,1)} %constant.137.clone.turn_high_ref) | copy-start | bytes 49156
  85.9 4.7 %collective-permute-start.1 = (f32[8,1,4224]{2,1,0:T(1,128)S(1)}, f32[8,1,4224]{2,1,0:T(1,128)S(1)}, u32[]{:S(2)}, u32[]{:S(2)}) collective-permute-start(f32[8,1,4224]{2,1,0:T(1,128)S(1)} %all-to-all-done.1.mine_ref), channel_id=1, source_target_pairs={{0,1},{1,0},{2,3},{3,2},{4,5},{5,4},{6,7},{7,6},{8,9},{9,8},{10,11... | collective-permute-start | bytes 405512 | tf_op jit(solution)/shard_map/ppermute | solution.py:643
  101.1 1.5 collective-permute-start.2
  116.8 3.8 %collective-permute-start.3 = (f32[32,1,1152]{2,1,0:T(1,128)S(1)}, f32[32,1,1152]{2,1,0:T(1,128)S(1)}, u32[]{:S(2)}, u32[]{:S(2)}) collective-permute-start(f32[32,1,1152]{2,1,0:T(1,128)S(1)} %get-tuple-element.55), channel_id=1, source_target_pairs={{0,1},{1,0},{2,3},{3,2},{4,5},{5,4},{6,7},{7,6},{8,9},{9,8},{10,11... | collective-permute-start | bytes 442376 | tf_op jit(solution)/shard_map/ppermute | solution.py:624
  120.7 40.6 %copy-start.1 = (bf16[256,512]{1,0:T(8,128)(2,1)S(1)}, bf16[256,512]{1,0:T(8,128)(2,1)}, u32[]{:S(2)}) copy-start(bf16[256,512]{1,0:T(8,128)(2,1)} %constant.131.clone.low_ref) | copy-start | bytes 786436
  121.5 39.8 %copy-start = (bf16[256,512]{1,0:T(8,128)(2,1)S(1)}, bf16[256,512]{1,0:T(8,128)(2,1)}, u32[]{:S(2)}) copy-start(bf16[256,512]{1,0:T(8,128)(2,1)} %constant.130.clone.high_ref) | copy-start | bytes 786436
  121.5 39.8 %all-to-all-start.3 = ((f32[32,1,1152]{2,1,0:T(1,128)}), f32[32,1,1152]{2,1,0:T(1,128)S(1)}, u32[]{:S(2)}, u32[]{:S(2)}) async-start(f32[32,1,1152]{2,1,0:T(1,128)} %add.51), calls=%async_computation.3 | async-start | bytes 294912 | tf_op jit(solution)/shard_map/all_to_all | solution.py:614
